TPU v7x, 32 devices: a whole 2x2x4 slice. The times are simulated.
32 devices in a mesh: gx: 4 (over x, core), gy: 4 (over z), gz: 2 (over y).
Axes of the slice: x: 2, y: 2, z: 4, core: 2. Of those that a mesh axis runs over, the one named last changes fastest.
Arguments:
- density: float32 [16, 128, 256], P('gx', 'gy', 'gz'), may hold values from 0.5 to 2
- velocity: float32 [3, 16, 128, 256], P(None, 'gx', 'gy', 'gz'), may hold values from -2.5 to 2.5
- pressure: float32 [16, 128, 256], P('gx', 'gy', 'gz'), may hold values from 0.5 to 2
Outputs:
- section_state: float32 [5, 16, 128, 256], P(None, 'gx', 'gy', 'gz')
All inputs are finite; a program needn't handle non-finite values.
Results may differ from a plain program's by a relative error of at most 0.0003.
Values sent between devices are 32-bit elements; how exact they have to be, the bound alone decides.
No kernel may reach another device: no remote copies, remote signals or barrier semaphores. Data moves between devices by JAX's collectives and lax.ppermute only.
A program may use at most 64 MiB of HBM per device.

v0:
```python
import jax
import jax.numpy as jnp
from jax import lax
from jax.sharding import PartitionSpec as P

gamma_gas = 1.4
weno_eps = 1e-06
cfl_number = 0.4


def padded_2(cells, sides, width):
    for axis, dim in sides:
        count = lax.axis_size(axis)
        head = lax.slice_in_dim(cells, 0, width, axis=dim)
        tail = lax.slice_in_dim(cells, cells.shape[dim] - width, cells.shape[dim], axis=dim)
        cells = jnp.concatenate(
            [
                lax.ppermute(tail, axis, [(i, (i + 1) % count) for i in range(count)]),
                cells,
                lax.ppermute(head, axis, [((i + 1) % count, i) for i in range(count)]),
            ],
            axis=dim,
        )
    return cells


def conserved(density, velocity, pressure):
    momenta = density[None] * velocity
    kinetic = 0.5 * density * jnp.sum(velocity * velocity, axis=0)
    energy = pressure / (gamma_gas - 1.0) + kinetic
    return jnp.concatenate([density[None], momenta, energy[None]], axis=0)


def wave_speed(density, velocity, pressure):
    sound = jnp.sqrt(gamma_gas * pressure / density)
    return jnp.max(jnp.sum(jnp.abs(velocity), axis=0) + 3.0 * sound)


def combine(coeffs, arrays):
    total = None
    for coeff, array in zip(coeffs, arrays):
        if isinstance(coeff, float) and coeff == 0.0:
            continue
        term = coeff * array
        total = term if total is None else total + term
    return total


def weno_face(values):
    first, second, third, fourth, fifth = values
    cand_left = (2.0 * first - 7.0 * second + 11.0 * third) / 6.0
    cand_middle = (-second + 5.0 * third + 2.0 * fourth) / 6.0
    cand_right = (2.0 * third + 5.0 * fourth - fifth) / 6.0
    smooth_left = (
        13.0 / 12.0 * (first - 2.0 * second + third) ** 2
        + 0.25 * (first - 4.0 * second + 3.0 * third) ** 2
    )
    smooth_middle = (
        13.0 / 12.0 * (second - 2.0 * third + fourth) ** 2 + 0.25 * (second - fourth) ** 2
    )
    smooth_right = (
        13.0 / 12.0 * (third - 2.0 * fourth + fifth) ** 2
        + 0.25 * (3.0 * third - 4.0 * fourth + fifth) ** 2
    )
    weight_left = 0.1 / (weno_eps + smooth_left) ** 2
    weight_middle = 0.6 / (weno_eps + smooth_middle) ** 2
    weight_right = 0.3 / (weno_eps + smooth_right) ** 2
    return (weight_left * cand_left + weight_middle * cand_middle + weight_right * cand_right) / (
        weight_left + weight_middle + weight_right
    )


def direction_flux(padded, field_dim, normal_comp):
    cells = padded.shape[field_dim + 1] - 6
    faces = cells + 1
    density = padded[0]
    energy = padded[4]
    velocity = [padded[1 + member] / density for member in range(3)]
    speed_sq = velocity[0] * velocity[0] + velocity[1] * velocity[1] + velocity[2] * velocity[2]
    pressure = (gamma_gas - 1.0) * (energy - 0.5 * density * speed_sq)
    sound_sq = gamma_gas * pressure / density
    sound = jnp.sqrt(sound_sq)
    enthalpy = (energy + pressure) / density
    normal_vel = velocity[normal_comp]
    others = [member for member in range(3) if member != normal_comp]
    order = [0, 1 + normal_comp, 1 + others[0], 1 + others[1], 4]
    state_perm = [padded[member] for member in order]
    flux_perm = [
        density * normal_vel,
        padded[1 + normal_comp] * normal_vel + pressure,
        padded[1 + others[0]] * normal_vel,
        padded[1 + others[1]] * normal_vel,
        (energy + pressure) * normal_vel,
    ]
    signal = jnp.abs(normal_vel) + sound

    def window(array, offset):
        return lax.slice_in_dim(array, offset, offset + faces, axis=field_dim)

    root_left = jnp.sqrt(window(density, 2))
    root_right = jnp.sqrt(window(density, 3))
    share_left = root_left / (root_left + root_right)
    share_right = root_right / (root_left + root_right)
    roe_vel = [
        share_left * window(member, 2) + share_right * window(member, 3) for member in velocity
    ]
    roe_enth = share_left * window(enthalpy, 2) + share_right * window(enthalpy, 3)
    jump_sq = sum(((window(member, 3) - window(member, 2)) ** 2 for member in velocity))
    roe_sound_sq = (
        share_left * window(sound_sq, 2)
        + share_right * window(sound_sq, 3)
        + 0.5 * (gamma_gas - 1.0) * share_left * share_right * jump_sq
    )
    roe_sound = jnp.sqrt(roe_sound_sq)
    normal_roe = roe_vel[normal_comp]
    tang_first = roe_vel[others[0]]
    tang_second = roe_vel[others[1]]
    roe_qsq = normal_roe * normal_roe + tang_first * tang_first + tang_second * tang_second
    b_one = (gamma_gas - 1.0) / roe_sound_sq
    b_two = 0.5 * b_one * roe_qsq
    inv_sound = 1.0 / roe_sound
    left_rows = [
        [
            0.5 * (b_two + normal_roe * inv_sound),
            -0.5 * (b_one * normal_roe + inv_sound),
            -0.5 * b_one * tang_first,
            -0.5 * b_one * tang_second,
            0.5 * b_one,
        ],
        [1.0 - b_two, b_one * normal_roe, b_one * tang_first, b_one * tang_second, -b_one],
        [-tang_first, 0.0, 1.0, 0.0, 0.0],
        [-tang_second, 0.0, 0.0, 1.0, 0.0],
        [
            0.5 * (b_two - normal_roe * inv_sound),
            -0.5 * (b_one * normal_roe - inv_sound),
            -0.5 * b_one * tang_first,
            -0.5 * b_one * tang_second,
            0.5 * b_one,
        ],
    ]
    right_rows = [
        [1.0, 1.0, 0.0, 0.0, 1.0],
        [normal_roe - roe_sound, normal_roe, 0.0, 0.0, normal_roe + roe_sound],
        [tang_first, tang_first, 1.0, 0.0, tang_first],
        [tang_second, tang_second, 0.0, 1.0, tang_second],
        [
            roe_enth - normal_roe * roe_sound,
            0.5 * roe_qsq,
            tang_first,
            tang_second,
            roe_enth + normal_roe * roe_sound,
        ],
    ]
    alpha = window(signal, 0)
    for offset in range(1, 6):
        alpha = jnp.maximum(alpha, window(signal, offset))
    plus_vals = [[None] * 6 for member in range(5)]
    minus_vals = [[None] * 6 for member in range(5)]
    for offset in range(6):
        state_here = [window(member, offset) for member in state_perm]
        flux_here = [window(member, offset) for member in flux_perm]
        for charac in range(5):
            char_state = combine(left_rows[charac], state_here)
            char_flux = combine(left_rows[charac], flux_here)
            plus_vals[charac][offset] = 0.5 * (char_flux + alpha * char_state)
            minus_vals[charac][offset] = 0.5 * (char_flux - alpha * char_state)
    hats = []
    for charac in range(5):
        upwind = weno_face(plus_vals[charac][0:5])
        downwind = weno_face(
            [
                minus_vals[charac][5],
                minus_vals[charac][4],
                minus_vals[charac][3],
                minus_vals[charac][2],
                minus_vals[charac][1],
            ]
        )
        hats.append(upwind + downwind)
    face_flux = [None] * 5
    for member in range(5):
        face_flux[order[member]] = combine(right_rows[member], hats)
    result = [
        lax.slice_in_dim(member, 1, faces, axis=field_dim)
        - lax.slice_in_dim(member, 0, faces - 1, axis=field_dim)
        for member in face_flux
    ]
    return jnp.stack(result, axis=0)


def local(density, velocity, pressure):
    state = conserved(density, velocity, pressure)
    local_top = wave_speed(density, velocity, pressure)
    top = lax.pmax(local_top, ("gx", "gy", "gz"))
    along_first = padded_2(state, (("gx", 1),), 3)
    along_second = padded_2(state, (("gy", 2),), 3)
    along_third = padded_2(state, (("gz", 3),), 3)
    total = direction_flux(along_first, 0, 0)
    total = total + direction_flux(along_second, 1, 1)
    total = total + direction_flux(along_third, 2, 2)
    step = cfl_number / top
    return state - step * total


def solution(mesh):
    in_specs = (P("gx", "gy", "gz"), P(None, "gx", "gy", "gz"), P("gx", "gy", "gz"))
    out_specs = P(None, "gx", "gy", "gz")
    return jax.shard_map(local, mesh=mesh, in_specs=in_specs, out_specs=out_specs, check_vma=False)
```

profile of v0, /device:TPU:1, one launch (start us, length us, event | category | flops | bytes accessed | tf_op | source)
XLA Modules:
  0.0 78.7 jit_solution(17060478465141477660)
XLA Ops:
  0.0 0.0 copy-start
  0.0 0.0 copy-start.1
  0.0 1.0 %abs_reduce_fusion = (f32[4,32,128]{2,1,0:T(8,128)S(1)}, f32[4,32,128]{2,1,0:T(8,128)S(1)}, f32[3,4,32,128]{3,2,1,0:T(8,128)S(1)}) fusion(f32[3,4,32,128]{3,2,1,0:T(8,128)} %param.4, f32[4,32,128]{2,1,0:T(8,128)} %param.3), kind=kLoop, calls=%fused_computation.7 | loop fusion | flops 212992 | bytes 589824 | tf_op jit(solution)/shard_map/reduce_sum | solution.py:36
  1.0 0.0 copy-done
  1.0 0.0 copy-done.1
  1.0 0.6 add_reduce_fusion
  1.7 0.2 fusion.149
  1.9 2.1 %collective-permute-start.5 = (f32[5,4,32,3]{3,2,1,0:T(8,128)S(1)}, f32[5,4,32,3]{3,2,1,0:T(8,128)S(1)}, u32[]{:S(2)}, u32[]{:S(2)}) collective-permute-start(f32[5,4,32,3]{3,2,1,0:T(8,128)S(1)} %get-tuple-element.103), channel_id=1, source_target_pairs={{1,0},{0,1},{3,2},{2,3},{5,4},{4,5},{7,6},{6,7},{9,8},{8,9},{11,10... | collective-permute-start | bytes 23048 | tf_op jit(solution)/shard_map/ppermute | solution.py:20
  4.0 0.1 collective-permute-start.4
  4.1 3.5 %collective-permute-start.3 = (f32[5,4,3,128]{3,2,1,0:T(4,128)S(1)}, f32[5,4,3,128]{3,2,1,0:T(4,128)S(1)}, u32[]{:S(2)}, u32[]{:S(2)}) collective-permute-start(f32[5,4,3,128]{3,2,1,0:T(4,128)S(1)} %get-tuple-element.97), channel_id=1, source_target_pairs={{2,0},{4,2},{6,4},{0,6},{3,1},{5,3},{7,5},{1,7},{10,8},{12,10},{14... | collective-permute-start | bytes 92168 | tf_op jit(solution)/shard_map/ppermute | solution.py:20
  7.6 0.0 collective-permute-start.2
  7.7 1.6 %collective-permute-start.1 = (f32[5,3,32,128]{3,2,1,0:T(8,128)S(1)}, f32[5,3,32,128]{3,2,1,0:T(8,128)S(1)}, u32[]{:S(2)}, u32[]{:S(2)}) collective-permute-start(f32[5,3,32,128]{3,2,1,0:T(8,128)S(1)} %get-tuple-element.101), channel_id=1, source_target_pairs={{8,0},{16,8},{24,16},{0,24},{9,1},{17,9},{25,17},{1,25},{10,2},{18... | collective-permute-start | bytes 737288 | tf_op jit(solution)/shard_map/ppermute | solution.py:20
  9.2 43.8 %pmax.7 = f32[]{:T(128)} all-reduce(f32[]{:T(128)} %get-tuple-element.116), channel_id=1, replica_groups=mesh['gx'=4,'gy'=4,'gz'=2] {'gx','gy','gz'}, use_global_device_ids=true, to_apply=%region_3.0 | all-reduce | flops 1 | bytes 8 | tf_op jit(solution)/shard_map/pmax | solution.py:194
  53.8 0.0 collective-permute-done.5
  53.8 3.2 %collective-permute-start = (f32[5,3,32,128]{3,2,1,0:T(8,128)S(1)}, f32[5,3,32,128]{3,2,1,0:T(8,128)S(1)}, u32[]{:S(2)}, u32[]{:S(2)}) collective-permute-start(f32[5,3,32,128]{3,2,1,0:T(8,128)S(1)} %get-tuple-element.100), channel_id=1, source_target_pairs={{0,8},{8,16},{16,24},{24,0},{1,9},{9,17},{17,25},{25,1},{2,10},{10... | collective-permute-start | bytes 737288 | tf_op jit(solution)/shard_map/ppermute | solution.py:18
  57.0 0.0 collective-permute-done.4
  57.0 0.3 pad_maximum_fusion.1
  57.4 0.1 slice_bitcast_fusion.5
  57.4 0.1 fusion.120
  57.5 0.2 add_divide_fusion.1
  57.7 0.1 fusion.129
  57.8 9.1 %multiply_add_fusion.3 = (f32[4,32,129]{2,1,0:T(8,128)S(1)}, f32[4,32,129]{2,1,0:T(8,128)S(1)}, f32[4,32,129]{2,1,0:T(8,128)S(1)}, f32[4,32,129]{2,1,0:T(8,128)S...) fusion(f32[4,32,129]{2,1,0:T(8,128)S(1)} %get-tuple-element.119, ...), kind=kLoop, calls=%fused_computation.47 | loop fusion | flops 18889728 | bytes 5812224 | tf_op jit(solution)/shard_map/add | solution.py:45
  66.9 0.1 multiply_add_fusion.4
  67.1 0.1 fusion.98
  67.1 0.1 fusion.96
  67.2 0.1 fusion.94
  67.3 0.1 fusion.92
  67.4 0.0 collective-permute-done.3
  67.4 0.0 collective-permute-done.2
  67.4 0.1 pad_maximum_fusion.3
  67.5 0.1 fusion.122
  67.6 0.1 add_divide_fusion.3
  67.7 0.1 fusion.124
  67.7 4.6 %multiply_add_fusion.15 = (f32[4,33,128]{2,1,0:T(8,128)S(1)}, f32[4,33,128]{2,1,0:T(8,128)S(1)}, f32[4,33,128]{2,1,0:T(8,128)S(1)}, f32[4,33,128]{2,1,0:T(8,128)...) fusion(f32[4,33,128]{2,1,0:T(8,128)S(1)} %get-tuple-element.121, ...), kind=kLoop, calls=%fused_computation.207 | loop fusion | flops 19329024 | bytes 5947392 | tf_op jit(solution)/shard_map/add | solution.py:45
  72.3 0.1 fusion.35
  72.5 0.1 fusion.90
  72.6 0.0 collective-permute-done.1
  72.6 0.0 collective-permute-done
  72.6 0.1 pad_maximum_fusion
  72.6 0.1 fusion.27
  72.8 0.2 multiply_add_fusion
  72.9 0.1 maximum_maximum_fusion
  73.1 0.1 fusion.34
  73.2 4.4 %multiply_add_fusion.22 = (f32[5,32,128]{2,1,0:T(8,128)S(1)}, f32[5,32,128]{2,1,0:T(8,128)S(1)}, f32[5,32,128]{2,1,0:T(8,128)S(1)}, f32[5,32,128]{2,1,0:T(8,128)...) fusion(f32[5,32,128]{2,1,0:T(8,128)S(1)} %get-tuple-element.115, f32[5,32,128]{2,1,0:T(8,128)S(1)} %get-tuple-element.114, ...), kind=kLoop, calls=%fused_computation.253 | loop fusion | flops 22937600 | bytes 6553600 | tf_op jit(solution)/shard_map/add | solution.py:45
  77.6 0.1 fusion.37
  77.8 0.9 %multiply_subtract_fusion = f32[5,4,32,128]{3,2,1,0:T(8,128)} fusion(f32[5,4,32,128]{3,2,1,0:T(8,128)S(1)} %get-tuple-element.122, f32[5,4,32,128]{3,2,1,0:T(8,128)S(1)} %fusion.110, f32[5,4,32,128]{3,2,1,0:T(8,128)S(1)} %get-tuple-element.123, f32[]{:T(128)S(6)} %div.735, f32[1,4,32,128]{3,2,1,0:T(8,128)S(1)} %get-tuple-element.117, ...), kind=kLoop, calls=%fused_computation.6 | loop fusion | flops 491520 | bytes 1638404 | tf_op jit(solution)/shard_map/sub | solution.py:202
  (14 shorter events, 0.2 us)
Async XLA Ops:
  0.0 1.0 %copy-start = (f32[4,32,128]{2,1,0:T(8,128)S(1)}, f32[4,32,128]{2,1,0:T(8,128)}, u32[]{:S(2)}) copy-start(f32[4,32,128]{2,1,0:T(8,128)} %param.3) | copy-start | bytes 196612
  0.0 1.0 %copy-start.1 = (f32[4,32,128]{2,1,0:T(8,128)S(1)}, f32[4,32,128]{2,1,0:T(8,128)}, u32[]{:S(2)}) copy-start(f32[4,32,128]{2,1,0:T(8,128)} %param.5) | copy-start | bytes 196612
  1.9 51.9 %collective-permute-start.5 = (f32[5,4,32,3]{3,2,1,0:T(8,128)S(1)}, f32[5,4,32,3]{3,2,1,0:T(8,128)S(1)}, u32[]{:S(2)}, u32[]{:S(2)}) collective-permute-start(f32[5,4,32,3]{3,2,1,0:T(8,128)S(1)} %get-tuple-element.103), channel_id=1, source_target_pairs={{1,0},{0,1},{3,2},{2,3},{5,4},{4,5},{7,6},{6,7},{9,8},{8,9},{11,10... | collective-permute-start | bytes 23048 | tf_op jit(solution)/shard_map/ppermute | solution.py:20
  4.0 53.0 %collective-permute-start.4 = (f32[5,4,32,3]{3,2,1,0:T(8,128)S(1)}, f32[5,4,32,3]{3,2,1,0:T(8,128)S(1)}, u32[]{:S(2)}, u32[]{:S(2)}) collective-permute-start(f32[5,4,32,3]{3,2,1,0:T(8,128)S(1)} %get-tuple-element.102), channel_id=1, source_target_pairs={{0,1},{1,0},{2,3},{3,2},{4,5},{5,4},{6,7},{7,6},{8,9},{9,8},{10,11... | collective-permute-start | bytes 23048 | tf_op jit(solution)/shard_map/ppermute | solution.py:18
  4.1 63.3 %collective-permute-start.3 = (f32[5,4,3,128]{3,2,1,0:T(4,128)S(1)}, f32[5,4,3,128]{3,2,1,0:T(4,128)S(1)}, u32[]{:S(2)}, u32[]{:S(2)}) collective-permute-start(f32[5,4,3,128]{3,2,1,0:T(4,128)S(1)} %get-tuple-element.97), channel_id=1, source_target_pairs={{2,0},{4,2},{6,4},{0,6},{3,1},{5,3},{7,5},{1,7},{10,8},{12,10},{14... | collective-permute-start | bytes 92168 | tf_op jit(solution)/shard_map/ppermute | solution.py:20
  7.6 59.8 %collective-permute-start.2 = (f32[5,4,3,128]{3,2,1,0:T(4,128)S(1)}, f32[5,4,3,128]{3,2,1,0:T(4,128)S(1)}, u32[]{:S(2)}, u32[]{:S(2)}) collective-permute-start(f32[5,4,3,128]{3,2,1,0:T(4,128)S(1)} %get-tuple-element.96), channel_id=1, source_target_pairs={{0,2},{2,4},{4,6},{6,0},{1,3},{3,5},{5,7},{7,1},{8,10},{10,12},{12... | collective-permute-start | bytes 92168 | tf_op jit(solution)/shard_map/ppermute | solution.py:18
  7.7 64.9 %collective-permute-start.1 = (f32[5,3,32,128]{3,2,1,0:T(8,128)S(1)}, f32[5,3,32,128]{3,2,1,0:T(8,128)S(1)}, u32[]{:S(2)}, u32[]{:S(2)}) collective-permute-start(f32[5,3,32,128]{3,2,1,0:T(8,128)S(1)} %get-tuple-element.101), channel_id=1, source_target_pairs={{8,0},{16,8},{24,16},{0,24},{9,1},{17,9},{25,17},{1,25},{10,2},{18... | collective-permute-start | bytes 737288 | tf_op jit(solution)/shard_map/ppermute | solution.py:20
  53.8 18.8 %collective-permute-start = (f32[5,3,32,128]{3,2,1,0:T(8,128)S(1)}, f32[5,3,32,128]{3,2,1,0:T(8,128)S(1)}, u32[]{:S(2)}, u32[]{:S(2)}) collective-permute-start(f32[5,3,32,128]{3,2,1,0:T(8,128)S(1)} %get-tuple-element.100), channel_id=1, source_target_pairs={{0,8},{8,16},{16,24},{24,0},{1,9},{9,17},{17,25},{25,1},{2,10},{10... | collective-permute-start | bytes 737288 | tf_op jit(solution)/shard_map/ppermute | solution.py:18
where the time goes:
time: 79 us; the launch traced here: 78.7 us
  blocking collectives  43.8 us (55%)
  other arithmetic  22.9 us (29%)
  starting transfers between devices  10.5 us (13%)
  between operations  1.02 us (1%)
    pmax x1, blocking collectives, local(): top = lax.pmax(local_top, ('gx', 'gy', 'gz'))  43.8 us
    add x6, other arithmetic, combine(): total = term if total is None else total + term  18.3 us
    ppermute x3, starting transfers between devices, padded_2(): lax.ppermute(head, axis, [((i + 1) % count, i) for i in range(count)])  7.21 us
    ppermute x3, starting transfers between devices, padded_2(): lax.ppermute(tail, axis, [(i, (i + 1) % count) for i in range(count)])  3.31 us
  transfers between devices with their start and end apart: 6, of which 0 were waited for; matrix products, arithmetic and copies ran while one was open for 20% of the time, Pallas kernels for 0%

commit v1 on v0

v1 whole, which is shorter than its diff:
```python
import functools
import math

import jax
import jax.numpy as jnp
from jax import lax
from jax.experimental import pallas as pl
from jax.experimental.pallas import tpu as pltpu
from jax.sharding import PartitionSpec as P

gamma_gas = 1.4
weno_eps = 1e-06
cfl_number = 0.4
f32 = jnp.float32

KX = math.sqrt(13.0 / 12.0)
KT = 0.5 / KX
KB = 1.0 / (6.0 * KX)
VMEM_LIMIT = 24 * 1024 * 1024


def rup(n, m):
    return (n + m - 1) // m * m


def cell_values(prim, tile, comps):
    rho, p = prim[0], prim[4]
    un, ut, us = (prim[1 + c] for c in comps)
    inv = 1.0 / rho
    mn, mt, ms = rho * un, rho * ut, rho * us
    mnun = mn * un
    energy = 2.5 * p + 0.5 * (mnun + mt * ut + ms * us)
    total = energy + p
    sound = jnp.sqrt(gamma_gas * p * inv)
    state = (rho, mn, mt, ms, energy)
    flux = (mn, mnun + p, mt * un, ms * un, total * un)
    return state, flux, total * inv, jnp.sqrt(rho), jnp.abs(un) + sound


def weno_excess(mid, xa, xb, xc, sign, eps):
    tau_a = xa - xb
    tau_c = xb - xc
    if sign > 0:
        mid_a = mid + KT * tau_a
        mid_c = mid + KT * tau_c
    else:
        mid_a = mid - KT * tau_a
        mid_c = mid - KT * tau_c
    sm_a = mid_a * mid_a + (xa * xa + eps)
    sm_b = mid * mid + (xb * xb + eps)
    sm_c = mid_c * mid_c + (xc * xc + eps)
    ga = 3.0 * (sm_a * sm_a)
    gb = sm_b * sm_b
    gc = sm_c * sm_c
    gc = gc + gc
    num = gb * (tau_a * gc + tau_c * ga)
    den = gb * gc + (ga + ga) * (gb + gc)
    return num / den


def characteristic(v, un, ut, us, qh, b1, ic):
    t = (qh * v[0] - un * v[1]) - (ut * v[2] + us * v[3]) + v[4]
    a = b1 * t
    n = (un * v[0] - v[1]) * ic
    return (a + n, v[0] - a, v[2] - ut * v[0], v[3] - us * v[0], a - n)


def face_values(get_prim, get_aux, get_cx, comps):
    rl, rr = get_aux(1, 2), get_aux(1, 3)
    share = rr / (rl + rr)

    def roe(left, right):
        return left + share * (right - left)

    un, ut, us = (roe(get_prim(1 + c, 2), get_prim(1 + c, 3)) for c in comps)
    enth = roe(get_aux(0, 2), get_aux(0, 3))
    qh = 0.5 * (un * un + ut * ut + us * us)
    c2 = (gamma_gas - 1.0) * (enth - qh)
    ic = lax.rsqrt(c2)
    c = c2 * ic
    b1 = (gamma_gas - 1.0) * (ic * ic)
    alpha = jnp.maximum(jnp.maximum(get_aux(2, 0), get_aux(2, 2)), get_aux(2, 4))

    cu2 = [alpha * get_cx(m, 2) for m in range(5)]
    cu3 = [alpha * get_cx(m, 3) for m in range(5)]
    args = (un, ut, us, qh, b1, ic)
    mid_p = characteristic([get_cx(5 + m, 2) + cu2[m] for m in range(5)], *args)
    mid_m = characteristic([get_cx(5 + m, 3) - cu3[m] for m in range(5)], *args)
    xu = {o: [alpha * get_cx(10 + m, o) for m in range(5)] for o in range(1, 5)}
    xp = {}
    xm = {}
    for o in (1, 2, 3, 4):
        xf = [get_cx(15 + m, o) for m in range(5)]
        if o <= 3:
            xp[o] = characteristic([xf[m] + xu[o][m] for m in range(5)], *args)
        if o >= 2:
            xm[o] = characteristic([xf[m] - xu[o][m] for m in range(5)], *args)
    g = []
    for m in range(5):
        eps = 4.0 * weno_eps if m in (0, 4) else weno_eps
        up = weno_excess(mid_p[m], xp[1][m], xp[2][m], xp[3][m], 1, eps)
        down = weno_excess(mid_m[m], xm[4][m], xm[3][m], xm[2][m], -1, eps)
        g.append(up + down)
    h2, h3, h4 = (g[m] + g[m] for m in (1, 2, 3))
    h15 = g[0] + g[4]
    dh = c * (g[4] - g[0])
    rr = h15 + h2
    upd = (
        rr,
        un * rr + dh,
        ut * rr + h3,
        us * rr + h4,
        enth * h15 + un * dh + qh * h2 + ut * h3 + us * h4,
    )
    return [
        (get_cx(20 + m, 2) + get_cx(20 + m, 3)) + (xu[3][m] - xu[2][m]) + upd[m] for m in range(5)
    ]


def sweep(prim, uf, aux, cx, flux, store, s, cell_tiles, pair_tiles, diff_tiles, face_tiles, out_tiles, comps):
    order = (0, 1 + comps[0], 1 + comps[1], 1 + comps[2], 4)

    def rows(i, offset=0):
        return pl.ds(pl.multiple_of(i * 8, 8) + offset, 8)

    @pl.loop(0, cell_tiles)
    def _(i):
        here = rows(i)
        state, fl, enth, root, sig = cell_values([prim[k, here, :] for k in range(5)], i, comps)
        for m in range(5):
            uf[m, here, :] = state[m]
            uf[5 + m, here, :] = fl[m]
        aux[0, here, :] = enth
        aux[1, here, :] = root
        aux[3, here, :] = sig

    @pl.loop(0, diff_tiles)
    def _(i):
        here = rows(i)
        for m in range(10):
            a, b, c = uf[m, here, :], uf[m, rows(i, s), :], uf[m, rows(i, 2 * s), :]
            both = a + c
            second = (0.5 * both - b) * KX
            cx[m, here, :] = 0.25 * (c - a)
            cx[10 + m, here, :] = second
            if m >= 5:
                cx[15 + m, here, :] = (0.5 / KB) * b - (1.0 / (6.0 * KB * KX)) * second

    @pl.loop(0, pair_tiles)
    def _(i):
        aux[2, rows(i), :] = jnp.maximum(aux[3, rows(i), :], aux[3, rows(i, s), :])

    @pl.loop(0, face_tiles)
    def _(i):
        values = face_values(
            lambda k, o: prim[k, rows(i, o * s), :],
            lambda k, o: aux[k, rows(i, o * s), :],
            lambda k, o: cx[k, rows(i, (o - 1) * s), :],
            comps,
        )
        for m in range(5):
            flux[order[m], rows(i), :] = values[m]

    if store is not None:

        @pl.loop(0, out_tiles)
        def _(i):
            store(i, [flux[k, rows(i, s), :] - flux[k, rows(i), :] for k in range(5)])


def prepare_kernel(nx, ny, nz, xeven, yeven, rho_ref, vel_ref, p_ref, q_ref, qt_ref, xa_ref, xb_ref, y_ref, z_ref, top_ref):
    rows, w = ny, nz
    n = nx * ny
    for k in range(5):
        for x in range(nx):
            src = rho_ref[x] if k == 0 else p_ref[x] if k == 4 else vel_ref[k - 1, x]
            q_ref[k, x * ny : (x + 1) * ny, :] = src
    top = None
    for i in range(n // 8):
        here = slice(8 * i, 8 * i + 8)
        sound = jnp.sqrt(gamma_gas * q_ref[4, here, :] / q_ref[0, here, :])
        speed = jnp.abs(q_ref[1, here, :]) + jnp.abs(q_ref[2, here, :]) + jnp.abs(q_ref[3, here, :]) + 3.0 * sound
        top = speed if top is None else jnp.maximum(top, speed)
    top_ref[...] = top
    width = 3 * ny
    high = (nx - 3) * ny
    if xeven:
        odd = lax.rem(lax.axis_index("gx"), 2)
        start_a = pl.multiple_of((1 - odd) * high, 8)
        start_b = pl.multiple_of(odd * high, 8)
    else:
        start_a, start_b = high, 0
    for k in range(5):
        xa_ref[k * width : (k + 1) * width, :] = q_ref[k, pl.ds(start_a, width), :]
        xb_ref[k * width : (k + 1) * width, :] = q_ref[k, pl.ds(start_b, width), :]
    xa_ref[5 * width : 5 * width + 8, :] = top
    edge = y_ref.shape[1]
    pad = edge - 15 * nx
    if pad:
        y_ref[0, 15 * nx :, :] = jnp.zeros((pad, w), f32)
        y_ref[1, 15 * nx :, :] = jnp.zeros((pad, w), f32)
    for k in range(5):
        for x in range(nx):
            at = (k * nx + x) * 3
            y_ref[0, at : at + 3, :] = q_ref[k, x * ny : x * ny + 3, :]
            y_ref[1, at : at + 3, :] = q_ref[k, (x + 1) * ny - 3 : (x + 1) * ny, :]
    z_ref[...] = jnp.zeros(z_ref.shape, f32)
    for k in range(5):
        qt_ref[k] = q_ref[k].T
        z_ref[0, 3 * k : 3 * k + 3, :] = qt_ref[k, 0:3, :]
        z_ref[1, 3 * k : 3 * k + 3, :] = qt_ref[k, nz - 3 : nz, :]


def x_kernel(nx, ny, xeven, q_ref, a_ref, b_ref, out_ref, prim, uf, aux, cx, flux):
    width = 3 * ny
    n = nx * ny
    far = (nx + 3) * ny
    if xeven:
        odd = lax.rem(lax.axis_index("gx"), 2)
        at_a = pl.multiple_of((1 - odd) * far, 8)
        at_b = pl.multiple_of(odd * far, 8)
    else:
        at_a, at_b = 0, far
    for k in range(5):
        prim[k, pl.ds(at_a, width), :] = a_ref[k * width : (k + 1) * width, :]
        prim[k, pl.ds(at_b, width), :] = b_ref[k * width : (k + 1) * width, :]
        prim[k, width : width + n, :] = q_ref[k]

    def store(i, values):
        for k in range(5):
            out_ref[k, pl.ds(pl.multiple_of(i * 8, 8), 8), :] = values[k]

    t = ny // 8
    sweep(prim, uf, aux, cx, flux, store, ny, (nx + 6) * t, (nx + 5) * t, (nx + 4) * t, (nx + 1) * t, nx * t, (0, 1, 2))


def y_kernel(nx, ny, block, q_ref, lo_ref, hi_ref, out_ref, prim, uf, aux, cx, flux):
    for k in range(5):
        for x in range(nx):
            at = (k * nx + x) * 3
            prim[k, x * block : x * block + 3, :] = lo_ref[at : at + 3, :]
            prim[k, x * block + 3 : x * block + 3 + ny, :] = q_ref[k, x * ny : (x + 1) * ny, :]
            prim[k, x * block + 3 + ny : x * block + 6 + ny, :] = hi_ref[at : at + 3, :]

    tiles = nx * block // 8

    sweep(prim, uf, aux, cx, flux, None, 1, tiles, tiles, tiles, tiles, 0, (1, 0, 2))
    for x in range(nx):
        for k in range(5):
            base = x * block
            out_ref[k, x * ny : (x + 1) * ny, :] = flux[k, base + 1 : base + 1 + ny, :] - flux[k, base : base + ny, :]


def z_kernel(n, nz, qt_ref, lo_ref, hi_ref, out_ref, prim, uf, aux, cx, flux):
    for k in range(5):
        prim[k, 0:3, :] = lo_ref[3 * k : 3 * k + 3, :]
        prim[k, 3 : 3 + nz, :] = qt_ref[k]
        prim[k, 3 + nz : 6 + nz, :] = hi_ref[3 * k : 3 * k + 3, :]
    tiles = rup(nz + 6, 8) // 8
    sweep(prim, uf, aux, cx, flux, None, 1, tiles, tiles, tiles, rup(nz + 1, 8) // 8, 0, (2, 0, 1))
    for k in range(5):
        out_ref[k] = (flux[k, 1 : nz + 1, :] - flux[k, 0:nz, :]).T


def final_kernel(nx, ny, q_ref, tx_ref, ty_ref, tz_ref, top_ref, out_ref):
    step = (cfl_number * KB) / jnp.max(top_ref[...], keepdims=True)
    for x in range(nx):
        here = slice(x * ny, (x + 1) * ny)
        rho, u1, u2, u3, p = (q_ref[k, here, :] for k in range(5))
        m1, m2, m3 = rho * u1, rho * u2, rho * u3
        energy = 2.5 * p + 0.5 * (m1 * u1 + m2 * u2 + m3 * u3)
        for k, value in enumerate((rho, m1, m2, m3, energy)):
            out_ref[k, x] = value - step * (tx_ref[k, here, :] + ty_ref[k, here, :] + tz_ref[k, here, :])


def call(kernel, outs, flops, scratch=()):
    return pl.pallas_call(
        kernel,
        out_shape=outs,
        scratch_shapes=scratch,
        compiler_params=pltpu.CompilerParams(vmem_limit_bytes=VMEM_LIMIT),
        cost_estimate=pl.CostEstimate(flops=flops, bytes_accessed=1000000, transcendentals=0),
    )


def sweep_scratch(rows, w):
    return [
        pltpu.VMEM((5, rows, w), f32),
        pltpu.VMEM((10, rows, w), f32),
        pltpu.VMEM((4, rows, w), f32),
        pltpu.VMEM((25, rows, w), f32),
        pltpu.VMEM((5, rows, w), f32),
    ]


def pairs_a(n):
    return [(i, i ^ 1) for i in range(n)]


def pairs_b(n):
    return [(i, (i + 1) % n if i % 2 else (i - 1) % n) for i in range(n)]


def top_over(top, axis, first):
    n = lax.axis_size(axis)
    if n & (n - 1):
        return lax.pmax(top, axis)
    d = first
    while d < n:
        top = jnp.maximum(top, lax.ppermute(top, axis, [(i, i ^ d) for i in range(n)]))
        d *= 2
    return top


def edge_trade(axis, low, high, top):
    n = lax.axis_size(axis)
    size = low.shape[0]
    if n == 1:
        return high, low, top
    if n == 2:
        got = lax.ppermute(jnp.concatenate([low, high, top]), axis, [(0, 1), (1, 0)])
        return got[size : 2 * size], got[:size], jnp.maximum(top, got[2 * size :])
    if n % 2:
        lower = lax.ppermute(high, axis, [(i, (i + 1) % n) for i in range(n)])
        upper = lax.ppermute(low, axis, [((i + 1) % n, i) for i in range(n)])
        return lower, upper, lax.pmax(top, axis)
    odd = lax.rem(lax.axis_index(axis), 2) == 1
    got_a = lax.ppermute(jnp.concatenate([jnp.where(odd, low, high), top]), axis, pairs_a(n))
    top = jnp.maximum(top, got_a[size:])
    send_b = jnp.where(odd, high, low)
    if n == 4:
        got_b = lax.ppermute(jnp.concatenate([send_b, top]), axis, pairs_b(n))
        top = jnp.maximum(top, got_b[size:])
    else:
        got_b = lax.ppermute(send_b, axis, pairs_b(n))
        top = top_over(top, axis, 2)
    lower = jnp.where(odd, got_a[:size], got_b[:size])
    upper = jnp.where(odd, got_b[:size], got_a[:size])
    return lower, upper, top


def local(density, velocity, pressure):
    nx, ny, nz = density.shape
    n = nx * ny
    gx = lax.axis_size("gx")
    xeven = gx % 2 == 0
    width = 15 * ny
    yrows = rup(15 * nx, 8)
    S = jax.ShapeDtypeStruct
    q, qt, xa, xb, ye, ze, top = call(
        functools.partial(prepare_kernel, nx, ny, nz, xeven, True),
        (
            S((5, n, nz), f32),
            S((5, nz, n), f32),
            S((width + 8, nz), f32),
            S((width, nz), f32),
            S((2, yrows, nz), f32),
            S((2, 16, n), f32),
            S((8, nz), f32),
        ),
        2000000,
    )(density, velocity, pressure)

    if xeven:
        got_b = lax.ppermute(xb, "gx", pairs_b(gx))
        got_a = lax.ppermute(xa, "gx", pairs_a(gx))
        top = jnp.maximum(top, got_a[width:])
    else:
        got_a = lax.ppermute(xa, "gx", [(i, (i + 1) % gx) for i in range(gx)])
        got_b = lax.ppermute(xb, "gx", [((i + 1) % gx, i) for i in range(gx)])
    ztop = top if n == nz else jnp.full((8, n), jnp.max(top))
    zlo, zhi, ztop = edge_trade("gz", ze[0], ze[1], ztop)
    top = ztop if n == nz else jnp.full((8, nz), jnp.max(ztop))
    ylo, yhi, top = edge_trade("gy", ye[0], ye[1], top)
    top = top_over(top, "gx", 2 if xeven else 1)

    sweep_flops = 16000000
    xr = (nx + 6) * ny
    tx = call(
        functools.partial(x_kernel, nx, ny, xeven), S((5, n, nz), f32), sweep_flops, sweep_scratch(xr, nz)
    )(q, got_a, got_b)
    zr = rup(nz + 6, 8) + 16
    tz = call(functools.partial(z_kernel, n, nz), S((5, n, nz), f32), sweep_flops, sweep_scratch(zr, n))(
        qt, zlo, zhi
    )
    block = rup(ny + 6, 8)
    yr = nx * block + 16
    ty = call(
        functools.partial(y_kernel, nx, ny, block), S((5, n, nz), f32), sweep_flops, sweep_scratch(yr, nz)
    )(q, ylo, yhi)
    return call(functools.partial(final_kernel, nx, ny), S((5, nx, ny, nz), f32), 1000000)(q, tx, ty, tz, top)


def solution(mesh):
    in_specs = (P("gx", "gy", "gz"), P(None, "gx", "gy", "gz"), P("gx", "gy", "gz"))
    out_specs = P(None, "gx", "gy", "gz")
    return jax.shard_map(local, mesh=mesh, in_specs=in_specs, out_specs=out_specs, check_vma=False)
```

time: 79 us -> 28.1 us (0.36)
  the two profiles are of different devices: /device:TPU:1 before, /device:TPU:0 now
where the time goes in v1:
time: 28.1 us; the launch traced here: 27.9 us
  starting transfers between devices  11.5 us (41%)
  Pallas kernels  10.7 us (38%)
  waiting for transfers between devices  3 us (11%)
  local copies, waits for them, and re-layouts  2.61 us (9%)
    pallas_call x1, Pallas kernels, local(): call(functools.partial(x_kernel, nx, ny, xeven), S((5, n, nz), f32), swee...  4.09 us
    ppermute x1, starting transfers between devices, edge_trade(): got_b = lax.ppermute(jnp.concatenate([send_b, top]), axis, pairs_b(n))  3.53 us
    pallas_call x1, Pallas kernels, local(): call(functools.partial(y_kernel, nx, ny, block), S((5, n, nz), f32), swee...  2.92 us
    unnamed x6, local copies, waits for them, and re-layouts  2.6 us
    ppermute x1, starting transfers between devices, local(): got_b = lax.ppermute(xb, 'gx', pairs_b(gx))  2.59 us
    pallas_call x1, Pallas kernels, local(): call(functools.partial(z_kernel, n, nz), S((5, n, nz), f32), sweep_flops,...  2.57 us
    ppermute x1, waiting for transfers between devices, edge_trade(): lax.ppermute(jnp.concatenate([low, high, top]), axis, [(0, 1), (1, 0)])  2.25 us
    ppermute x1, starting transfers between devices, edge_trade(): lax.ppermute(jnp.concatenate([jnp.where(odd, low, high), top]), axis, pai...  1.63 us
  transfers between devices with their start and end apart: 6, of which 2 were waited for; matrix products, arithmetic and copies ran while one was open for 0% of the time, Pallas kernels for 34%

profile of v1, /device:TPU:0, one launch (start us, length us, event | category | flops | bytes accessed | tf_op | source)
XLA Modules:
  0.0 27.9 jit_solution(5120340121572037836)
XLA Ops:
  0.0 0.0 copy-start
  0.0 0.9 %copy-done = f32[3,4,32,128]{3,2,1,0:T(8,128)S(1)} copy-done((f32[3,4,32,128]{3,2,1,0:T(8,128)S(1)}, f32[3,4,32,128]{3,2,1,0:T(8,128)}, u32[]{:S(2)}) %copy-start) | copy-done | bytes 196632
  0.9 0.0 copy-start.1
  0.9 0.8 %copy-done.1 = f32[4,32,128]{2,1,0:T(8,128)S(1)} copy-done((f32[4,32,128]{2,1,0:T(8,128)S(1)}, f32[4,32,128]{2,1,0:T(8,128)}, u32[]{:S(2)}) %copy-start.1) | copy-done | bytes 65560
  1.8 0.0 copy-start.2
  1.8 0.8 %copy-done.2 = f32[4,32,128]{2,1,0:T(8,128)S(1)} copy-done((f32[4,32,128]{2,1,0:T(8,128)S(1)}, f32[4,32,128]{2,1,0:T(8,128)}, u32[]{:S(2)}) %copy-start.2) | copy-done | bytes 65560
  2.6 0.2 shard_map.37
  2.8 0.6 %collective-permute-start = (f32[488,128]{1,0:T(8,128)S(1)}, f32[488,128]{1,0:T(8,128)S(1)}, u32[]{:S(2)}, u32[]{:S(2)}) collective-permute-start(f32[488,128]{1,0:T(8,128)S(1)} %get-tuple-element.13), channel_id=1, source_target_pairs={{0,8},{8,0},{16,24},{24,16},{1,9},{9,1},{17,25},{25,17},{2,10},{10... | collective-permute-start | bytes 749576 | tf_op jit(solution)/shard_map/ppermute | solution.py:366
  3.4 2.6 %collective-permute-start.1 = (f32[480,128]{1,0:T(8,128)S(1)}, f32[480,128]{1,0:T(8,128)S(1)}, u32[]{:S(2)}, u32[]{:S(2)}) collective-permute-start(f32[480,128]{1,0:T(8,128)S(1)} %get-tuple-element.14), channel_id=1, source_target_pairs={{0,24},{8,16},{16,8},{24,0},{1,25},{9,17},{17,9},{25,1},{2,26},{10... | collective-permute-start | bytes 737288 | tf_op jit(solution)/shard_map/ppermute | solution.py:365
  6.0 0.0 collective-permute-done.a_ref
  6.0 1.6 %collective-permute-start.2 = (f32[40,128]{1,0:T(8,128)S(1)}, f32[40,128]{1,0:T(8,128)S(1)}, u32[]{:S(2)}, u32[]{:S(2)}) collective-permute-start(f32[40,128]{1,0:T(8,128)S(1)} %pad_maximum_fusion.2), channel_id=1, source_target_pairs={{0,1},{1,0},{2,3},{3,2},{4,5},{5,4},{6,7},{7,6},{8,9},{9,8},{10,11... | collective-permute-start | bytes 61448 | tf_op jit(solution)/shard_map/ppermute | solution.py:321
  7.6 2.3 %collective-permute-done.2 = f32[40,128]{1,0:T(8,128)S(1)} collective-permute-done((f32[40,128]{1,0:T(8,128)S(1)}, f32[40,128]{1,0:T(8,128)S(1)}, u32[]{:S(2)}, u32[]{:S(2)}) %collective-permute-start.2) | collective-permute-done | bytes 20512 | tf_op jit(solution)/shard_map/ppermute | solution.py:321
  9.9 1.6 %collective-permute-start.3 = (f32[72,128]{1,0:T(8,128)S(1)}, f32[72,128]{1,0:T(8,128)S(1)}, u32[]{:S(2)}, u32[]{:S(2)}) collective-permute-start(f32[72,128]{1,0:T(8,128)S(1)} %pad_maximum_fusion), channel_id=1, source_target_pairs={{0,2},{2,0},{4,6},{6,4},{1,3},{3,1},{5,7},{7,5},{8,10},{10,8},{12,... | collective-permute-start | bytes 110600 | tf_op jit(solution)/shard_map/ppermute | solution.py:328
  11.5 0.7 %collective-permute-done.1.b_ref = f32[480,128]{1,0:T(8,128)S(1)} collective-permute-done((f32[480,128]{1,0:T(8,128)S(1)}, f32[480,128]{1,0:T(8,128)S(1)}, u32[]{:S(2)}, u32[]{:S(2)}) %collective-permute-start.1) | collective-permute-done | bytes 245792 | tf_op jit(solution)/shard_map/ppermute | solution.py:365
  12.2 4.1 %shard_map.38.tx_ref = f32[5,128,128]{2,1,0:T(8,128)S(1)} custom-call(f32[5,128,128]{2,1,0:T(8,128)S(1)} %get-tuple-element.12.q_ref, f32[488,128]{1,0:T(8,128)S(1)} %collective-permute-done.a_ref, f32[480,128]{1,0:T(8,128)S(1)} %collective-permute-done.1.b_ref), custom_call_target="tpu_custom_call" | custom-call | flops 16000000 | bytes 1000000 | tf_op jit(solution)/shard_map/pallas_call | solution.py:379
  16.3 0.0 collective-permute-done.3
  16.4 3.5 %collective-permute-start.4 = (f32[72,128]{1,0:T(8,128)S(1)}, f32[72,128]{1,0:T(8,128)S(1)}, u32[]{:S(2)}, u32[]{:S(2)}) collective-permute-start(f32[72,128]{1,0:T(8,128)S(1)} %pad_maximum_fusion.1), channel_id=1, source_target_pairs={{0,6},{2,4},{4,2},{6,0},{1,7},{3,5},{5,3},{7,1},{8,14},{10,12},{12... | collective-permute-start | bytes 110600 | tf_op jit(solution)/shard_map/ppermute | solution.py:332
  19.9 2.6 %shard_map.40.tz_ref = f32[5,128,128]{2,1,0:T(8,128)S(1)} custom-call(f32[5,128,128]{2,1,0:T(8,128)S(1)} %get-tuple-element.18.qt_ref, f32[16,128]{1,0:T(8,128)S(1)} %get-tuple-element.24.lo_ref, f32[16,128]{1,0:T(8,128)S(1)} %get-tuple-element.23.hi_ref), custom_call_target="tpu_custom_call" | custom-call | flops 16000000 | bytes 1000000 | tf_op jit(solution)/shard_map/pallas_call | solution.py:383
  22.5 0.0 collective-permute-done.4
  22.5 1.6 %collective-permute-start.5 = (f32[8,128]{1,0:T(8,128)S(1)}, f32[8,128]{1,0:T(8,128)S(1)}, u32[]{:S(2)}, u32[]{:S(2)}) collective-permute-start(f32[8,128]{1,0:T(8,128)S(1)} %slice_maximum_fusion), channel_id=1, source_target_pairs={{0,16},{8,24},{16,0},{24,8},{1,17},{9,25},{17,1},{25,9},{2,18},{10... | collective-permute-start | bytes 12296 | tf_op jit(solution)/shard_map/ppermute | solution.py:310
  24.1 2.9 %shard_map.39.ty_ref = f32[5,128,128]{2,1,0:T(8,128)S(1)} custom-call(f32[5,128,128]{2,1,0:T(8,128)S(1)} %get-tuple-element.12.q_ref, f32[64,128]{1,0:T(8,128)S(1)} %get-tuple-element.20.lo_ref, f32[64,128]{1,0:T(8,128)S(1)} %get-tuple-element.19.hi_ref), custom_call_target="tpu_custom_call" | custom-call | flops 16000000 | bytes 1000000 | tf_op jit(solution)/shard_map/pallas_call | solution.py:388
  27.0 0.0 collective-permute-done.5
  27.0 0.9 %shard_map.41 = f32[5,4,32,128]{3,2,1,0:T(8,128)} custom-call(f32[5,128,128]{2,1,0:T(8,128)S(1)} %get-tuple-element.12.q_ref, f32[5,128,128]{2,1,0:T(8,128)S(1)} %shard_map.38.tx_ref, f32[5,128,128]{2,1,0:T(8,128)S(1)} %shard_map.39.ty_ref, f32[5,128,128]{2,1,0:T(8,128)S(1)} %shard_map.40.tz_ref, f32[8,128]{1,0:T(8,128)S(1)} %max.19.top_ref), custom_call_target="tpu_custom_call" | custom-call | flops 1000000 | bytes 1000000 | tf_op jit(solution)/shard_map/pallas_call | solution.py:391
  (12 shorter events, 0.1 us)
Async XLA Ops:
  0.0 0.9 %copy-start = (f32[3,4,32,128]{3,2,1,0:T(8,128)S(1)}, f32[3,4,32,128]{3,2,1,0:T(8,128)}, u32[]{:S(2)}) copy-start(f32[3,4,32,128]{3,2,1,0:T(8,128)} %vel_ref.1) | copy-start | bytes 589828
  0.9 0.8 %copy-start.1 = (f32[4,32,128]{2,1,0:T(8,128)S(1)}, f32[4,32,128]{2,1,0:T(8,128)}, u32[]{:S(2)}) copy-start(f32[4,32,128]{2,1,0:T(8,128)} %rho_ref.1) | copy-start | bytes 196612
  1.8 0.8 %copy-start.2 = (f32[4,32,128]{2,1,0:T(8,128)S(1)}, f32[4,32,128]{2,1,0:T(8,128)}, u32[]{:S(2)}) copy-start(f32[4,32,128]{2,1,0:T(8,128)} %p_ref.1) | copy-start | bytes 196612
  2.8 3.2 %collective-permute-start = (f32[488,128]{1,0:T(8,128)S(1)}, f32[488,128]{1,0:T(8,128)S(1)}, u32[]{:S(2)}, u32[]{:S(2)}) collective-permute-start(f32[488,128]{1,0:T(8,128)S(1)} %get-tuple-element.13), channel_id=1, source_target_pairs={{0,8},{8,0},{16,24},{24,16},{1,9},{9,1},{17,25},{25,17},{2,10},{10... | collective-permute-start | bytes 749576 | tf_op jit(solution)/shard_map/ppermute | solution.py:366
  3.4 8.8 %collective-permute-start.1 = (f32[480,128]{1,0:T(8,128)S(1)}, f32[480,128]{1,0:T(8,128)S(1)}, u32[]{:S(2)}, u32[]{:S(2)}) collective-permute-start(f32[480,128]{1,0:T(8,128)S(1)} %get-tuple-element.14), channel_id=1, source_target_pairs={{0,24},{8,16},{16,8},{24,0},{1,25},{9,17},{17,9},{25,1},{2,26},{10... | collective-permute-start | bytes 737288 | tf_op jit(solution)/shard_map/ppermute | solution.py:365
  6.0 3.8 %collective-permute-start.2 = (f32[40,128]{1,0:T(8,128)S(1)}, f32[40,128]{1,0:T(8,128)S(1)}, u32[]{:S(2)}, u32[]{:S(2)}) collective-permute-start(f32[40,128]{1,0:T(8,128)S(1)} %pad_maximum_fusion.2), channel_id=1, source_target_pairs={{0,1},{1,0},{2,3},{3,2},{4,5},{5,4},{6,7},{7,6},{8,9},{9,8},{10,11... | collective-permute-start | bytes 61448 | tf_op jit(solution)/shard_map/ppermute | solution.py:321
  9.9 6.5 %collective-permute-start.3 = (f32[72,128]{1,0:T(8,128)S(1)}, f32[72,128]{1,0:T(8,128)S(1)}, u32[]{:S(2)}, u32[]{:S(2)}) collective-permute-start(f32[72,128]{1,0:T(8,128)S(1)} %pad_maximum_fusion), channel_id=1, source_target_pairs={{0,2},{2,0},{4,6},{6,4},{1,3},{3,1},{5,7},{7,5},{8,10},{10,8},{12,... | collective-permute-start | bytes 110600 | tf_op jit(solution)/shard_map/ppermute | solution.py:328
  16.4 6.1 %collective-permute-start.4 = (f32[72,128]{1,0:T(8,128)S(1)}, f32[72,128]{1,0:T(8,128)S(1)}, u32[]{:S(2)}, u32[]{:S(2)}) collective-permute-start(f32[72,128]{1,0:T(8,128)S(1)} %pad_maximum_fusion.1), channel_id=1, source_target_pairs={{0,6},{2,4},{4,2},{6,0},{1,7},{3,5},{5,3},{7,1},{8,14},{10,12},{12... | collective-permute-start | bytes 110600 | tf_op jit(solution)/shard_map/ppermute | solution.py:332
  22.5 4.5 %collective-permute-start.5 = (f32[8,128]{1,0:T(8,128)S(1)}, f32[8,128]{1,0:T(8,128)S(1)}, u32[]{:S(2)}, u32[]{:S(2)}) collective-permute-start(f32[8,128]{1,0:T(8,128)S(1)} %slice_maximum_fusion), channel_id=1, source_target_pairs={{0,16},{8,24},{16,0},{24,8},{1,17},{9,25},{17,1},{25,9},{2,18},{10... | collective-permute-start | bytes 12296 | tf_op jit(solution)/shard_map/ppermute | solution.py:310

commit v2 on v1

v2 whole, which is shorter than its diff:
```python
import functools
import math

import jax
import jax.numpy as jnp
from jax import lax
from jax.experimental import pallas as pl
from jax.experimental.pallas import tpu as pltpu
from jax.sharding import PartitionSpec as P

gamma_gas = 1.4
weno_eps = 1e-06
cfl_number = 0.4
f32 = jnp.float32

KX = math.sqrt(13.0 / 12.0)
KT = 0.5 / KX
KB = 1.0 / (6.0 * KX)
VMEM_LIMIT = 24 * 1024 * 1024


def rup(n, m):
    return (n + m - 1) // m * m


def rows(i, offset=0):
    return pl.ds(pl.multiple_of(i * 8, 8) + offset, 8)


def over(count, unroll, body):
    whole = count // unroll
    if whole:

        @pl.loop(0, whole)
        def _(j):
            for u in range(unroll):
                body(j * unroll + u)

    for i in range(whole * unroll, count):
        body(i)


def cell_pass(prim, uf, aux, count, comps):
    def body(i):
        here = rows(i)
        rho, p = prim[0, here, :], prim[4, here, :]
        un, ut, us = (prim[1 + c, here, :] for c in comps)
        inv = 1.0 / rho
        mn, mt, ms = rho * un, rho * ut, rho * us
        mnun = mn * un
        energy = 2.5 * p + 0.5 * (mnun + mt * ut + ms * us)
        total = energy + p
        values = (rho, mn, mt, ms, energy, mn, mnun + p, mt * un, ms * un, total * un)
        for m in range(10):
            uf[m, here, :] = values[m]
        aux[0, here, :] = total * inv
        aux[1, here, :] = jnp.sqrt(rho)
        aux[3, here, :] = jnp.abs(un) + jnp.sqrt(gamma_gas * p * inv)

    over(count, 4, body)


def diff_pass(uf, aux, cx, count, pairs, s):
    def body(i):
        here = rows(i)
        for m in range(10):
            a, b, c = uf[m, here, :], uf[m, rows(i, s), :], uf[m, rows(i, 2 * s), :]
            second = (0.5 * (a + c) - b) * KX
            cx[m, here, :] = 0.25 * (c - a)
            cx[10 + m, here, :] = second
            if m >= 5:
                cx[15 + m, here, :] = (0.5 / KB) * b - (1.0 / (6.0 * KB * KX)) * second

    def pair(i):
        aux[2, rows(i), :] = jnp.maximum(aux[3, rows(i), :], aux[3, rows(i, s), :])

    over(count, 2, body)
    over(pairs, 8, pair)


def weno_excess(mid, xa, xb, xc, sign, eps):
    tau_a = xa - xb
    tau_c = xb - xc
    if sign > 0:
        mid_a = mid + KT * tau_a
        mid_c = mid + KT * tau_c
    else:
        mid_a = mid - KT * tau_a
        mid_c = mid - KT * tau_c
    sm_a = mid_a * mid_a + (xa * xa + eps)
    sm_b = mid * mid + (xb * xb + eps)
    sm_c = mid_c * mid_c + (xc * xc + eps)
    ga = 3.0 * (sm_a * sm_a)
    gb = sm_b * sm_b
    gc = sm_c * sm_c
    gc = gc + gc
    num = gb * (tau_a * gc + tau_c * ga)
    den = gb * gc + (ga + ga) * (gb + gc)
    return num / den


def characteristic(v, un, ut, us, qh, b1, ic):
    t = (qh * v[0] - un * v[1]) - (ut * v[2] + us * v[3]) + v[4]
    a = b1 * t
    n = (un * v[0] - v[1]) * ic
    return (a + n, v[0] - a, v[2] - ut * v[0], v[3] - us * v[0], a - n)


def face_average(prim, aux, i, s, comps):
    def at(ref, k, o):
        return ref[k, rows(i, o * s), :]

    rl, rr = at(aux, 1, 2), at(aux, 1, 3)
    share = rr / (rl + rr)

    def roe(ref, k):
        left, right = at(ref, k, 2), at(ref, k, 3)
        return left + share * (right - left)

    un, ut, us = (roe(prim, 1 + c) for c in comps)
    enth = roe(aux, 0)
    qh = 0.5 * (un * un + ut * ut + us * us)
    c2 = (gamma_gas - 1.0) * (enth - qh)
    ic = lax.rsqrt(c2)
    b1 = (gamma_gas - 1.0) * (ic * ic)
    alpha = jnp.maximum(jnp.maximum(at(aux, 2, 0), at(aux, 2, 2)), at(aux, 2, 4))
    return un, ut, us, enth, qh, c2 * ic, ic, b1, alpha


def face_values(get_cx, average):
    un, ut, us, enth, qh, c, ic, b1, alpha = average
    args = (un, ut, us, qh, b1, ic)
    mid_p = characteristic([get_cx(5 + m, 2) + alpha * get_cx(m, 2) for m in range(5)], *args)
    mid_m = characteristic([get_cx(5 + m, 3) - alpha * get_cx(m, 3) for m in range(5)], *args)
    xu = {o: [alpha * get_cx(10 + m, o) for m in range(5)] for o in range(1, 5)}
    xp = {}
    xm = {}
    for o in (1, 2, 3, 4):
        xf = [get_cx(15 + m, o) for m in range(5)]
        if o <= 3:
            xp[o] = characteristic([xf[m] + xu[o][m] for m in range(5)], *args)
        if o >= 2:
            xm[o] = characteristic([xf[m] - xu[o][m] for m in range(5)], *args)
    g = []
    for m in range(5):
        eps = 4.0 * weno_eps if m in (0, 4) else weno_eps
        up = weno_excess(mid_p[m], xp[1][m], xp[2][m], xp[3][m], 1, eps)
        down = weno_excess(mid_m[m], xm[4][m], xm[3][m], xm[2][m], -1, eps)
        g.append(up + down)
    h2, h3, h4 = (g[m] + g[m] for m in (1, 2, 3))
    h15 = g[0] + g[4]
    dh = c * (g[4] - g[0])
    rr = h15 + h2
    upd = (
        rr,
        un * rr + dh,
        ut * rr + h3,
        us * rr + h4,
        enth * h15 + un * dh + qh * h2 + ut * h3 + us * h4,
    )
    return [
        (get_cx(20 + m, 2) + get_cx(20 + m, 3)) + (xu[3][m] - xu[2][m]) + upd[m] for m in range(5)
    ]


def face_pass(prim, aux, cx, count, s, comps, put):
    order = (0, 1 + comps[0], 1 + comps[1], 1 + comps[2], 4)

    def step(i, average):
        ahead = face_average(prim, aux, i + 1, s, comps)
        values = face_values(lambda k, o: cx[k, rows(i, (o - 1) * s), :], average)
        for m in range(5):
            put(order[m], i, values[m])
        return ahead

    lax.fori_loop(0, count, step, face_average(prim, aux, 0, s, comps))


def prepare_kernel(nx, ny, nz, xeven, rho, vel, p, q_ref, qt_ref, xa_ref, xb_ref, y_ref, z_ref, top_ref, sems):
    n = nx * ny
    sources = (rho, vel.at[0], vel.at[1], vel.at[2], p)
    copies = [
        pltpu.make_async_copy(src, q_ref.at[k, pl.ds(0, n), :], sems.at[k])
        for k, src in enumerate(sources)
    ]
    for copy in copies:
        copy.start()
    for copy in copies:
        copy.wait()
    top = None
    for i in range(n // 8):
        here = slice(8 * i, 8 * i + 8)
        sound = jnp.sqrt(gamma_gas * q_ref[4, here, :] / q_ref[0, here, :])
        speed = (jnp.abs(q_ref[1, here, :]) + jnp.abs(q_ref[2, here, :])) + (
            jnp.abs(q_ref[3, here, :]) + 3.0 * sound
        )
        top = speed if top is None else jnp.maximum(top, speed)
    top_ref[...] = top
    width = 3 * ny
    high = (nx - 3) * ny
    if xeven:
        odd = lax.rem(lax.axis_index("gx"), 2)
        start_a = pl.multiple_of((1 - odd) * high, 8)
        start_b = pl.multiple_of(odd * high, 8)
    else:
        start_a, start_b = high, 0
    for k in range(5):
        xa_ref[k * width : (k + 1) * width, :] = q_ref[k, pl.ds(start_a, width), :]
        xb_ref[k * width : (k + 1) * width, :] = q_ref[k, pl.ds(start_b, width), :]
    xa_ref[5 * width : 5 * width + 8, :] = top
    pad = y_ref.shape[1] - 15 * nx
    for side in (0, 1):
        if pad:
            y_ref[side, 15 * nx :, :] = jnp.zeros((pad, nz), f32)
        for k in range(5):
            for e in range(3):
                at = (3 * k + e) * nx
                row = e + side * (ny - 3)
                y_ref[side, at : at + nx, :] = q_ref[k, pl.ds(row, nx, stride=ny), :]
    z_ref[...] = jnp.zeros(z_ref.shape, f32)
    for k in range(5):
        qt_ref[k, 0:nz, :] = q_ref[k, 0:n, :].T
        z_ref[0, 3 * k : 3 * k + 3, :] = qt_ref[k, 0:3, :]
        z_ref[1, 3 * k : 3 * k + 3, :] = qt_ref[k, nz - 3 : nz, :]


def x_kernel(nx, ny, xeven, q_ref, a_ref, b_ref, after, out_ref, prim, uf, aux, cx, flux):
    width = 3 * ny
    n = nx * ny
    far = (nx + 3) * ny
    if xeven:
        odd = lax.rem(lax.axis_index("gx"), 2)
        at_a = pl.multiple_of((1 - odd) * far, 8)
        at_b = pl.multiple_of(odd * far, 8)
    else:
        at_a, at_b = 0, far
    for k in range(5):
        prim[k, pl.ds(at_a, width), :] = a_ref[k * width : (k + 1) * width, :]
        prim[k, pl.ds(at_b, width), :] = b_ref[k * width : (k + 1) * width, :]
        prim[k, width : width + n, :] = q_ref[k, 0:n, :]
    t = ny // 8
    comps = (0, 1, 2)
    cell_pass(prim, uf, aux, (nx + 6) * t, comps)
    diff_pass(uf, aux, cx, (nx + 4) * t, (nx + 5) * t, ny)

    def put(k, i, value):
        flux[k, rows(i), :] = value

    face_pass(prim, aux, cx, (nx + 1) * t, ny, comps, put)
    for k in range(5):
        out_ref[k] = flux[k, ny : ny + n, :] - flux[k, 0:n, :]


def inner_kernel(count, length, block, comps, q_ref, after, out_ref, uf, aux, cx):
    cell_pass(q_ref, uf, aux, count, comps)
    diff_pass(uf, aux, cx, count, count, 1)
    tiles = length // 8

    def put(k, i, value):
        if block:
            i = lax.div(i, tiles) * (block // 8) + lax.rem(i, tiles)
        out_ref[k, rows(i, 3), :] = value

    face_pass(q_ref, aux, cx, count, 1, comps, put)


def edge_kernel(nx, ny, nz, block, q_ref, qt_ref, ylo, yhi, zlo, zhi, fy_ref, fz_ref, after, out_ref, prim, uf, aux, cx, flux, fy, fz):
    n = nx * ny
    sb = rup(2 * nx, 8)
    for k in range(5):
        for e in range(8):
            if e < 3:
                low = ylo[(3 * k + e) * nx : (3 * k + e + 1) * nx, :]
            else:
                low = q_ref[k, pl.ds(e - 3, nx, stride=ny), :]
            if e < 5:
                high = q_ref[k, pl.ds(ny - 5 + e, nx, stride=ny), :]
            else:
                high = yhi[(3 * k + e - 5) * nx : (3 * k + e - 4) * nx, :]
            prim[k, e * sb : e * sb + nx, :] = low
            prim[k, e * sb + nx : e * sb + 2 * nx, :] = high
    t = sb // 8
    comps = (1, 0, 2)
    cell_pass(prim, uf, aux, 8 * t, comps)
    diff_pass(uf, aux, cx, 6 * t, 7 * t, sb)

    def put(k, i, value):
        flux[k, rows(i), :] = value

    face_pass(prim, aux, cx, 3 * t, sb, comps, put)
    for k in range(5):
        fy[k, 0 : nx * block, :] = fy_ref[k, 0 : nx * block, :]
        for f in range(3):
            fy[k, pl.ds(f, nx, stride=block), :] = flux[k, f * sb : f * sb + nx, :]
            fy[k, pl.ds(ny - 2 + f, nx, stride=block), :] = flux[k, f * sb + nx : f * sb + 2 * nx, :]
    for k in range(5):
        prim[k, 0:3, :] = zlo[3 * k : 3 * k + 3, :]
        prim[k, 3:8, :] = qt_ref[k, 0:5, :]
        prim[k, 8:13, :] = qt_ref[k, nz - 5 : nz, :]
        prim[k, 13:16, :] = zhi[3 * k : 3 * k + 3, :]
    comps = (2, 0, 1)
    cell_pass(prim, uf, aux, 2, comps)
    diff_pass(uf, aux, cx, 2, 2, 1)
    face_pass(prim, aux, cx, 2, 1, comps, put)
    for k in range(5):
        fz[k, 0 : nz + 8, :] = fz_ref[k, 0 : nz + 8, :]
        fz[k, 0:3, :] = flux[k, 0:3, :]
        fz[k, nz - 2 : nz + 1, :] = flux[k, 8:11, :]
    for k in range(5):
        across = (fz[k, 1 : nz + 1, :] - fz[k, 0:nz, :]).T
        for x in range(nx):
            at = x * block
            out_ref[k, x * ny : (x + 1) * ny, :] = across[x * ny : (x + 1) * ny, :] + (
                fy[k, at + 1 : at + 1 + ny, :] - fy[k, at : at + ny, :]
            )


def final_kernel(nx, ny, q_ref, tx_ref, t_ref, top_ref, out_ref):
    step = (cfl_number * KB) / jnp.max(top_ref[...], keepdims=True)
    for x in range(nx):
        here = slice(x * ny, (x + 1) * ny)
        rho, u1, u2, u3, p = (q_ref[k, here, :] for k in range(5))
        m1, m2, m3 = rho * u1, rho * u2, rho * u3
        energy = 2.5 * p + 0.5 * (m1 * u1 + m2 * u2 + m3 * u3)
        for k, value in enumerate((rho, m1, m2, m3, energy)):
            out_ref[k, x] = value - step * (tx_ref[k, here, :] + t_ref[k, here, :])


VMEM = pl.BlockSpec(memory_space=pltpu.VMEM)
HBM = pl.BlockSpec(memory_space=pltpu.HBM)
ANY = pl.BlockSpec(memory_space=pl.ANY)


def call(kernel, outs, flops, scratch=(), in_specs=None):
    extra = {} if in_specs is None else {"in_specs": in_specs}
    return pl.pallas_call(
        kernel,
        out_shape=outs,
        scratch_shapes=scratch,
        compiler_params=pltpu.CompilerParams(vmem_limit_bytes=VMEM_LIMIT),
        cost_estimate=pl.CostEstimate(flops=flops, bytes_accessed=1000000, transcendentals=0),
        **extra,
    )


def fields(*counts, r, w):
    return [pltpu.VMEM((count, r, w), f32) for count in counts]


def pairs_a(n):
    return [(i, i ^ 1) for i in range(n)]


def pairs_b(n):
    return [(i, (i + 1) % n if i % 2 else (i - 1) % n) for i in range(n)]


def top_over(top, axis, first):
    n = lax.axis_size(axis)
    if n & (n - 1):
        return lax.pmax(top, axis)
    d = first
    while d < n:
        top = jnp.maximum(top, lax.ppermute(top, axis, [(i, i ^ d) for i in range(n)]))
        d *= 2
    return top


def edge_trade(axis, low, high, top, mids=None):
    n = lax.axis_size(axis)
    size = low.shape[0]
    if n == 1:
        return high, low, top
    if n == 2:
        got = lax.ppermute(jnp.concatenate([low, high, top]), axis, [(0, 1), (1, 0)])
        return got[size : 2 * size], got[:size], jnp.maximum(top, got[2 * size :])
    if n % 2:
        lower = lax.ppermute(high, axis, [(i, (i + 1) % n) for i in range(n)])
        upper = lax.ppermute(low, axis, [((i + 1) % n, i) for i in range(n)])
        return lower, upper, lax.pmax(top, axis)
    odd = lax.rem(lax.axis_index(axis), 2) == 1
    got_a = lax.ppermute(jnp.concatenate([jnp.where(odd, low, high), top]), axis, pairs_a(n))
    top = jnp.maximum(top, got_a[size:])
    if mids is not None:
        mids.append(top)
    send_b = jnp.where(odd, high, low)
    if n == 4:
        got_b = lax.ppermute(jnp.concatenate([send_b, top]), axis, pairs_b(n))
        top = jnp.maximum(top, got_b[size:])
    else:
        got_b = lax.ppermute(send_b, axis, pairs_b(n))
        top = top_over(top, axis, 2)
    lower = jnp.where(odd, got_a[:size], got_b[:size])
    upper = jnp.where(odd, got_b[:size], got_a[:size])
    return lower, upper, top


def local(density, velocity, pressure):
    nx, ny, nz = density.shape
    n = nx * ny
    gx = lax.axis_size("gx")
    xeven = gx % 2 == 0
    width = 15 * ny
    S = jax.ShapeDtypeStruct
    q, qt, xa, xb, ye, ze, top = call(
        functools.partial(prepare_kernel, nx, ny, nz, xeven),
        (
            S((5, n + 16, nz), f32),
            S((5, nz + 16, n), f32),
            S((width + 8, nz), f32),
            S((width, nz), f32),
            S((2, rup(15 * nx, 8), nz), f32),
            S((2, 16, n), f32),
            S((8, nz), f32),
        ),
        2000000,
        [pltpu.SemaphoreType.DMA((5,))],
        [HBM] * 3,
    )(density.reshape(n, nz), velocity.reshape(3, n, nz), pressure.reshape(n, nz))

    sweep_flops = 16000000

    def inner(source, rows_in, lanes, length, block, comps, rows_out, after):
        return call(
            functools.partial(inner_kernel, rows_in // 8, length, block, comps),
            S((5, rows_out, lanes), f32),
            sweep_flops,
            fields(10, 4, 25, r=rows_in + 16, w=lanes),
            [VMEM, ANY],
        )(source, after)

    if xeven:
        got_b = lax.ppermute(xb, "gx", pairs_b(gx))
        got_a = lax.ppermute(xa, "gx", pairs_a(gx))
        top = jnp.maximum(top, got_a[width:])
    else:
        got_a = lax.ppermute(xa, "gx", [(i, (i + 1) % gx) for i in range(gx)])
        got_b = lax.ppermute(xb, "gx", [((i + 1) % gx, i) for i in range(gx)])
    ztop = top if n == nz else jnp.full((8, n), jnp.max(top))
    fz = inner(qt, nz, n, nz, 0, (2, 0, 1), nz + 16, ztop)
    zlo, zhi, ztop = edge_trade("gz", ze[0], ze[1], ztop)
    top = ztop if n == nz else jnp.full((8, nz), jnp.max(ztop))
    block = rup(ny + 6, 8)
    fy = inner(q, n, nz, ny, block, (1, 0, 2), nx * block + 16, top)
    mids = []
    ylo, yhi, top = edge_trade("gy", ye[0], ye[1], top, mids)
    tx = call(
        functools.partial(x_kernel, nx, ny, xeven),
        S((5, n, nz), f32),
        sweep_flops,
        fields(5, 10, 4, 25, 5, r=(nx + 6) * ny, w=nz),
        [VMEM] * 3 + [ANY],
    )(q, got_a, got_b, mids[0] if mids else top)
    near = 8 * rup(2 * nx, 8) + 16
    lanes = max(n, nz)
    t = call(
        functools.partial(edge_kernel, nx, ny, nz, block),
        S((5, n, nz), f32),
        sweep_flops // 2,
        fields(5, 10, 4, 25, 5, r=near, w=lanes)
        + [pltpu.VMEM((5, nx * block + 16, nz), f32), pltpu.VMEM((5, nz + 16, n), f32)],
        [VMEM] * 8 + [ANY],
    )(q, qt, ylo, yhi, zlo, zhi, fy, fz, top)
    top = top_over(top, "gx", 2 if xeven else 1)
    return call(functools.partial(final_kernel, nx, ny), S((5, nx, ny, nz), f32), 1000000)(q, tx, t, top)


def solution(mesh):
    in_specs = (P("gx", "gy", "gz"), P(None, "gx", "gy", "gz"), P("gx", "gy", "gz"))
    out_specs = P(None, "gx", "gy", "gz")
    return jax.shard_map(local, mesh=mesh, in_specs=in_specs, out_specs=out_specs, check_vma=False)
```

time: 28.1 us -> 27.9 us (level)
  waiting for transfers between devices: 3 us -> 4.35 us
  Pallas kernels: 10.7 us -> 9.62 us
  starting transfers between devices: 11.5 us -> 11 us
    ppermute x1, starting transfers between devices: 2.59 us -> 0.01 us  [local(): got_b = lax.ppermute(xb, 'gx', pairs_b(gx))]
    ppermute x1, starting transfers between devices: 1.58 us -> 2.88 us  [edge_trade(): lax.ppermute(jnp.concatenate([low, high, top]), axis, [(0, 1), (1, 0)])]
    ppermute x1, waiting for transfers between devices: 0.01 us -> 1.26 us  [top_over(): lax.ppermute(top, axis, [(i, i ^ d) for i in range(n)])]
    ppermute x1, waiting for transfers between devices: 0.01 us -> 1.14 us  [local(): got_a = lax.ppermute(xa, 'gx', pairs_a(gx))]
    pallas_call x1, Pallas kernels: 4.09 us -> 3.06 us  [local(): call(functools.partial(x_kernel, nx, ny, xeven), S((5, n, nz), f32), swee...]
    ppermute x1, waiting for transfers between devices: 0.73 us -> 0.19 us  [local(): got_b = lax.ppermute(xb, 'gx', pairs_b(gx))]
    ppermute x1, starting transfers between devices: 1.63 us -> 2.14 us  [edge_trade(): lax.ppermute(jnp.concatenate([jnp.where(odd, low, high), top]), axis, pai...]
    ppermute x1, waiting for transfers between devices: 2.25 us -> 1.75 us  [edge_trade(): lax.ppermute(jnp.concatenate([low, high, top]), axis, [(0, 1), (1, 0)])]
  transfers between devices with their start and end apart: 6 -> 6, of which waited for: 2 -> 4; matrix products, arithmetic and copies ran while one was open for 0% -> 0% of each run, Pallas kernels for 34% -> 29%
where the time goes in v2:
time: 27.9 us; the launch traced here: 27.7 us
  starting transfers between devices  11 us (39%)
  Pallas kernels  9.62 us (34%)
  waiting for transfers between devices  4.35 us (16%)
  local copies, waits for them, and re-layouts  2.61 us (9%)
    ppermute x1, starting transfers between devices, edge_trade(): got_b = lax.ppermute(jnp.concatenate([send_b, top]), axis, pairs_b(n))  4.02 us
    pallas_call x2, Pallas kernels, inner(): call(functools.partial(inner_kernel, rows_in // 8, length, block, comps),...  3.94 us
    pallas_call x1, Pallas kernels, local(): call(functools.partial(x_kernel, nx, ny, xeven), S((5, n, nz), f32), swee...  3.06 us
    ppermute x1, starting transfers between devices, edge_trade(): lax.ppermute(jnp.concatenate([low, high, top]), axis, [(0, 1), (1, 0)])  2.88 us
    unnamed x6, local copies, waits for them, and re-layouts  2.6 us
    ppermute x1, starting transfers between devices, edge_trade(): lax.ppermute(jnp.concatenate([jnp.where(odd, low, high), top]), axis, pai...  2.14 us
    ppermute x1, waiting for transfers between devices, edge_trade(): lax.ppermute(jnp.concatenate([low, high, top]), axis, [(0, 1), (1, 0)])  1.75 us
    ppermute x1, starting transfers between devices, top_over(): lax.ppermute(top, axis, [(i, i ^ d) for i in range(n)])  1.38 us
  transfers between devices with their start and end apart: 6, of which 4 were waited for; matrix products, arithmetic and copies ran while one was open for 0% of the time, Pallas kernels for 29%

profile of v2, /device:TPU:0, one launch (start us, length us, event | category | flops | bytes accessed | tf_op | source)
XLA Modules:
  0.0 27.7 jit_solution(12108237614122437453)
XLA Ops:
  0.0 0.0 copy-start
  0.0 0.9 %copy-done = f32[3,4,32,128]{3,2,1,0:T(8,128)S(1)} copy-done((f32[3,4,32,128]{3,2,1,0:T(8,128)S(1)}, f32[3,4,32,128]{3,2,1,0:T(8,128)}, u32[]{:S(2)}) %copy-start) | copy-done | bytes 196632
  0.9 0.0 copy-start.1
  0.9 0.8 %copy-done.1 = f32[4,32,128]{2,1,0:T(8,128)S(1)} copy-done((f32[4,32,128]{2,1,0:T(8,128)S(1)}, f32[4,32,128]{2,1,0:T(8,128)}, u32[]{:S(2)}) %copy-start.1) | copy-done | bytes 65560
  1.8 0.0 copy-start.2
  1.8 0.8 %copy-done.2 = f32[4,32,128]{2,1,0:T(8,128)S(1)} copy-done((f32[4,32,128]{2,1,0:T(8,128)S(1)}, f32[4,32,128]{2,1,0:T(8,128)}, u32[]{:S(2)}) %copy-start.2) | copy-done | bytes 65560
  2.6 0.7 %shard_map.37 = (f32[5,144,128]{2,1,0:T(8,128)S(1)}, f32[5,144,128]{2,1,0:T(8,128)S(1)}, f32[488,128]{1,0:T(8,128)S(1)}, f32[480,128]{1,0:T(8,128)S(1)}, f32[2,6...) custom-call(f32[128,128]{1,0:T(8,128)S(1)} %bitcast.12, f32[3,128,128]{2,1,0:T(8,128)S(1)} %bitcast.11, ...), custom_call_target="tpu_custom_call" | custom-call | flops 2000000 | bytes 1000000 | tf_op jit(solution)/shard_map/pallas_call | solution.py:405
  3.3 0.6 %collective-permute-start = (f32[488,128]{1,0:T(8,128)S(1)}, f32[488,128]{1,0:T(8,128)S(1)}, u32[]{:S(2)}, u32[]{:S(2)}) collective-permute-start(f32[488,128]{1,0:T(8,128)S(1)} %get-tuple-element.13), channel_id=1, source_target_pairs={{0,8},{8,0},{16,24},{24,16},{1,9},{9,1},{17,25},{25,17},{2,10},{10... | collective-permute-start | bytes 749576 | tf_op jit(solution)/shard_map/ppermute | solution.py:434
  3.9 1.1 %collective-permute-done.a_ref = f32[488,128]{1,0:T(8,128)S(1)} collective-permute-done((f32[488,128]{1,0:T(8,128)S(1)}, f32[488,128]{1,0:T(8,128)S(1)}, u32[]{:S(2)}, u32[]{:S(2)}) %collective-permute-start) | collective-permute-done | bytes 249888 | tf_op jit(solution)/shard_map/ppermute | solution.py:434
  5.0 2.9 %collective-permute-start.2 = (f32[40,128]{1,0:T(8,128)S(1)}, f32[40,128]{1,0:T(8,128)S(1)}, u32[]{:S(2)}, u32[]{:S(2)}) collective-permute-start(f32[40,128]{1,0:T(8,128)S(1)} %pad_maximum_fusion.2), channel_id=1, source_target_pairs={{0,1},{1,0},{2,3},{3,2},{4,5},{5,4},{6,7},{7,6},{8,9},{9,8},{10,11... | collective-permute-start | bytes 61448 | tf_op jit(solution)/shard_map/ppermute | solution.py:375
  7.9 1.8 %collective-permute-done.2 = f32[40,128]{1,0:T(8,128)S(1)} collective-permute-done((f32[40,128]{1,0:T(8,128)S(1)}, f32[40,128]{1,0:T(8,128)S(1)}, u32[]{:S(2)}, u32[]{:S(2)}) %collective-permute-start.2) | collective-permute-done | bytes 20512 | tf_op jit(solution)/shard_map/ppermute | solution.py:375
  9.7 2.1 %collective-permute-start.3 = (f32[72,128]{1,0:T(8,128)S(1)}, f32[72,128]{1,0:T(8,128)S(1)}, u32[]{:S(2)}, u32[]{:S(2)}) collective-permute-start(f32[72,128]{1,0:T(8,128)S(1)} %pad_maximum_fusion), channel_id=1, source_target_pairs={{0,2},{2,0},{4,6},{6,4},{1,3},{3,1},{5,7},{7,5},{8,10},{10,8},{12,... | collective-permute-start | bytes 110600 | tf_op jit(solution)/shard_map/ppermute | solution.py:382
  11.8 0.0 collective-permute-start.1
  11.8 2.0 %shard_map.40.fz_ref = f32[5,144,128]{2,1,0:T(8,128)S(1)} custom-call(f32[5,144,128]{2,1,0:T(8,128)S(1)} %get-tuple-element.18.q_ref.qt_ref, f32[8,128]{1,0:T(8,128)S(1)} %slice_maximum_fusion.3.after), custom_call_target="tpu_custom_call" | custom-call | flops 16000000 | bytes 1000000 | tf_op jit(solution)/shard_map/pallas_call | solution.py:424
  13.8 0.0 collective-permute-done.3
  13.8 4.0 %collective-permute-start.4 = (f32[72,128]{1,0:T(8,128)S(1)}, f32[72,128]{1,0:T(8,128)S(1)}, u32[]{:S(2)}, u32[]{:S(2)}) collective-permute-start(f32[72,128]{1,0:T(8,128)S(1)} %pad_maximum_fusion.1), channel_id=1, source_target_pairs={{0,6},{2,4},{4,2},{6,0},{1,7},{3,5},{5,3},{7,1},{8,14},{10,12},{12... | collective-permute-start | bytes 110600 | tf_op jit(solution)/shard_map/ppermute | solution.py:388
  17.9 2.0 %shard_map.39.fy_ref = f32[5,176,128]{2,1,0:T(8,128)S(1)} custom-call(f32[5,144,128]{2,1,0:T(8,128)S(1)} %get-tuple-element.12.q_ref, f32[8,128]{1,0:T(8,128)S(1)} %slice_maximum_fusion.2.after), custom_call_target="tpu_custom_call" | custom-call | flops 16000000 | bytes 1000000 | tf_op jit(solution)/shard_map/pallas_call | solution.py:424
  19.8 0.2 collective-permute-done.1.b_ref
  20.0 3.1 %shard_map.38.tx_ref = f32[5,128,128]{2,1,0:T(8,128)S(1)} custom-call(f32[5,144,128]{2,1,0:T(8,128)S(1)} %get-tuple-element.12.q_ref, f32[488,128]{1,0:T(8,128)S(1)} %collective-permute-done.a_ref, f32[480,128]{1,0:T(8,128)S(1)} %collective-permute-done.1.b_ref, f32[8,128]{1,0:T(8,128)S(1)} %slice_maximum_fusion.1.after), custom_call_target="tpu_custom_call" | custom-call | flops 16000000 | bytes 1000000 | tf_op jit(solution)/shard_map/pallas_call | solution.py:447
  23.1 0.0 collective-permute-done.4
  23.1 1.4 %collective-permute-start.5 = (f32[8,128]{1,0:T(8,128)S(1)}, f32[8,128]{1,0:T(8,128)S(1)}, u32[]{:S(2)}, u32[]{:S(2)}) collective-permute-start(f32[8,128]{1,0:T(8,128)S(1)} %slice_maximum_fusion.after), channel_id=1, source_target_pairs={{0,16},{8,24},{16,0},{24,8},{1,17},{9,25},{17,1},{25,9},{2,18},{10... | collective-permute-start | bytes 12296 | tf_op jit(solution)/shard_map/ppermute | solution.py:364
  24.5 1.0 %shard_map.41.t_ref = f32[5,128,128]{2,1,0:T(8,128)S(1)} custom-call(f32[5,144,128]{2,1,0:T(8,128)S(1)} %get-tuple-element.12.q_ref, f32[5,144,128]{2,1,0:T(8,128)S(1)} %get-tuple-element.18.q_ref.qt_ref, f32[64,128]{1,0:T(8,128)S(1)} %get-tuple-element.20.ylo, f32[64,128]{1,0:T(8,128)S(1)} %get-tuple-element.19.yhi, f32[16,128]{1,0:T(8,128)S(1)} %get-tuple-element.24.zlo, ...), custom_call_target="tpu_custom_call" | custom-call | flops 8000000 | bytes 1000000 | tf_op jit(solution)/shard_map/pallas_call | solution.py:456
  25.5 1.3 %collective-permute-done.5 = f32[8,128]{1,0:T(8,128)S(1)} collective-permute-done((f32[8,128]{1,0:T(8,128)S(1)}, f32[8,128]{1,0:T(8,128)S(1)}, u32[]{:S(2)}, u32[]{:S(2)}) %collective-permute-start.5) | collective-permute-done | bytes 4128 | tf_op jit(solution)/shard_map/ppermute | solution.py:364
  26.8 0.9 %shard_map.42 = f32[5,4,32,128]{3,2,1,0:T(8,128)} custom-call(f32[5,144,128]{2,1,0:T(8,128)S(1)} %get-tuple-element.12.q_ref, f32[5,128,128]{2,1,0:T(8,128)S(1)} %shard_map.38.tx_ref, f32[5,128,128]{2,1,0:T(8,128)S(1)} %shard_map.41.t_ref, f32[8,128]{1,0:T(8,128)S(1)} %max.19.top_ref), custom_call_target="tpu_custom_call" | custom-call | flops 1000000 | bytes 1000000 | tf_op jit(solution)/shard_map/pallas_call | solution.py:465
  (12 shorter events, 0.1 us)
Async XLA Ops:
  0.0 0.9 %copy-start = (f32[3,4,32,128]{3,2,1,0:T(8,128)S(1)}, f32[3,4,32,128]{3,2,1,0:T(8,128)}, u32[]{:S(2)}) copy-start(f32[3,4,32,128]{3,2,1,0:T(8,128)} %param.4) | copy-start | bytes 589828
  0.9 0.8 %copy-start.1 = (f32[4,32,128]{2,1,0:T(8,128)S(1)}, f32[4,32,128]{2,1,0:T(8,128)}, u32[]{:S(2)}) copy-start(f32[4,32,128]{2,1,0:T(8,128)} %param.3) | copy-start | bytes 196612
  1.8 0.8 %copy-start.2 = (f32[4,32,128]{2,1,0:T(8,128)S(1)}, f32[4,32,128]{2,1,0:T(8,128)}, u32[]{:S(2)}) copy-start(f32[4,32,128]{2,1,0:T(8,128)} %param.5) | copy-start | bytes 196612
  3.3 1.7 %collective-permute-start = (f32[488,128]{1,0:T(8,128)S(1)}, f32[488,128]{1,0:T(8,128)S(1)}, u32[]{:S(2)}, u32[]{:S(2)}) collective-permute-start(f32[488,128]{1,0:T(8,128)S(1)} %get-tuple-element.13), channel_id=1, source_target_pairs={{0,8},{8,0},{16,24},{24,16},{1,9},{9,1},{17,25},{25,17},{2,10},{10... | collective-permute-start | bytes 749576 | tf_op jit(solution)/shard_map/ppermute | solution.py:434
  5.0 4.6 %collective-permute-start.2 = (f32[40,128]{1,0:T(8,128)S(1)}, f32[40,128]{1,0:T(8,128)S(1)}, u32[]{:S(2)}, u32[]{:S(2)}) collective-permute-start(f32[40,128]{1,0:T(8,128)S(1)} %pad_maximum_fusion.2), channel_id=1, source_target_pairs={{0,1},{1,0},{2,3},{3,2},{4,5},{5,4},{6,7},{7,6},{8,9},{9,8},{10,11... | collective-permute-start | bytes 61448 | tf_op jit(solution)/shard_map/ppermute | solution.py:375
  9.7 4.1 %collective-permute-start.3 = (f32[72,128]{1,0:T(8,128)S(1)}, f32[72,128]{1,0:T(8,128)S(1)}, u32[]{:S(2)}, u32[]{:S(2)}) collective-permute-start(f32[72,128]{1,0:T(8,128)S(1)} %pad_maximum_fusion), channel_id=1, source_target_pairs={{0,2},{2,0},{4,6},{6,4},{1,3},{3,1},{5,7},{7,5},{8,10},{10,8},{12,... | collective-permute-start | bytes 110600 | tf_op jit(solution)/shard_map/ppermute | solution.py:382
  11.8 8.2 %collective-permute-start.1 = (f32[480,128]{1,0:T(8,128)S(1)}, f32[480,128]{1,0:T(8,128)S(1)}, u32[]{:S(2)}, u32[]{:S(2)}) collective-permute-start(f32[480,128]{1,0:T(8,128)S(1)} %get-tuple-element.14), channel_id=1, source_target_pairs={{0,24},{8,16},{16,8},{24,0},{1,25},{9,17},{17,9},{25,1},{2,26},{10... | collective-permute-start | bytes 737288 | tf_op jit(solution)/shard_map/ppermute | solution.py:433
  13.8 9.2 %collective-permute-start.4 = (f32[72,128]{1,0:T(8,128)S(1)}, f32[72,128]{1,0:T(8,128)S(1)}, u32[]{:S(2)}, u32[]{:S(2)}) collective-permute-start(f32[72,128]{1,0:T(8,128)S(1)} %pad_maximum_fusion.1), channel_id=1, source_target_pairs={{0,6},{2,4},{4,2},{6,0},{1,7},{3,5},{5,3},{7,1},{8,14},{10,12},{12... | collective-permute-start | bytes 110600 | tf_op jit(solution)/shard_map/ppermute | solution.py:388
  23.1 3.7 %collective-permute-start.5 = (f32[8,128]{1,0:T(8,128)S(1)}, f32[8,128]{1,0:T(8,128)S(1)}, u32[]{:S(2)}, u32[]{:S(2)}) collective-permute-start(f32[8,128]{1,0:T(8,128)S(1)} %slice_maximum_fusion.after), channel_id=1, source_target_pairs={{0,16},{8,24},{16,0},{24,8},{1,17},{9,25},{17,1},{25,9},{2,18},{10... | collective-permute-start | bytes 12296 | tf_op jit(solution)/shard_map/ppermute | solution.py:364

commit v3 on v2

--- a/solution.py
+++ b/solution.py
@@ -7,6 +7,7 @@
 from jax.experimental import pallas as pl
 from jax.experimental.pallas import tpu as pltpu
 from jax.sharding import PartitionSpec as P
+
 
 gamma_gas = 1.4
 weno_eps = 1e-06
@@ -265,7 +266,6 @@
 
 
 def edge_kernel(nx, ny, nz, block, q_ref, qt_ref, ylo, yhi, zlo, zhi, fy_ref, fz_ref, after, out_ref, prim, uf, aux, cx, flux, fy, fz):
-    n = nx * ny
     sb = rup(2 * nx, 8)
     for k in range(5):
         for e in range(8):
@@ -402,6 +402,10 @@
     xeven = gx % 2 == 0
     width = 15 * ny
     S = jax.ShapeDtypeStruct
+    density, velocity, pressure = (
+        pltpu.with_memory_space_constraint(a, pltpu.HBM)
+        for a in (density.reshape(n, nz), velocity.reshape(3, n, nz), pressure.reshape(n, nz))
+    )
     q, qt, xa, xb, ye, ze, top = call(
         functools.partial(prepare_kernel, nx, ny, nz, xeven),
         (
@@ -416,7 +420,7 @@
         2000000,
         [pltpu.SemaphoreType.DMA((5,))],
         [HBM] * 3,
-    )(density.reshape(n, nz), velocity.reshape(3, n, nz), pressure.reshape(n, nz))
+    )(density, velocity, pressure)
 
     sweep_flops = 16000000
 
@@ -468,4 +472,5 @@
 def solution(mesh):
     in_specs = (P("gx", "gy", "gz"), P(None, "gx", "gy", "gz"), P("gx", "gy", "gz"))
     out_specs = P(None, "gx", "gy", "gz")
+
     return jax.shard_map(local, mesh=mesh, in_specs=in_specs, out_specs=out_specs, check_vma=False)

time: 27.9 us -> 25.8 us (0.925)
  local copies, waits for them, and re-layouts: 2.61 us -> 0.01 us
  Pallas kernels: 9.62 us -> 10.2 us
    unnamed x6 -> x0, local copies, waits for them, and re-layouts: 2.6 us -> none
    pallas_call x1, Pallas kernels: 0.7 us -> 1.27 us  [local(): call(functools.partial(prepare_kernel, nx, ny, nz, xeven), (S((5, n + 16,...]
  transfers between devices with their start and end apart: 6 -> 6, of which waited for: 4 -> 4; matrix products, arithmetic and copies ran while one was open for 0% -> 0% of each run, Pallas kernels for 29% -> 31%
where the time goes in v3:
time: 25.8 us; the launch traced here: 25.6 us
  starting transfers between devices  11 us (43%)
  Pallas kernels  10.2 us (40%)
  waiting for transfers between devices  4.35 us (17%)
    ppermute x1, starting transfers between devices, edge_trade(): got_b = lax.ppermute(jnp.concatenate([send_b, top]), axis, pairs_b(n))  4.02 us
    pallas_call x2, Pallas kernels, inner(): call(functools.partial(inner_kernel, rows_in // 8, length, block, comps),...  3.94 us
    pallas_call x1, Pallas kernels, local(): call(functools.partial(x_kernel, nx, ny, xeven), S((5, n, nz), f32), swee...  3.06 us
    ppermute x1, starting transfers between devices, edge_trade(): lax.ppermute(jnp.concatenate([low, high, top]), axis, [(0, 1), (1, 0)])  2.88 us
    ppermute x1, starting transfers between devices, edge_trade(): lax.ppermute(jnp.concatenate([jnp.where(odd, low, high), top]), axis, pai...  2.14 us
    ppermute x1, waiting for transfers between devices, edge_trade(): lax.ppermute(jnp.concatenate([low, high, top]), axis, [(0, 1), (1, 0)])  1.75 us
    ppermute x1, starting transfers between devices, top_over(): lax.ppermute(top, axis, [(i, i ^ d) for i in range(n)])  1.38 us
    pallas_call x1, Pallas kernels, local(): call(functools.partial(prepare_kernel, nx, ny, nz, xeven), (S((5, n + 16,...  1.27 us
  transfers between devices with their start and end apart: 6, of which 4 were waited for; matrix products, arithmetic and copies ran while one was open for 0% of the time, Pallas kernels for 31%

profile of v3, /device:TPU:0, one launch (start us, length us, event | category | flops | bytes accessed | tf_op | source)
XLA Modules:
  0.0 25.6 jit_solution(14142535503537908424)
XLA Ops:
  0.0 1.3 %shard_map.37 = (f32[5,144,128]{2,1,0:T(8,128)S(1)}, f32[5,144,128]{2,1,0:T(8,128)S(1)}, f32[488,128]{1,0:T(8,128)S(1)}, f32[480,128]{1,0:T(8,128)S(1)}, f32[2,6...) custom-call(f32[128,128]{1,0:T(8,128)} %bitcast.12, f32[3,128,128]{2,1,0:T(8,128)} %bitcast.11, ...), custom_call_target="tpu_custom_call" | custom-call | flops 2000000 | bytes 1000000 | tf_op jit(solution)/shard_map/pallas_call | solution.py:409
  1.3 0.6 %collective-permute-start = (f32[488,128]{1,0:T(8,128)S(1)}, f32[488,128]{1,0:T(8,128)S(1)}, u32[]{:S(2)}, u32[]{:S(2)}) collective-permute-start(f32[488,128]{1,0:T(8,128)S(1)} %get-tuple-element.13), channel_id=1, source_target_pairs={{0,8},{8,0},{16,24},{24,16},{1,9},{9,1},{17,25},{25,17},{2,10},{10... | collective-permute-start | bytes 749576 | tf_op jit(solution)/shard_map/ppermute | solution.py:438
  1.8 1.1 %collective-permute-done.a_ref = f32[488,128]{1,0:T(8,128)S(1)} collective-permute-done((f32[488,128]{1,0:T(8,128)S(1)}, f32[488,128]{1,0:T(8,128)S(1)}, u32[]{:S(2)}, u32[]{:S(2)}) %collective-permute-start) | collective-permute-done | bytes 249888 | tf_op jit(solution)/shard_map/ppermute | solution.py:438
  3.0 2.9 %collective-permute-start.2 = (f32[40,128]{1,0:T(8,128)S(1)}, f32[40,128]{1,0:T(8,128)S(1)}, u32[]{:S(2)}, u32[]{:S(2)}) collective-permute-start(f32[40,128]{1,0:T(8,128)S(1)} %pad_maximum_fusion.2), channel_id=1, source_target_pairs={{0,1},{1,0},{2,3},{3,2},{4,5},{5,4},{6,7},{7,6},{8,9},{9,8},{10,11... | collective-permute-start | bytes 61448 | tf_op jit(solution)/shard_map/ppermute | solution.py:375
  5.9 1.8 %collective-permute-done.2 = f32[40,128]{1,0:T(8,128)S(1)} collective-permute-done((f32[40,128]{1,0:T(8,128)S(1)}, f32[40,128]{1,0:T(8,128)S(1)}, u32[]{:S(2)}, u32[]{:S(2)}) %collective-permute-start.2) | collective-permute-done | bytes 20512 | tf_op jit(solution)/shard_map/ppermute | solution.py:375
  7.6 2.1 %collective-permute-start.3 = (f32[72,128]{1,0:T(8,128)S(1)}, f32[72,128]{1,0:T(8,128)S(1)}, u32[]{:S(2)}, u32[]{:S(2)}) collective-permute-start(f32[72,128]{1,0:T(8,128)S(1)} %pad_maximum_fusion), channel_id=1, source_target_pairs={{0,2},{2,0},{4,6},{6,4},{1,3},{3,1},{5,7},{7,5},{8,10},{10,8},{12,... | collective-permute-start | bytes 110600 | tf_op jit(solution)/shard_map/ppermute | solution.py:382
  9.8 0.0 collective-permute-start.1
  9.8 2.0 %shard_map.40.fz_ref = f32[5,144,128]{2,1,0:T(8,128)S(1)} custom-call(f32[5,144,128]{2,1,0:T(8,128)S(1)} %get-tuple-element.18.q_ref.qt_ref, f32[8,128]{1,0:T(8,128)S(1)} %slice_maximum_fusion.3.after), custom_call_target="tpu_custom_call" | custom-call | flops 16000000 | bytes 1000000 | tf_op jit(solution)/shard_map/pallas_call | solution.py:428
  11.8 0.0 collective-permute-done.3
  11.8 4.0 %collective-permute-start.4 = (f32[72,128]{1,0:T(8,128)S(1)}, f32[72,128]{1,0:T(8,128)S(1)}, u32[]{:S(2)}, u32[]{:S(2)}) collective-permute-start(f32[72,128]{1,0:T(8,128)S(1)} %pad_maximum_fusion.1), channel_id=1, source_target_pairs={{0,6},{2,4},{4,2},{6,0},{1,7},{3,5},{5,3},{7,1},{8,14},{10,12},{12... | collective-permute-start | bytes 110600 | tf_op jit(solution)/shard_map/ppermute | solution.py:388
  15.8 2.0 %shard_map.39.fy_ref = f32[5,176,128]{2,1,0:T(8,128)S(1)} custom-call(f32[5,144,128]{2,1,0:T(8,128)S(1)} %get-tuple-element.12.q_ref, f32[8,128]{1,0:T(8,128)S(1)} %slice_maximum_fusion.2.after), custom_call_target="tpu_custom_call" | custom-call | flops 16000000 | bytes 1000000 | tf_op jit(solution)/shard_map/pallas_call | solution.py:428
  17.8 0.2 collective-permute-done.1.b_ref
  18.0 3.1 %shard_map.38.tx_ref = f32[5,128,128]{2,1,0:T(8,128)S(1)} custom-call(f32[5,144,128]{2,1,0:T(8,128)S(1)} %get-tuple-element.12.q_ref, f32[488,128]{1,0:T(8,128)S(1)} %collective-permute-done.a_ref, f32[480,128]{1,0:T(8,128)S(1)} %collective-permute-done.1.b_ref, f32[8,128]{1,0:T(8,128)S(1)} %slice_maximum_fusion.1.after), custom_call_target="tpu_custom_call" | custom-call | flops 16000000 | bytes 1000000 | tf_op jit(solution)/shard_map/pallas_call | solution.py:451
  21.1 0.0 collective-permute-done.4
  21.1 1.4 %collective-permute-start.5 = (f32[8,128]{1,0:T(8,128)S(1)}, f32[8,128]{1,0:T(8,128)S(1)}, u32[]{:S(2)}, u32[]{:S(2)}) collective-permute-start(f32[8,128]{1,0:T(8,128)S(1)} %slice_maximum_fusion.after), channel_id=1, source_target_pairs={{0,16},{8,24},{16,0},{24,8},{1,17},{9,25},{17,1},{25,9},{2,18},{10... | collective-permute-start | bytes 12296 | tf_op jit(solution)/shard_map/ppermute | solution.py:364
  22.5 1.0 %shard_map.41.t_ref = f32[5,128,128]{2,1,0:T(8,128)S(1)} custom-call(f32[5,144,128]{2,1,0:T(8,128)S(1)} %get-tuple-element.12.q_ref, f32[5,144,128]{2,1,0:T(8,128)S(1)} %get-tuple-element.18.q_ref.qt_ref, f32[64,128]{1,0:T(8,128)S(1)} %get-tuple-element.20.ylo, f32[64,128]{1,0:T(8,128)S(1)} %get-tuple-element.19.yhi, f32[16,128]{1,0:T(8,128)S(1)} %get-tuple-element.24.zlo, ...), custom_call_target="tpu_custom_call" | custom-call | flops 8000000 | bytes 1000000 | tf_op jit(solution)/shard_map/pallas_call | solution.py:460
  23.5 1.3 %collective-permute-done.5 = f32[8,128]{1,0:T(8,128)S(1)} collective-permute-done((f32[8,128]{1,0:T(8,128)S(1)}, f32[8,128]{1,0:T(8,128)S(1)}, u32[]{:S(2)}, u32[]{:S(2)}) %collective-permute-start.5) | collective-permute-done | bytes 4128 | tf_op jit(solution)/shard_map/ppermute | solution.py:364
  24.8 0.9 %shard_map.42 = f32[5,4,32,128]{3,2,1,0:T(8,128)} custom-call(f32[5,144,128]{2,1,0:T(8,128)S(1)} %get-tuple-element.12.q_ref, f32[5,128,128]{2,1,0:T(8,128)S(1)} %shard_map.38.tx_ref, f32[5,128,128]{2,1,0:T(8,128)S(1)} %shard_map.41.t_ref, f32[8,128]{1,0:T(8,128)S(1)} %max.19.top_ref), custom_call_target="tpu_custom_call" | custom-call | flops 1000000 | bytes 1000000 | tf_op jit(solution)/shard_map/pallas_call | solution.py:469
  (12 shorter events, 0.1 us)
Async XLA Ops:
  1.3 1.7 %collective-permute-start = (f32[488,128]{1,0:T(8,128)S(1)}, f32[488,128]{1,0:T(8,128)S(1)}, u32[]{:S(2)}, u32[]{:S(2)}) collective-permute-start(f32[488,128]{1,0:T(8,128)S(1)} %get-tuple-element.13), channel_id=1, source_target_pairs={{0,8},{8,0},{16,24},{24,16},{1,9},{9,1},{17,25},{25,17},{2,10},{10... | collective-permute-start | bytes 749576 | tf_op jit(solution)/shard_map/ppermute | solution.py:438
  3.0 4.6 %collective-permute-start.2 = (f32[40,128]{1,0:T(8,128)S(1)}, f32[40,128]{1,0:T(8,128)S(1)}, u32[]{:S(2)}, u32[]{:S(2)}) collective-permute-start(f32[40,128]{1,0:T(8,128)S(1)} %pad_maximum_fusion.2), channel_id=1, source_target_pairs={{0,1},{1,0},{2,3},{3,2},{4,5},{5,4},{6,7},{7,6},{8,9},{9,8},{10,11... | collective-permute-start | bytes 61448 | tf_op jit(solution)/shard_map/ppermute | solution.py:375
  7.6 4.1 %collective-permute-start.3 = (f32[72,128]{1,0:T(8,128)S(1)}, f32[72,128]{1,0:T(8,128)S(1)}, u32[]{:S(2)}, u32[]{:S(2)}) collective-permute-start(f32[72,128]{1,0:T(8,128)S(1)} %pad_maximum_fusion), channel_id=1, source_target_pairs={{0,2},{2,0},{4,6},{6,4},{1,3},{3,1},{5,7},{7,5},{8,10},{10,8},{12,... | collective-permute-start | bytes 110600 | tf_op jit(solution)/shard_map/ppermute | solution.py:382
  9.8 8.2 %collective-permute-start.1 = (f32[480,128]{1,0:T(8,128)S(1)}, f32[480,128]{1,0:T(8,128)S(1)}, u32[]{:S(2)}, u32[]{:S(2)}) collective-permute-start(f32[480,128]{1,0:T(8,128)S(1)} %get-tuple-element.14), channel_id=1, source_target_pairs={{0,24},{8,16},{16,8},{24,0},{1,25},{9,17},{17,9},{25,1},{2,26},{10... | collective-permute-start | bytes 737288 | tf_op jit(solution)/shard_map/ppermute | solution.py:437
  11.8 9.2 %collective-permute-start.4 = (f32[72,128]{1,0:T(8,128)S(1)}, f32[72,128]{1,0:T(8,128)S(1)}, u32[]{:S(2)}, u32[]{:S(2)}) collective-permute-start(f32[72,128]{1,0:T(8,128)S(1)} %pad_maximum_fusion.1), channel_id=1, source_target_pairs={{0,6},{2,4},{4,2},{6,0},{1,7},{3,5},{5,3},{7,1},{8,14},{10,12},{12... | collective-permute-start | bytes 110600 | tf_op jit(solution)/shard_map/ppermute | solution.py:388
  21.1 3.7 %collective-permute-start.5 = (f32[8,128]{1,0:T(8,128)S(1)}, f32[8,128]{1,0:T(8,128)S(1)}, u32[]{:S(2)}, u32[]{:S(2)}) collective-permute-start(f32[8,128]{1,0:T(8,128)S(1)} %slice_maximum_fusion.after), channel_id=1, source_target_pairs={{0,16},{8,24},{16,0},{24,8},{1,17},{9,25},{17,1},{25,9},{2,18},{10... | collective-permute-start | bytes 12296 | tf_op jit(solution)/shard_map/ppermute | solution.py:364

commit v4 on v3

--- a/solution.py
+++ b/solution.py
@@ -196,6 +196,7 @@
             jnp.abs(q_ref[3, here, :]) + 3.0 * sound
         )
         top = speed if top is None else jnp.maximum(top, speed)
+    top = jnp.broadcast_to(jnp.max(top, keepdims=True), (8, nz))
     top_ref[...] = top
     width = 3 * ny
     high = (nx - 3) * ny
@@ -316,7 +317,7 @@
 
 
 def final_kernel(nx, ny, q_ref, tx_ref, t_ref, top_ref, out_ref):
-    step = (cfl_number * KB) / jnp.max(top_ref[...], keepdims=True)
+    step = (cfl_number * KB) / top_ref[0:1, :]
     for x in range(nx):
         here = slice(x * ny, (x + 1) * ny)
         rho, u1, u2, u3, p = (q_ref[k, here, :] for k in range(5))
@@ -355,43 +356,69 @@
     return [(i, (i + 1) % n if i % 2 else (i - 1) % n) for i in range(n)]
 
 
-def top_over(top, axis, first):
+def top_over(top, axis, first, leads):
     n = lax.axis_size(axis)
     if n & (n - 1):
         return lax.pmax(top, axis)
     d = first
     while d < n:
-        top = jnp.maximum(top, lax.ppermute(top, axis, [(i, i ^ d) for i in range(n)]))
+        got = lead_permute(top, axis, [(i, i ^ d) for i in range(n)], leads)
+        top = jnp.maximum(top, got)
         d *= 2
     return top
 
 
-def edge_trade(axis, low, high, top, mids=None):
+def lead_permute(value, axis, pairs, leads):
+    gx = lax.axis_size("gx")
+    if axis == "gx":
+        return lax.ppermute(value, "gx", [(i, j) for i, j in pairs if leads(i)])
+    n = lax.axis_size(axis)
+    return lax.ppermute(
+        value, ("gx", axis), [(g * n + i, g * n + j) for g in range(gx) if leads(g) for i, j in pairs]
+    )
+
+
+def with_top(edges, used, top):
+    row = lax.broadcasted_iota(jnp.int32, edges.shape, 0)
+    return jnp.where(row >= used, top[0:1], edges)
+
+
+def got_top(top, got, row):
+    return jnp.maximum(top, got[row : row + 1])
+
+
+def edge_trade(axis, low, high, used, top, lead, leads, mids=None):
     n = lax.axis_size(axis)
     size = low.shape[0]
+
+    def both(bare, pairs, top):
+        led = lead_permute(with_top(bare, bare.shape[0] - size + used, top), axis, pairs, leads)
+        if lead is None:
+            return led, led
+        rest = lead_permute(bare, axis, pairs, lambda i: not leads(i))
+        return led, jnp.where(lead, led, rest)
+
     if n == 1:
         return high, low, top
     if n == 2:
-        got = lax.ppermute(jnp.concatenate([low, high, top]), axis, [(0, 1), (1, 0)])
-        return got[size : 2 * size], got[:size], jnp.maximum(top, got[2 * size :])
+        led, got = both(jnp.concatenate([low, high]), [(0, 1), (1, 0)], top)
+        return got[size:], got[:size], got_top(top, led, size + used)
     if n % 2:
         lower = lax.ppermute(high, axis, [(i, (i + 1) % n) for i in range(n)])
         upper = lax.ppermute(low, axis, [((i + 1) % n, i) for i in range(n)])
         return lower, upper, lax.pmax(top, axis)
     odd = lax.rem(lax.axis_index(axis), 2) == 1
-    got_a = lax.ppermute(jnp.concatenate([jnp.where(odd, low, high), top]), axis, pairs_a(n))
-    top = jnp.maximum(top, got_a[size:])
+    led, got_a = both(jnp.where(odd, low, high), pairs_a(n), top)
+    top = got_top(top, led, used)
     if mids is not None:
         mids.append(top)
-    send_b = jnp.where(odd, high, low)
+    led, got_b = both(jnp.where(odd, high, low), pairs_b(n), top)
     if n == 4:
-        got_b = lax.ppermute(jnp.concatenate([send_b, top]), axis, pairs_b(n))
-        top = jnp.maximum(top, got_b[size:])
+        top = got_top(top, led, used)
     else:
-        got_b = lax.ppermute(send_b, axis, pairs_b(n))
-        top = top_over(top, axis, 2)
-    lower = jnp.where(odd, got_a[:size], got_b[:size])
-    upper = jnp.where(odd, got_b[:size], got_a[:size])
+        top = top_over(top, axis, 2, leads)
+    lower = jnp.where(odd, got_a, got_b)
+    upper = jnp.where(odd, got_b, got_a)
     return lower, upper, top
 
 
@@ -413,7 +440,7 @@
             S((5, nz + 16, n), f32),
             S((width + 8, nz), f32),
             S((width, nz), f32),
-            S((2, rup(15 * nx, 8), nz), f32),
+            S((2, rup(15 * nx + 1, 8), nz), f32),
             S((2, 16, n), f32),
             S((8, nz), f32),
         ),
@@ -442,12 +469,15 @@
         got_b = lax.ppermute(xb, "gx", [((i + 1) % gx, i) for i in range(gx)])
     ztop = top if n == nz else jnp.full((8, n), jnp.max(top))
     fz = inner(qt, nz, n, nz, 0, (2, 0, 1), nz + 16, ztop)
-    zlo, zhi, ztop = edge_trade("gz", ze[0], ze[1], ztop)
+    lead, leads = None, lambda i: True
+    if xeven:
+        lead, leads = lax.rem(lax.axis_index("gx"), 2) == 1, lambda i: i % 2 == 1
+    zlo, zhi, ztop = edge_trade("gz", ze[0], ze[1], 15, ztop, lead, leads)
     top = ztop if n == nz else jnp.full((8, nz), jnp.max(ztop))
     block = rup(ny + 6, 8)
     fy = inner(q, n, nz, ny, block, (1, 0, 2), nx * block + 16, top)
     mids = []
-    ylo, yhi, top = edge_trade("gy", ye[0], ye[1], top, mids)
+    ylo, yhi, top = edge_trade("gy", ye[0], ye[1], 15 * nx, top, lead, leads, mids)
     tx = call(
         functools.partial(x_kernel, nx, ny, xeven),
         S((5, n, nz), f32),
@@ -465,7 +495,9 @@
         + [pltpu.VMEM((5, nx * block + 16, nz), f32), pltpu.VMEM((5, nz + 16, n), f32)],
         [VMEM] * 8 + [ANY],
     )(q, qt, ylo, yhi, zlo, zhi, fy, fz, top)
-    top = top_over(top, "gx", 2 if xeven else 1)
+    top = top_over(top, "gx", 2 if xeven else 1, leads)
+    if xeven:
+        top = jnp.maximum(top, lax.ppermute(top, "gx", [(i + 1, i) for i in range(0, gx, 2)]))
     return call(functools.partial(final_kernel, nx, ny), S((5, nx, ny, nz), f32), 1000000)(q, tx, t, top)
 
 

time: 25.8 us -> 37.6 us (1.46)
  starting transfers between devices: 11 us -> 24.7 us
  waiting for transfers between devices: 4.35 us -> 1.84 us
    ppermute x1, starting transfers between devices: 0.01 us -> 8.96 us  [local(): got_b = lax.ppermute(xb, 'gx', pairs_b(gx))]
    ppermute x4 -> x8, starting transfers between devices: 10.4 us -> 15.2 us  [the longest x6 13.2 us: lead_permute(): lax.ppermute(value, ('gx', axis), [(g * n + i, g * n + j) for g in range(...]
    ppermute x4 -> x8, waiting for transfers between devices: 3.02 us -> 0.71 us  [the longest x1 0.69 us: local(): lax.ppermute(top, 'gx', [(i + 1, i) for i in range(0, gx, 2)])]
  transfers between devices with their start and end apart: 6 -> 10, of which waited for: 4 -> 2; matrix products, arithmetic and copies ran while one was open for 0% -> 0% of each run, Pallas kernels for 31% -> 22%
where the time goes in v4:
time: 37.6 us; the launch traced here: 37.3 us
  starting transfers between devices  24.7 us (66%)
  Pallas kernels  10.2 us (27%)
  waiting for transfers between devices  1.84 us (5%)
    ppermute x6, starting transfers between devices, lead_permute(): lax.ppermute(value, ('gx', axis), [(g * n + i, g * n + j) for g in range(...  13.2 us
    ppermute x1, starting transfers between devices, local(): got_b = lax.ppermute(xb, 'gx', pairs_b(gx))  8.96 us
    pallas_call x2, Pallas kernels, inner(): call(functools.partial(inner_kernel, rows_in // 8, length, block, comps),...  3.96 us
    pallas_call x1, Pallas kernels, local(): call(functools.partial(x_kernel, nx, ny, xeven), S((5, n, nz), f32), swee...  3.06 us
    pallas_call x1, Pallas kernels, local(): call(functools.partial(prepare_kernel, nx, ny, nz, xeven), (S((5, n + 16,...  1.3 us
    ppermute x1, starting transfers between devices, local(): lax.ppermute(top, 'gx', [(i + 1, i) for i in range(0, gx, 2)])  1.29 us
    ppermute x1, waiting for transfers between devices, local(): got_a = lax.ppermute(xa, 'gx', pairs_a(gx))  1.14 us
    pallas_call x1, Pallas kernels, local(): call(functools.partial(edge_kernel, nx, ny, nz, block), S((5, n, nz), f32...  1.02 us
  transfers between devices with their start and end apart: 10, of which 2 were waited for; matrix products, arithmetic and copies ran while one was open for 0% of the time, Pallas kernels for 22%

profile of v4, /device:TPU:0, one launch (start us, length us, event | category | flops | bytes accessed | tf_op | source)
XLA Modules:
  0.0 37.3 jit_solution(9287449376683150572)
XLA Ops:
  0.0 1.3 %shard_map.37 = (f32[5,144,128]{2,1,0:T(8,128)S(1)}, f32[5,144,128]{2,1,0:T(8,128)S(1)}, f32[488,128]{1,0:T(8,128)S(1)}, f32[480,128]{1,0:T(8,128)S(1)}, f32[2,6...) custom-call(f32[128,128]{1,0:T(8,128)} %bitcast.26, f32[3,128,128]{2,1,0:T(8,128)} %bitcast.25, ...), custom_call_target="tpu_custom_call" | custom-call | flops 2000000 | bytes 1000000 | tf_op jit(solution)/shard_map/pallas_call | solution.py:436
  1.3 0.6 %collective-permute-start = (f32[488,128]{1,0:T(8,128)S(1)}, f32[488,128]{1,0:T(8,128)S(1)}, u32[]{:S(2)}, u32[]{:S(2)}) collective-permute-start(f32[488,128]{1,0:T(8,128)S(1)} %get-tuple-element.13), channel_id=1, source_target_pairs={{0,8},{8,0},{16,24},{24,16},{1,9},{9,1},{17,25},{25,17},{2,10},{10... | collective-permute-start | bytes 749576 | tf_op jit(solution)/shard_map/ppermute | solution.py:465
  1.9 1.1 %collective-permute-done.a_ref = f32[488,128]{1,0:T(8,128)S(1)} collective-permute-done((f32[488,128]{1,0:T(8,128)S(1)}, f32[488,128]{1,0:T(8,128)S(1)}, u32[]{:S(2)}, u32[]{:S(2)}) %collective-permute-start) | collective-permute-done | bytes 249888 | tf_op jit(solution)/shard_map/ppermute | solution.py:465
  3.0 0.1 pad_maximum_fusion
  3.1 0.7 %collective-permute-start.2 = (f32[32,128]{1,0:T(8,128)S(1)}, f32[32,128]{1,0:T(8,128)S(1)}, u32[]{:S(2)}, u32[]{:S(2)}) collective-permute-start(f32[32,128]{1,0:T(8,128)S(1)} %get-tuple-element.28), channel_id=1, source_target_pairs={{8,9},{9,8},{24,25},{25,24},{10,11},{11,10},{26,27},{27,26},{12,13... | collective-permute-start | bytes 49160 | tf_op jit(solution)/shard_map/ppermute | solution.py:376
  3.8 0.0 collective-permute-done.2
  3.8 0.1 broadcast_select_fusion.1
  3.9 0.7 %collective-permute-start.3 = (f32[64,128]{1,0:T(8,128)S(1)}, f32[64,128]{1,0:T(8,128)S(1)}, u32[]{:S(2)}, u32[]{:S(2)}) collective-permute-start(f32[64,128]{1,0:T(8,128)S(1)} %get-tuple-element.21), channel_id=1, source_target_pairs={{8,10},{10,8},{12,14},{14,12},{24,26},{26,24},{28,30},{30,28},{9,1... | collective-permute-start | bytes 98312 | tf_op jit(solution)/shard_map/ppermute | solution.py:376
  4.6 9.0 %collective-permute-start.1 = (f32[480,128]{1,0:T(8,128)S(1)}, f32[480,128]{1,0:T(8,128)S(1)}, u32[]{:S(2)}, u32[]{:S(2)}) collective-permute-start(f32[480,128]{1,0:T(8,128)S(1)} %get-tuple-element.14), channel_id=1, source_target_pairs={{0,24},{8,16},{16,8},{24,0},{1,25},{9,17},{17,9},{25,1},{2,26},{10... | collective-permute-start | bytes 737288 | tf_op jit(solution)/shard_map/ppermute | solution.py:464
  13.5 3.4 %collective-permute-start.7 = (f32[32,128]{1,0:T(8,128)S(1)}, f32[32,128]{1,0:T(8,128)S(1)}, u32[]{:S(2)}, u32[]{:S(2)}) collective-permute-start(f32[32,128]{1,0:T(8,128)S(1)} %get-tuple-element.27), channel_id=1, source_target_pairs={{0,1},{1,0},{16,17},{17,16},{2,3},{3,2},{18,19},{19,18},{4,5},{5,4... | collective-permute-start | bytes 49160 | tf_op jit(solution)/shard_map/ppermute | solution.py:376
  16.9 2.0 %shard_map.40.fz_ref = f32[5,144,128]{2,1,0:T(8,128)S(1)} custom-call(f32[5,144,128]{2,1,0:T(8,128)S(1)} %get-tuple-element.18.q_ref.qt_ref, f32[8,128]{1,0:T(8,128)S(1)} %slice_maximum_fusion.after), custom_call_target="tpu_custom_call" | custom-call | flops 16000000 | bytes 1000000 | tf_op jit(solution)/shard_map/pallas_call | solution.py:455
  18.9 0.0 collective-permute-done.3
  19.0 0.1 broadcast_select_fusion
  19.1 0.7 %collective-permute-start.5 = (f32[64,128]{1,0:T(8,128)S(1)}, f32[64,128]{1,0:T(8,128)S(1)}, u32[]{:S(2)}, u32[]{:S(2)}) collective-permute-start(f32[64,128]{1,0:T(8,128)S(1)} %get-tuple-element.19), channel_id=1, source_target_pairs={{8,14},{10,12},{12,10},{14,8},{24,30},{26,28},{28,26},{30,24},{9,1... | collective-permute-start | bytes 98312 | tf_op jit(solution)/shard_map/ppermute | solution.py:376
  19.7 0.0 collective-permute-done.7
  19.8 0.0 collective-permute-done.5
  19.8 0.7 %collective-permute-start.8 = (f32[8,128]{1,0:T(8,128)S(1)}, f32[8,128]{1,0:T(8,128)S(1)}, u32[]{:S(2)}, u32[]{:S(2)}) collective-permute-start(f32[8,128]{1,0:T(8,128)S(1)} %broadcast_maximum_fusion.after), channel_id=1, source_target_pairs={{8,24},{24,8},{9,25},{25,9},{10,26},{26,10},{11,27},{27,11},{12,28... | collective-permute-start | bytes 12296 | tf_op jit(solution)/shard_map/ppermute | solution.py:374
  20.5 2.4 %collective-permute-start.4 = (f32[64,128]{1,0:T(8,128)S(1)}, f32[64,128]{1,0:T(8,128)S(1)}, u32[]{:S(2)}, u32[]{:S(2)}) collective-permute-start(f32[64,128]{1,0:T(8,128)S(1)} %get-tuple-element.22), channel_id=1, source_target_pairs={{0,2},{2,0},{4,6},{6,4},{16,18},{18,16},{20,22},{22,20},{1,3},{3,1... | collective-permute-start | bytes 98312 | tf_op jit(solution)/shard_map/ppermute | solution.py:376
  22.8 2.0 %shard_map.39.fy_ref = f32[5,176,128]{2,1,0:T(8,128)S(1)} custom-call(f32[5,144,128]{2,1,0:T(8,128)S(1)} %get-tuple-element.12.q_ref, f32[8,128]{1,0:T(8,128)S(1)} %broadcast_maximum_fusion.2.after), custom_call_target="tpu_custom_call" | custom-call | flops 16000000 | bytes 1000000 | tf_op jit(solution)/shard_map/pallas_call | solution.py:455
  24.8 5.5 %collective-permute-start.6 = (f32[64,128]{1,0:T(8,128)S(1)}, f32[64,128]{1,0:T(8,128)S(1)}, u32[]{:S(2)}, u32[]{:S(2)}) collective-permute-start(f32[64,128]{1,0:T(8,128)S(1)} %get-tuple-element.20), channel_id=1, source_target_pairs={{0,6},{2,4},{4,2},{6,0},{16,22},{18,20},{20,18},{22,16},{1,7},{3,5... | collective-permute-start | bytes 98312 | tf_op jit(solution)/shard_map/ppermute | solution.py:376
  30.3 0.0 collective-permute-done.1.b_ref
  30.3 3.1 %shard_map.38.tx_ref = f32[5,128,128]{2,1,0:T(8,128)S(1)} custom-call(f32[5,144,128]{2,1,0:T(8,128)S(1)} %get-tuple-element.12.q_ref, f32[488,128]{1,0:T(8,128)S(1)} %collective-permute-done.a_ref, f32[480,128]{1,0:T(8,128)S(1)} %collective-permute-done.1.b_ref, f32[8,128]{1,0:T(8,128)S(1)} %broadcast_maximum_fusion.1.after), custom_call_target="tpu_custom_call" | custom-call | flops 16000000 | bytes 1000000 | tf_op jit(solution)/shard_map/pallas_call | solution.py:481
  33.4 0.0 collective-permute-done.8
  33.4 1.3 %collective-permute-start.9 = (f32[8,128]{1,0:T(8,128)S(1)}, f32[8,128]{1,0:T(8,128)S(1)}, u32[]{:S(2)}, u32[]{:S(2)}) collective-permute-start(f32[8,128]{1,0:T(8,128)S(1)} %fusion.1), channel_id=1, source_target_pairs={{8,0},{24,16},{9,1},{25,17},{10,2},{26,18},{11,3},{27,19},{12,4},{... | collective-permute-start | bytes 12296 | tf_op jit(solution)/shard_map/ppermute | solution.py:500
  34.7 0.0 collective-permute-done.4
  34.7 0.0 collective-permute-done.6
  34.8 1.0 %shard_map.41.t_ref = f32[5,128,128]{2,1,0:T(8,128)S(1)} custom-call(f32[5,144,128]{2,1,0:T(8,128)S(1)} %get-tuple-element.12.q_ref, f32[5,144,128]{2,1,0:T(8,128)S(1)} %get-tuple-element.18.q_ref.qt_ref, f32[64,128]{1,0:T(8,128)S(1)} %get-tuple-element.24.ylo, f32[64,128]{1,0:T(8,128)S(1)} %get-tuple-element.23.yhi, f32[16,128]{1,0:T(8,128)S(1)} %get-tuple-element.26.zlo, ...), custom_call_target="tpu_custom_call" | custom-call | flops 8000000 | bytes 1000000 | tf_op jit(solution)/shard_map/pallas_call | solution.py:490
  35.8 0.7 %collective-permute-done.9 = f32[8,128]{1,0:T(8,128)S(1)} collective-permute-done((f32[8,128]{1,0:T(8,128)S(1)}, f32[8,128]{1,0:T(8,128)S(1)}, u32[]{:S(2)}, u32[]{:S(2)}) %collective-permute-start.9) | collective-permute-done | bytes 4128 | tf_op jit(solution)/shard_map/ppermute | solution.py:500
  36.5 0.8 %shard_map.42 = f32[5,4,32,128]{3,2,1,0:T(8,128)} custom-call(f32[5,144,128]{2,1,0:T(8,128)S(1)} %get-tuple-element.12.q_ref, f32[5,128,128]{2,1,0:T(8,128)S(1)} %shard_map.38.tx_ref, f32[5,128,128]{2,1,0:T(8,128)S(1)} %shard_map.41.t_ref, f32[8,128]{1,0:T(8,128)S(1)} %max.50.top_ref), custom_call_target="tpu_custom_call" | custom-call | flops 1000000 | bytes 1000000 | tf_op jit(solution)/shard_map/pallas_call | solution.py:501
  (18 shorter events, 0.1 us)
Async XLA Ops:
  1.3 1.7 %collective-permute-start = (f32[488,128]{1,0:T(8,128)S(1)}, f32[488,128]{1,0:T(8,128)S(1)}, u32[]{:S(2)}, u32[]{:S(2)}) collective-permute-start(f32[488,128]{1,0:T(8,128)S(1)} %get-tuple-element.13), channel_id=1, source_target_pairs={{0,8},{8,0},{16,24},{24,16},{1,9},{9,1},{17,25},{25,17},{2,10},{10... | collective-permute-start | bytes 749576 | tf_op jit(solution)/shard_map/ppermute | solution.py:465
  3.1 0.7 %collective-permute-start.2 = (f32[32,128]{1,0:T(8,128)S(1)}, f32[32,128]{1,0:T(8,128)S(1)}, u32[]{:S(2)}, u32[]{:S(2)}) collective-permute-start(f32[32,128]{1,0:T(8,128)S(1)} %get-tuple-element.28), channel_id=1, source_target_pairs={{8,9},{9,8},{24,25},{25,24},{10,11},{11,10},{26,27},{27,26},{12,13... | collective-permute-start | bytes 49160 | tf_op jit(solution)/shard_map/ppermute | solution.py:376
  3.9 15.1 %collective-permute-start.3 = (f32[64,128]{1,0:T(8,128)S(1)}, f32[64,128]{1,0:T(8,128)S(1)}, u32[]{:S(2)}, u32[]{:S(2)}) collective-permute-start(f32[64,128]{1,0:T(8,128)S(1)} %get-tuple-element.21), channel_id=1, source_target_pairs={{8,10},{10,8},{12,14},{14,12},{24,26},{26,24},{28,30},{30,28},{9,1... | collective-permute-start | bytes 98312 | tf_op jit(solution)/shard_map/ppermute | solution.py:376
  4.6 25.8 %collective-permute-start.1 = (f32[480,128]{1,0:T(8,128)S(1)}, f32[480,128]{1,0:T(8,128)S(1)}, u32[]{:S(2)}, u32[]{:S(2)}) collective-permute-start(f32[480,128]{1,0:T(8,128)S(1)} %get-tuple-element.14), channel_id=1, source_target_pairs={{0,24},{8,16},{16,8},{24,0},{1,25},{9,17},{17,9},{25,1},{2,26},{10... | collective-permute-start | bytes 737288 | tf_op jit(solution)/shard_map/ppermute | solution.py:464
  13.5 6.2 %collective-permute-start.7 = (f32[32,128]{1,0:T(8,128)S(1)}, f32[32,128]{1,0:T(8,128)S(1)}, u32[]{:S(2)}, u32[]{:S(2)}) collective-permute-start(f32[32,128]{1,0:T(8,128)S(1)} %get-tuple-element.27), channel_id=1, source_target_pairs={{0,1},{1,0},{16,17},{17,16},{2,3},{3,2},{18,19},{19,18},{4,5},{5,4... | collective-permute-start | bytes 49160 | tf_op jit(solution)/shard_map/ppermute | solution.py:376
  19.1 0.7 %collective-permute-start.5 = (f32[64,128]{1,0:T(8,128)S(1)}, f32[64,128]{1,0:T(8,128)S(1)}, u32[]{:S(2)}, u32[]{:S(2)}) collective-permute-start(f32[64,128]{1,0:T(8,128)S(1)} %get-tuple-element.19), channel_id=1, source_target_pairs={{8,14},{10,12},{12,10},{14,8},{24,30},{26,28},{28,26},{30,24},{9,1... | collective-permute-start | bytes 98312 | tf_op jit(solution)/shard_map/ppermute | solution.py:376
  19.8 13.6 %collective-permute-start.8 = (f32[8,128]{1,0:T(8,128)S(1)}, f32[8,128]{1,0:T(8,128)S(1)}, u32[]{:S(2)}, u32[]{:S(2)}) collective-permute-start(f32[8,128]{1,0:T(8,128)S(1)} %broadcast_maximum_fusion.after), channel_id=1, source_target_pairs={{8,24},{24,8},{9,25},{25,9},{10,26},{26,10},{11,27},{27,11},{12,28... | collective-permute-start | bytes 12296 | tf_op jit(solution)/shard_map/ppermute | solution.py:374
  20.5 14.3 %collective-permute-start.4 = (f32[64,128]{1,0:T(8,128)S(1)}, f32[64,128]{1,0:T(8,128)S(1)}, u32[]{:S(2)}, u32[]{:S(2)}) collective-permute-start(f32[64,128]{1,0:T(8,128)S(1)} %get-tuple-element.22), channel_id=1, source_target_pairs={{0,2},{2,0},{4,6},{6,4},{16,18},{18,16},{20,22},{22,20},{1,3},{3,1... | collective-permute-start | bytes 98312 | tf_op jit(solution)/shard_map/ppermute | solution.py:376
  24.8 9.9 %collective-permute-start.6 = (f32[64,128]{1,0:T(8,128)S(1)}, f32[64,128]{1,0:T(8,128)S(1)}, u32[]{:S(2)}, u32[]{:S(2)}) collective-permute-start(f32[64,128]{1,0:T(8,128)S(1)} %get-tuple-element.20), channel_id=1, source_target_pairs={{0,6},{2,4},{4,2},{6,0},{16,22},{18,20},{20,18},{22,16},{1,7},{3,5... | collective-permute-start | bytes 98312 | tf_op jit(solution)/shard_map/ppermute | solution.py:376
  33.4 3.1 %collective-permute-start.9 = (f32[8,128]{1,0:T(8,128)S(1)}, f32[8,128]{1,0:T(8,128)S(1)}, u32[]{:S(2)}, u32[]{:S(2)}) collective-permute-start(f32[8,128]{1,0:T(8,128)S(1)} %fusion.1), channel_id=1, source_target_pairs={{8,0},{24,16},{9,1},{25,17},{10,2},{26,18},{11,3},{27,19},{12,4},{... | collective-permute-start | bytes 12296 | tf_op jit(solution)/shard_map/ppermute | solution.py:500

commit v5 on v3

--- a/solution.py
+++ b/solution.py
@@ -196,6 +196,7 @@
             jnp.abs(q_ref[3, here, :]) + 3.0 * sound
         )
         top = speed if top is None else jnp.maximum(top, speed)
+    top = jnp.broadcast_to(jnp.max(top, keepdims=True), (8, nz))
     top_ref[...] = top
     width = 3 * ny
     high = (nx - 3) * ny
@@ -225,10 +226,8 @@
         z_ref[1, 3 * k : 3 * k + 3, :] = qt_ref[k, nz - 3 : nz, :]
 
 
-def x_kernel(nx, ny, xeven, q_ref, a_ref, b_ref, after, out_ref, prim, uf, aux, cx, flux):
-    width = 3 * ny
-    n = nx * ny
-    far = (nx + 3) * ny
+def x_kernel(nx, ny, first, ys, xeven, q_ref, a_ref, b_ref, after, out_ref, prim, uf, aux, cx, flux):
+    far = (nx + 3) * ys
     if xeven:
         odd = lax.rem(lax.axis_index("gx"), 2)
         at_a = pl.multiple_of((1 - odd) * far, 8)
@@ -236,20 +235,25 @@
     else:
         at_a, at_b = 0, far
     for k in range(5):
-        prim[k, pl.ds(at_a, width), :] = a_ref[k * width : (k + 1) * width, :]
-        prim[k, pl.ds(at_b, width), :] = b_ref[k * width : (k + 1) * width, :]
-        prim[k, width : width + n, :] = q_ref[k, 0:n, :]
-    t = ny // 8
+        for e in range(3):
+            row = (3 * k + e) * ny + first
+            prim[k, pl.ds(pl.multiple_of(at_a + e * ys, 8), ys), :] = a_ref[row : row + ys, :]
+            prim[k, pl.ds(pl.multiple_of(at_b + e * ys, 8), ys), :] = b_ref[row : row + ys, :]
+        for x in range(nx):
+            row = x * ny + first
+            prim[k, (3 + x) * ys : (4 + x) * ys, :] = q_ref[k, row : row + ys, :]
+    t = ys // 8
     comps = (0, 1, 2)
     cell_pass(prim, uf, aux, (nx + 6) * t, comps)
-    diff_pass(uf, aux, cx, (nx + 4) * t, (nx + 5) * t, ny)
+    diff_pass(uf, aux, cx, (nx + 4) * t, (nx + 5) * t, ys)
 
     def put(k, i, value):
         flux[k, rows(i), :] = value
 
-    face_pass(prim, aux, cx, (nx + 1) * t, ny, comps, put)
-    for k in range(5):
-        out_ref[k] = flux[k, ny : ny + n, :] - flux[k, 0:n, :]
+    face_pass(prim, aux, cx, (nx + 1) * t, ys, comps, put)
+    n = nx * ys
+    for k in range(5):
+        out_ref[k] = flux[k, ys : ys + n, :] - flux[k, 0:n, :]
 
 
 def inner_kernel(count, length, block, comps, q_ref, after, out_ref, uf, aux, cx):
@@ -315,15 +319,17 @@
             )
 
 
-def final_kernel(nx, ny, q_ref, tx_ref, t_ref, top_ref, out_ref):
-    step = (cfl_number * KB) / jnp.max(top_ref[...], keepdims=True)
+def final_kernel(nx, ny, split, q_ref, tx_ref, rest_ref, t_ref, top_ref, out_ref):
+    step = (cfl_number * KB) / top_ref[0:1, :]
     for x in range(nx):
-        here = slice(x * ny, (x + 1) * ny)
-        rho, u1, u2, u3, p = (q_ref[k, here, :] for k in range(5))
-        m1, m2, m3 = rho * u1, rho * u2, rho * u3
-        energy = 2.5 * p + 0.5 * (m1 * u1 + m2 * u2 + m3 * u3)
-        for k, value in enumerate((rho, m1, m2, m3, energy)):
-            out_ref[k, x] = value - step * (tx_ref[k, here, :] + t_ref[k, here, :])
+        for lo, hi, part in ((0, split, tx_ref), (split, ny, rest_ref)):
+            here = slice(x * ny + lo, x * ny + hi)
+            there = slice(x * (hi - lo), (x + 1) * (hi - lo))
+            rho, u1, u2, u3, p = (q_ref[k, here, :] for k in range(5))
+            m1, m2, m3 = rho * u1, rho * u2, rho * u3
+            energy = 2.5 * p + 0.5 * (m1 * u1 + m2 * u2 + m3 * u3)
+            for k, value in enumerate((rho, m1, m2, m3, energy)):
+                out_ref[k, x, lo:hi] = value - step * (part[k, there, :] + t_ref[k, here, :])
 
 
 VMEM = pl.BlockSpec(memory_space=pltpu.VMEM)
@@ -343,6 +349,10 @@
     )
 
 
+def permute(value, axis, pairs):
+    return lax.ppermute(value, axis, pairs)
+
+
 def fields(*counts, r, w):
     return [pltpu.VMEM((count, r, w), f32) for count in counts]
 
@@ -361,37 +371,44 @@
         return lax.pmax(top, axis)
     d = first
     while d < n:
-        top = jnp.maximum(top, lax.ppermute(top, axis, [(i, i ^ d) for i in range(n)]))
+        top = jnp.maximum(top, permute(top, axis, [(i, i ^ d) for i in range(n)]))
         d *= 2
     return top
 
 
-def edge_trade(axis, low, high, top, mids=None):
+def with_top(edges, used, top):
+    row = lax.broadcasted_iota(jnp.int32, edges.shape, 0)
+    return jnp.where(row >= used, top[0:1], edges)
+
+
+def got_top(top, got, row):
+    return jnp.maximum(top, got[row : row + 1])
+
+
+def edge_trade(axis, low, high, used, top, mids=None):
     n = lax.axis_size(axis)
     size = low.shape[0]
     if n == 1:
         return high, low, top
     if n == 2:
-        got = lax.ppermute(jnp.concatenate([low, high, top]), axis, [(0, 1), (1, 0)])
-        return got[size : 2 * size], got[:size], jnp.maximum(top, got[2 * size :])
+        got = permute(with_top(jnp.concatenate([low, high]), size + used, top), axis, [(0, 1), (1, 0)])
+        return got[size:], got[:size], got_top(top, got, size + used)
     if n % 2:
-        lower = lax.ppermute(high, axis, [(i, (i + 1) % n) for i in range(n)])
-        upper = lax.ppermute(low, axis, [((i + 1) % n, i) for i in range(n)])
+        lower = permute(high, axis, [(i, (i + 1) % n) for i in range(n)])
+        upper = permute(low, axis, [((i + 1) % n, i) for i in range(n)])
         return lower, upper, lax.pmax(top, axis)
     odd = lax.rem(lax.axis_index(axis), 2) == 1
-    got_a = lax.ppermute(jnp.concatenate([jnp.where(odd, low, high), top]), axis, pairs_a(n))
-    top = jnp.maximum(top, got_a[size:])
+    got_a = permute(with_top(jnp.where(odd, low, high), used, top), axis, pairs_a(n))
+    top = got_top(top, got_a, used)
     if mids is not None:
         mids.append(top)
-    send_b = jnp.where(odd, high, low)
+    got_b = permute(with_top(jnp.where(odd, high, low), used, top), axis, pairs_b(n))
     if n == 4:
-        got_b = lax.ppermute(jnp.concatenate([send_b, top]), axis, pairs_b(n))
-        top = jnp.maximum(top, got_b[size:])
+        top = got_top(top, got_b, used)
     else:
-        got_b = lax.ppermute(send_b, axis, pairs_b(n))
         top = top_over(top, axis, 2)
-    lower = jnp.where(odd, got_a[:size], got_b[:size])
-    upper = jnp.where(odd, got_b[:size], got_a[:size])
+    lower = jnp.where(odd, got_a, got_b)
+    upper = jnp.where(odd, got_b, got_a)
     return lower, upper, top
 
 
@@ -413,7 +430,7 @@
             S((5, nz + 16, n), f32),
             S((width + 8, nz), f32),
             S((width, nz), f32),
-            S((2, rup(15 * nx, 8), nz), f32),
+            S((2, rup(15 * nx + 1, 8), nz), f32),
             S((2, 16, n), f32),
             S((8, nz), f32),
         ),
@@ -434,27 +451,33 @@
         )(source, after)
 
     if xeven:
-        got_b = lax.ppermute(xb, "gx", pairs_b(gx))
-        got_a = lax.ppermute(xa, "gx", pairs_a(gx))
+        got_b = permute(xb, "gx", pairs_b(gx))
+        got_a = permute(xa, "gx", pairs_a(gx))
         top = jnp.maximum(top, got_a[width:])
     else:
-        got_a = lax.ppermute(xa, "gx", [(i, (i + 1) % gx) for i in range(gx)])
-        got_b = lax.ppermute(xb, "gx", [((i + 1) % gx, i) for i in range(gx)])
+        got_a = permute(xa, "gx", [(i, (i + 1) % gx) for i in range(gx)])
+        got_b = permute(xb, "gx", [((i + 1) % gx, i) for i in range(gx)])
     ztop = top if n == nz else jnp.full((8, n), jnp.max(top))
     fz = inner(qt, nz, n, nz, 0, (2, 0, 1), nz + 16, ztop)
-    zlo, zhi, ztop = edge_trade("gz", ze[0], ze[1], ztop)
+    zlo, zhi, ztop = edge_trade("gz", ze[0], ze[1], 15, ztop)
     top = ztop if n == nz else jnp.full((8, nz), jnp.max(ztop))
     block = rup(ny + 6, 8)
     fy = inner(q, n, nz, ny, block, (1, 0, 2), nx * block + 16, top)
     mids = []
-    ylo, yhi, top = edge_trade("gy", ye[0], ye[1], top, mids)
-    tx = call(
-        functools.partial(x_kernel, nx, ny, xeven),
-        S((5, n, nz), f32),
-        sweep_flops,
-        fields(5, 10, 4, 25, 5, r=(nx + 6) * ny, w=nz),
-        [VMEM] * 3 + [ANY],
-    )(q, got_a, got_b, mids[0] if mids else top)
+    ylo, yhi, top = edge_trade("gy", ye[0], ye[1], 15 * nx, top, mids)
+
+    def along_x(first, ys, after):
+        return call(
+            functools.partial(x_kernel, nx, ny, first, ys, xeven),
+            S((5, nx * ys, nz), f32),
+            sweep_flops,
+            fields(5, 10, 4, 25, 5, r=(nx + 6) * ys + 16, w=nz),
+            [VMEM] * 3 + [ANY],
+        )(q, got_a, got_b, after)
+
+    split = rup(3 * ny // 4, 8)
+    tx = along_x(0, split, mids[0] if mids else top)
+    tx_rest = along_x(split, ny - split, top)
     near = 8 * rup(2 * nx, 8) + 16
     lanes = max(n, nz)
     t = call(
@@ -466,7 +489,9 @@
         [VMEM] * 8 + [ANY],
     )(q, qt, ylo, yhi, zlo, zhi, fy, fz, top)
     top = top_over(top, "gx", 2 if xeven else 1)
-    return call(functools.partial(final_kernel, nx, ny), S((5, nx, ny, nz), f32), 1000000)(q, tx, t, top)
+    return call(functools.partial(final_kernel, nx, ny, split), S((5, nx, ny, nz), f32), 1000000)(
+        q, tx, tx_rest, t, top
+    )
 
 
 def solution(mesh):

time: 25.8 us -> 25 us (0.969)
  waiting for transfers between devices: 4.35 us -> 3.52 us
    ppermute x6, waiting for transfers between devices: 4.35 us -> 3.52 us  [permute(): return lax.ppermute(value, axis, pairs)]
    pallas_call x2 -> x3, Pallas kernels: 3.95 us -> 3.75 us  [the longest x2 2.94 us: along_x(): call(functools.partial(x_kernel, nx, ny, first, ys, xeven), S((5, nx * ys...]
  transfers between devices with their start and end apart: 6 -> 6, of which waited for: 4 -> 4; matrix products, arithmetic and copies ran while one was open for 0% -> 0% of each run, Pallas kernels for 31% -> 32%
where the time goes in v5:
time: 25 us; the launch traced here: 24.8 us
  starting transfers between devices  10.9 us (44%)
  Pallas kernels  10 us (40%)
  waiting for transfers between devices  3.52 us (14%)
  other arithmetic  0.27 us (1%)
    ppermute x6, starting transfers between devices, permute(): return lax.ppermute(value, axis, pairs)  10.9 us
    pallas_call x2, Pallas kernels, inner(): call(functools.partial(inner_kernel, rows_in // 8, length, block, comps),...  3.94 us
    ppermute x6, waiting for transfers between devices, permute(): return lax.ppermute(value, axis, pairs)  3.52 us
    pallas_call x2, Pallas kernels, along_x(): call(functools.partial(x_kernel, nx, ny, first, ys, xeven), S((5, nx * ys...  2.94 us
    pallas_call x1, Pallas kernels, local(): call(functools.partial(prepare_kernel, nx, ny, nz, xeven), (S((5, n + 16,...  1.3 us
    pallas_call x1, Pallas kernels, local(): call(functools.partial(edge_kernel, nx, ny, nz, block), S((5, n, nz), f32...  1.02 us
    pallas_call x1, Pallas kernels, local(): call(functools.partial(final_kernel, nx, ny, split), S((5, nx, ny, nz), f...  0.82 us
  transfers between devices with their start and end apart: 6, of which 4 were waited for; matrix products, arithmetic and copies ran while one was open for 0% of the time, Pallas kernels for 32%

profile of v5, /device:TPU:0, one launch (start us, length us, event | category | flops | bytes accessed | tf_op | source)
XLA Modules:
  0.0 24.8 jit_solution(1949477451153330756)
XLA Ops:
  0.0 1.3 %shard_map.37 = (f32[5,144,128]{2,1,0:T(8,128)S(1)}, f32[5,144,128]{2,1,0:T(8,128)S(1)}, f32[488,128]{1,0:T(8,128)S(1)}, f32[480,128]{1,0:T(8,128)S(1)}, f32[2,6...) custom-call(f32[128,128]{1,0:T(8,128)} %bitcast.24, f32[3,128,128]{2,1,0:T(8,128)} %bitcast.23, ...), custom_call_target="tpu_custom_call" | custom-call | flops 2000000 | bytes 1000000 | tf_op jit(solution)/shard_map/pallas_call | solution.py:426
  1.3 0.6 %collective-permute-start = (f32[488,128]{1,0:T(8,128)S(1)}, f32[488,128]{1,0:T(8,128)S(1)}, u32[]{:S(2)}, u32[]{:S(2)}) collective-permute-start(f32[488,128]{1,0:T(8,128)S(1)} %get-tuple-element.13), channel_id=1, source_target_pairs={{0,8},{8,0},{16,24},{24,16},{1,9},{9,1},{17,25},{25,17},{2,10},{10... | collective-permute-start | bytes 749576 | tf_op jit(solution)/shard_map/ppermute | solution.py:353
  1.9 1.1 %collective-permute-done.a_ref = f32[488,128]{1,0:T(8,128)S(1)} collective-permute-done((f32[488,128]{1,0:T(8,128)S(1)}, f32[488,128]{1,0:T(8,128)S(1)}, u32[]{:S(2)}, u32[]{:S(2)}) %collective-permute-start) | collective-permute-done | bytes 249888 | tf_op jit(solution)/shard_map/ppermute | solution.py:353
  3.0 0.1 maximum_select_fusion
  3.1 2.9 %collective-permute-start.2 = (f32[32,128]{1,0:T(8,128)S(1)}, f32[32,128]{1,0:T(8,128)S(1)}, u32[]{:S(2)}, u32[]{:S(2)}) collective-permute-start(f32[32,128]{1,0:T(8,128)S(1)} %maximum_select_fusion), channel_id=1, source_target_pairs={{0,1},{1,0},{2,3},{3,2},{4,5},{5,4},{6,7},{7,6},{8,9},{9,8},{10,11... | collective-permute-start | bytes 49160 | tf_op jit(solution)/shard_map/ppermute | solution.py:353
  6.0 1.7 %collective-permute-done.2 = f32[32,128]{1,0:T(8,128)S(1)} collective-permute-done((f32[32,128]{1,0:T(8,128)S(1)}, f32[32,128]{1,0:T(8,128)S(1)}, u32[]{:S(2)}, u32[]{:S(2)}) %collective-permute-start.2) | collective-permute-done | bytes 16416 | tf_op jit(solution)/shard_map/ppermute | solution.py:353
  7.7 0.1 bitcast_select_fusion.1
  7.8 2.1 %collective-permute-start.3 = (f32[64,128]{1,0:T(8,128)S(1)}, f32[64,128]{1,0:T(8,128)S(1)}, u32[]{:S(2)}, u32[]{:S(2)}) collective-permute-start(f32[64,128]{1,0:T(8,128)S(1)} %bitcast_select_fusion.1), channel_id=1, source_target_pairs={{0,2},{2,0},{4,6},{6,4},{1,3},{3,1},{5,7},{7,5},{8,10},{10,8},{12,... | collective-permute-start | bytes 98312 | tf_op jit(solution)/shard_map/ppermute | solution.py:353
  9.9 0.0 collective-permute-start.1
  9.9 2.0 %shard_map.41.fz_ref = f32[5,144,128]{2,1,0:T(8,128)S(1)} custom-call(f32[5,144,128]{2,1,0:T(8,128)S(1)} %get-tuple-element.18.q_ref.qt_ref, f32[8,128]{1,0:T(8,128)S(1)} %slice_maximum_fusion.after), custom_call_target="tpu_custom_call" | custom-call | flops 16000000 | bytes 1000000 | tf_op jit(solution)/shard_map/pallas_call | solution.py:445
  11.9 0.0 collective-permute-done.3
  11.9 0.1 bitcast_select_fusion
  12.0 3.9 %collective-permute-start.4 = (f32[64,128]{1,0:T(8,128)S(1)}, f32[64,128]{1,0:T(8,128)S(1)}, u32[]{:S(2)}, u32[]{:S(2)}) collective-permute-start(f32[64,128]{1,0:T(8,128)S(1)} %bitcast_select_fusion), channel_id=1, source_target_pairs={{0,6},{2,4},{4,2},{6,0},{1,7},{3,5},{5,3},{7,1},{8,14},{10,12},{12... | collective-permute-start | bytes 98312 | tf_op jit(solution)/shard_map/ppermute | solution.py:353
  16.0 2.0 %shard_map.40.fy_ref = f32[5,176,128]{2,1,0:T(8,128)S(1)} custom-call(f32[5,144,128]{2,1,0:T(8,128)S(1)} %get-tuple-element.12.q_ref, f32[8,128]{1,0:T(8,128)S(1)} %broadcast_maximum_fusion.2.after), custom_call_target="tpu_custom_call" | custom-call | flops 16000000 | bytes 1000000 | tf_op jit(solution)/shard_map/pallas_call | solution.py:445
  17.9 0.2 collective-permute-done.1.b_ref
  18.1 2.2 %shard_map.38.tx_ref = f32[5,96,128]{2,1,0:T(8,128)S(1)} custom-call(f32[5,144,128]{2,1,0:T(8,128)S(1)} %get-tuple-element.12.q_ref, f32[488,128]{1,0:T(8,128)S(1)} %collective-permute-done.a_ref, f32[480,128]{1,0:T(8,128)S(1)} %collective-permute-done.1.b_ref, f32[8,128]{1,0:T(8,128)S(1)} %broadcast_maximum_fusion.1.after), custom_call_target="tpu_custom_call" | custom-call | flops 16000000 | bytes 1000000 | tf_op jit(solution)/shard_map/pallas_call | solution.py:470
  20.3 0.0 collective-permute-done.4
  20.4 1.4 %collective-permute-start.5 = (f32[8,128]{1,0:T(8,128)S(1)}, f32[8,128]{1,0:T(8,128)S(1)}, u32[]{:S(2)}, u32[]{:S(2)}) collective-permute-start(f32[8,128]{1,0:T(8,128)S(1)} %broadcast_maximum_fusion.after), channel_id=1, source_target_pairs={{0,16},{8,24},{16,0},{24,8},{1,17},{9,25},{17,1},{25,9},{2,18},{10... | collective-permute-start | bytes 12296 | tf_op jit(solution)/shard_map/ppermute | solution.py:353
  21.8 1.0 %shard_map.42.t_ref = f32[5,128,128]{2,1,0:T(8,128)S(1)} custom-call(f32[5,144,128]{2,1,0:T(8,128)S(1)} %get-tuple-element.12.q_ref, f32[5,144,128]{2,1,0:T(8,128)S(1)} %get-tuple-element.18.q_ref.qt_ref, f32[64,128]{1,0:T(8,128)S(1)} %get-tuple-element.20.ylo, f32[64,128]{1,0:T(8,128)S(1)} %get-tuple-element.19.yhi, f32[16,128]{1,0:T(8,128)S(1)} %get-tuple-element.22.zlo, ...), custom_call_target="tpu_custom_call" | custom-call | flops 8000000 | bytes 1000000 | tf_op jit(solution)/shard_map/pallas_call | solution.py:483
  22.8 0.7 %shard_map.39.rest_ref = f32[5,32,128]{2,1,0:T(8,128)S(1)} custom-call(f32[5,144,128]{2,1,0:T(8,128)S(1)} %get-tuple-element.12.q_ref, f32[488,128]{1,0:T(8,128)S(1)} %collective-permute-done.a_ref, f32[480,128]{1,0:T(8,128)S(1)} %collective-permute-done.1.b_ref, f32[8,128]{1,0:T(8,128)S(1)} %broadcast_maximum_fusion.after), custom_call_target="tpu_custom_call" | custom-call | flops 16000000 | bytes 1000000 | tf_op jit(solution)/shard_map/pallas_call | solution.py:470
  23.5 0.5 %collective-permute-done.5 = f32[8,128]{1,0:T(8,128)S(1)} collective-permute-done((f32[8,128]{1,0:T(8,128)S(1)}, f32[8,128]{1,0:T(8,128)S(1)}, u32[]{:S(2)}, u32[]{:S(2)}) %collective-permute-start.5) | collective-permute-done | bytes 4128 | tf_op jit(solution)/shard_map/ppermute | solution.py:353
  24.0 0.8 %shard_map.43 = f32[5,4,32,128]{3,2,1,0:T(8,128)} custom-call(f32[5,144,128]{2,1,0:T(8,128)S(1)} %get-tuple-element.12.q_ref, f32[5,96,128]{2,1,0:T(8,128)S(1)} %shard_map.38.tx_ref, f32[5,32,128]{2,1,0:T(8,128)S(1)} %shard_map.39.rest_ref, f32[5,128,128]{2,1,0:T(8,128)S(1)} %shard_map.42.t_ref, f32[8,128]{1,0:T(8,128)S(1)} %fusion.1.top_ref), custom_call_target="tpu_custom_call" | custom-call | flops 1000000 | bytes 1000000 | tf_op jit(solution)/shard_map/pallas_call | solution.py:492
  (16 shorter events, 0.1 us)
Async XLA Ops:
  1.3 1.7 %collective-permute-start = (f32[488,128]{1,0:T(8,128)S(1)}, f32[488,128]{1,0:T(8,128)S(1)}, u32[]{:S(2)}, u32[]{:S(2)}) collective-permute-start(f32[488,128]{1,0:T(8,128)S(1)} %get-tuple-element.13), channel_id=1, source_target_pairs={{0,8},{8,0},{16,24},{24,16},{1,9},{9,1},{17,25},{25,17},{2,10},{10... | collective-permute-start | bytes 749576 | tf_op jit(solution)/shard_map/ppermute | solution.py:353
  3.1 4.6 %collective-permute-start.2 = (f32[32,128]{1,0:T(8,128)S(1)}, f32[32,128]{1,0:T(8,128)S(1)}, u32[]{:S(2)}, u32[]{:S(2)}) collective-permute-start(f32[32,128]{1,0:T(8,128)S(1)} %maximum_select_fusion), channel_id=1, source_target_pairs={{0,1},{1,0},{2,3},{3,2},{4,5},{5,4},{6,7},{7,6},{8,9},{9,8},{10,11... | collective-permute-start | bytes 49160 | tf_op jit(solution)/shard_map/ppermute | solution.py:353
  7.8 4.1 %collective-permute-start.3 = (f32[64,128]{1,0:T(8,128)S(1)}, f32[64,128]{1,0:T(8,128)S(1)}, u32[]{:S(2)}, u32[]{:S(2)}) collective-permute-start(f32[64,128]{1,0:T(8,128)S(1)} %bitcast_select_fusion.1), channel_id=1, source_target_pairs={{0,2},{2,0},{4,6},{6,4},{1,3},{3,1},{5,7},{7,5},{8,10},{10,8},{12,... | collective-permute-start | bytes 98312 | tf_op jit(solution)/shard_map/ppermute | solution.py:353
  9.9 8.2 %collective-permute-start.1 = (f32[480,128]{1,0:T(8,128)S(1)}, f32[480,128]{1,0:T(8,128)S(1)}, u32[]{:S(2)}, u32[]{:S(2)}) collective-permute-start(f32[480,128]{1,0:T(8,128)S(1)} %get-tuple-element.14), channel_id=1, source_target_pairs={{0,24},{8,16},{16,8},{24,0},{1,25},{9,17},{17,9},{25,1},{2,26},{10... | collective-permute-start | bytes 737288 | tf_op jit(solution)/shard_map/ppermute | solution.py:353
  12.0 8.3 %collective-permute-start.4 = (f32[64,128]{1,0:T(8,128)S(1)}, f32[64,128]{1,0:T(8,128)S(1)}, u32[]{:S(2)}, u32[]{:S(2)}) collective-permute-start(f32[64,128]{1,0:T(8,128)S(1)} %bitcast_select_fusion), channel_id=1, source_target_pairs={{0,6},{2,4},{4,2},{6,0},{1,7},{3,5},{5,3},{7,1},{8,14},{10,12},{12... | collective-permute-start | bytes 98312 | tf_op jit(solution)/shard_map/ppermute | solution.py:353
  20.4 3.7 %collective-permute-start.5 = (f32[8,128]{1,0:T(8,128)S(1)}, f32[8,128]{1,0:T(8,128)S(1)}, u32[]{:S(2)}, u32[]{:S(2)}) collective-permute-start(f32[8,128]{1,0:T(8,128)S(1)} %broadcast_maximum_fusion.after), channel_id=1, source_target_pairs={{0,16},{8,24},{16,0},{24,8},{1,17},{9,25},{17,1},{25,9},{2,18},{10... | collective-permute-start | bytes 12296 | tf_op jit(solution)/shard_map/ppermute | solution.py:353

commit v6 on v5

--- a/solution.py
+++ b/solution.py
@@ -41,11 +41,11 @@
         body(i)
 
 
-def cell_pass(prim, uf, aux, count, comps):
+def cell_pass(prim, uf, aux, count, comps, first=0):
     def body(i):
-        here = rows(i)
-        rho, p = prim[0, here, :], prim[4, here, :]
-        un, ut, us = (prim[1 + c, here, :] for c in comps)
+        here, there = rows(i), rows(i + first)
+        rho, p = prim[0, there, :], prim[4, there, :]
+        un, ut, us = (prim[1 + c, there, :] for c in comps)
         inv = 1.0 / rho
         mn, mt, ms = rho * un, rho * ut, rho * us
         mnun = mn * un
@@ -107,9 +107,9 @@
     return (a + n, v[0] - a, v[2] - ut * v[0], v[3] - us * v[0], a - n)
 
 
-def face_average(prim, aux, i, s, comps):
+def face_average(prim, aux, i, s, comps, first):
     def at(ref, k, o):
-        return ref[k, rows(i, o * s), :]
+        return ref[k, rows(i if ref is aux else i + first, o * s), :]
 
     rl, rr = at(aux, 1, 2), at(aux, 1, 3)
     share = rr / (rl + rr)
@@ -164,20 +164,20 @@
     ]
 
 
-def face_pass(prim, aux, cx, count, s, comps, put):
+def face_pass(prim, aux, cx, count, s, comps, put, first=0):
     order = (0, 1 + comps[0], 1 + comps[1], 1 + comps[2], 4)
 
     def step(i, average):
-        ahead = face_average(prim, aux, i + 1, s, comps)
+        ahead = face_average(prim, aux, i + 1, s, comps, first)
         values = face_values(lambda k, o: cx[k, rows(i, (o - 1) * s), :], average)
         for m in range(5):
             put(order[m], i, values[m])
         return ahead
 
-    lax.fori_loop(0, count, step, face_average(prim, aux, 0, s, comps))
-
-
-def prepare_kernel(nx, ny, nz, xeven, rho, vel, p, q_ref, qt_ref, xa_ref, xb_ref, y_ref, z_ref, top_ref, sems):
+    lax.fori_loop(0, count, step, face_average(prim, aux, 0, s, comps, first))
+
+
+def prepare_kernel(nx, ny, nz, xeven, rho, vel, p, q_ref, xa_ref, top_ref, sems):
     n = nx * ny
     sources = (rho, vel.at[0], vel.at[1], vel.at[2], p)
     copies = [
@@ -199,17 +199,24 @@
     top = jnp.broadcast_to(jnp.max(top, keepdims=True), (8, nz))
     top_ref[...] = top
     width = 3 * ny
+    start, _ = edge_starts(nx, ny, xeven)
+    for k in range(5):
+        xa_ref[k * width : (k + 1) * width, :] = q_ref[k, pl.ds(start, width), :]
+    xa_ref[5 * width : 5 * width + 8, :] = top
+
+
+def edge_starts(nx, ny, xeven):
     high = (nx - 3) * ny
-    if xeven:
-        odd = lax.rem(lax.axis_index("gx"), 2)
-        start_a = pl.multiple_of((1 - odd) * high, 8)
-        start_b = pl.multiple_of(odd * high, 8)
-    else:
-        start_a, start_b = high, 0
-    for k in range(5):
-        xa_ref[k * width : (k + 1) * width, :] = q_ref[k, pl.ds(start_a, width), :]
-        xb_ref[k * width : (k + 1) * width, :] = q_ref[k, pl.ds(start_b, width), :]
-    xa_ref[5 * width : 5 * width + 8, :] = top
+    if not xeven:
+        return high, 0
+    odd = lax.rem(lax.axis_index("gx"), 2)
+    return pl.multiple_of((1 - odd) * high, 8), pl.multiple_of(odd * high, 8)
+
+
+def turn_kernel(nx, ny, nz, xeven, q_ref, after, qt_ref, xb_ref, y_ref, z_ref):
+    n = nx * ny
+    for k in range(5):
+        qt_ref[k, 0:nz, :] = q_ref[k, 0:n, :].T
     pad = y_ref.shape[1] - 15 * nx
     for side in (0, 1):
         if pad:
@@ -219,9 +226,12 @@
                 at = (3 * k + e) * nx
                 row = e + side * (ny - 3)
                 y_ref[side, at : at + nx, :] = q_ref[k, pl.ds(row, nx, stride=ny), :]
+    width = 3 * ny
+    _, start = edge_starts(nx, ny, xeven)
+    for k in range(5):
+        xb_ref[k * width : (k + 1) * width, :] = q_ref[k, pl.ds(start, width), :]
     z_ref[...] = jnp.zeros(z_ref.shape, f32)
     for k in range(5):
-        qt_ref[k, 0:nz, :] = q_ref[k, 0:n, :].T
         z_ref[0, 3 * k : 3 * k + 3, :] = qt_ref[k, 0:3, :]
         z_ref[1, 3 * k : 3 * k + 3, :] = qt_ref[k, nz - 3 : nz, :]
 
@@ -256,9 +266,9 @@
         out_ref[k] = flux[k, ys : ys + n, :] - flux[k, 0:n, :]
 
 
-def inner_kernel(count, length, block, comps, q_ref, after, out_ref, uf, aux, cx):
-    cell_pass(q_ref, uf, aux, count, comps)
-    diff_pass(uf, aux, cx, count, count, 1)
+def inner_kernel(first, count, more, length, block, comps, q_ref, after, out_ref, uf, aux, cx):
+    cell_pass(q_ref, uf, aux, count + more, comps, first)
+    diff_pass(uf, aux, cx, count + more, count + more, 1)
     tiles = length // 8
 
     def put(k, i, value):
@@ -266,10 +276,10 @@
             i = lax.div(i, tiles) * (block // 8) + lax.rem(i, tiles)
         out_ref[k, rows(i, 3), :] = value
 
-    face_pass(q_ref, aux, cx, count, 1, comps, put)
-
-
-def edge_kernel(nx, ny, nz, block, q_ref, qt_ref, ylo, yhi, zlo, zhi, fy_ref, fz_ref, after, out_ref, prim, uf, aux, cx, flux, fy, fz):
+    face_pass(q_ref, aux, cx, count, 1, comps, put, first)
+
+
+def edge_kernel(nx, ny, nz, block, q_ref, qt_ref, ylo, yhi, zlo, zhi, fy_ref, fz_ref, fz2_ref, after, out_ref, prim, uf, aux, cx, flux, fy, fz):
     sb = rup(2 * nx, 8)
     for k in range(5):
         for e in range(8):
@@ -307,7 +317,9 @@
     diff_pass(uf, aux, cx, 2, 2, 1)
     face_pass(prim, aux, cx, 2, 1, comps, put)
     for k in range(5):
-        fz[k, 0 : nz + 8, :] = fz_ref[k, 0 : nz + 8, :]
+        part = fz_ref.shape[1] - 8
+        fz[k, 3 : part + 3, :] = fz_ref[k, 3 : part + 3, :]
+        fz[k, part + 3 : nz + 3, :] = fz2_ref[k, 3 : nz - part + 3, :]
         fz[k, 0:3, :] = flux[k, 0:3, :]
         fz[k, nz - 2 : nz + 1, :] = flux[k, 8:11, :]
     for k in range(5):
@@ -423,30 +435,34 @@
         pltpu.with_memory_space_constraint(a, pltpu.HBM)
         for a in (density.reshape(n, nz), velocity.reshape(3, n, nz), pressure.reshape(n, nz))
     )
-    q, qt, xa, xb, ye, ze, top = call(
+    q, xa, top = call(
         functools.partial(prepare_kernel, nx, ny, nz, xeven),
-        (
-            S((5, n + 16, nz), f32),
-            S((5, nz + 16, n), f32),
-            S((width + 8, nz), f32),
-            S((width, nz), f32),
-            S((2, rup(15 * nx + 1, 8), nz), f32),
-            S((2, 16, n), f32),
-            S((8, nz), f32),
-        ),
+        (S((5, n + 16, nz), f32), S((width + 8, nz), f32), S((8, nz), f32)),
         2000000,
         [pltpu.SemaphoreType.DMA((5,))],
         [HBM] * 3,
     )(density, velocity, pressure)
+    qt, xb, ye, ze = call(
+        functools.partial(turn_kernel, nx, ny, nz, xeven),
+        (
+            S((5, nz + 16, n), f32),
+            S((width, nz), f32),
+            S((2, rup(15 * nx + 1, 8), nz), f32),
+            S((2, 16, n), f32),
+        ),
+        2000000,
+        (),
+        [VMEM, ANY],
+    )(q, top)
 
     sweep_flops = 16000000
 
-    def inner(source, rows_in, lanes, length, block, comps, rows_out, after):
+    def inner(source, first, count, more, lanes, length, block, comps, rows_out, after):
         return call(
-            functools.partial(inner_kernel, rows_in // 8, length, block, comps),
+            functools.partial(inner_kernel, first, count, more, length, block, comps),
             S((5, rows_out, lanes), f32),
             sweep_flops,
-            fields(10, 4, 25, r=rows_in + 16, w=lanes),
+            fields(10, 4, 25, r=8 * (count + more) + 16, w=lanes),
             [VMEM, ANY],
         )(source, after)
 
@@ -458,11 +474,16 @@
         got_a = permute(xa, "gx", [(i, (i + 1) % gx) for i in range(gx)])
         got_b = permute(xb, "gx", [((i + 1) % gx, i) for i in range(gx)])
     ztop = top if n == nz else jnp.full((8, n), jnp.max(top))
-    fz = inner(qt, nz, n, nz, 0, (2, 0, 1), nz + 16, ztop)
+    zt = nz // 8
+    half = zt // 2
+    fz = [
+        inner(qt, 0, half, 1, n, nz, 0, (2, 0, 1), 8 * half + 8, ye),
+        inner(qt, half, zt - half, 0, n, nz, 0, (2, 0, 1), 8 * (zt - half) + 8, ztop),
+    ]
     zlo, zhi, ztop = edge_trade("gz", ze[0], ze[1], 15, ztop)
     top = ztop if n == nz else jnp.full((8, nz), jnp.max(ztop))
     block = rup(ny + 6, 8)
-    fy = inner(q, n, nz, ny, block, (1, 0, 2), nx * block + 16, top)
+    fy = inner(q, 0, n // 8, 0, nz, ny, block, (1, 0, 2), nx * block + 16, top)
     mids = []
     ylo, yhi, top = edge_trade("gy", ye[0], ye[1], 15 * nx, top, mids)
 
@@ -486,8 +507,8 @@
         sweep_flops // 2,
         fields(5, 10, 4, 25, 5, r=near, w=lanes)
         + [pltpu.VMEM((5, nx * block + 16, nz), f32), pltpu.VMEM((5, nz + 16, n), f32)],
-        [VMEM] * 8 + [ANY],
-    )(q, qt, ylo, yhi, zlo, zhi, fy, fz, top)
+        [VMEM] * 9 + [ANY],
+    )(q, qt, ylo, yhi, zlo, zhi, fy, *fz, top)
     top = top_over(top, "gx", 2 if xeven else 1)
     return call(functools.partial(final_kernel, nx, ny, split), S((5, nx, ny, nz), f32), 1000000)(
         q, tx, tx_rest, t, top

time: 25 us -> 24.9 us (level)
    pallas_call x2 -> x4, Pallas kernels: 3.94 us -> 4.12 us  [the longest x3 3.94 us: inner(): call(functools.partial(inner_kernel, first, count, more, length, block, c...]
  transfers between devices with their start and end apart: 6 -> 6, of which waited for: 4 -> 4; matrix products, arithmetic and copies ran while one was open for 0% -> 0% of each run, Pallas kernels for 32% -> 33%
where the time goes in v6:
time: 24.9 us; the launch traced here: 24.7 us
  starting transfers between devices  10.9 us (44%)
  Pallas kernels  10.1 us (41%)
  waiting for transfers between devices  3.33 us (13%)
  other arithmetic  0.27 us (1%)
    ppermute x6, starting transfers between devices, permute(): return lax.ppermute(value, axis, pairs)  10.9 us
    pallas_call x3, Pallas kernels, inner(): call(functools.partial(inner_kernel, first, count, more, length, block, c...  3.94 us
    ppermute x6, waiting for transfers between devices, permute(): return lax.ppermute(value, axis, pairs)  3.33 us
    pallas_call x2, Pallas kernels, along_x(): call(functools.partial(x_kernel, nx, ny, first, ys, xeven), S((5, nx * ys...  2.94 us
    pallas_call x1, Pallas kernels, local(): call(functools.partial(prepare_kernel, nx, ny, nz, xeven), (S((5, n + 16,...  1.17 us
    pallas_call x1, Pallas kernels, local(): call(functools.partial(edge_kernel, nx, ny, nz, block), S((5, n, nz), f32...  1.03 us
    pallas_call x1, Pallas kernels, local(): call(functools.partial(final_kernel, nx, ny, split), S((5, nx, ny, nz), f...  0.8 us
  transfers between devices with their start and end apart: 6, of which 4 were waited for; matrix products, arithmetic and copies ran while one was open for 0% of the time, Pallas kernels for 33%

profile of v6, /device:TPU:0, one launch (start us, length us, event | category | flops | bytes accessed | tf_op | source)
XLA Modules:
  0.0 24.7 jit_solution(1832557916997481078)
XLA Ops:
  0.0 1.2 %shard_map.37 = (f32[5,144,128]{2,1,0:T(8,128)S(1)}, f32[488,128]{1,0:T(8,128)S(1)}, f32[8,128]{1,0:T(8,128)S(1)}) custom-call(f32[128,128]{1,0:T(8,128)} %bitcast.24, f32[3,128,128]{2,1,0:T(8,128)} %bitcast.23, f32[128,128]{1,0:T(8,128)} %bitcast.25), custom_call_target="tpu_custom_call" | custom-call | flops 2000000 | bytes 1000000 | tf_op jit(solution)/shard_map/pallas_call | solution.py:438
  1.2 0.6 %collective-permute-start = (f32[488,128]{1,0:T(8,128)S(1)}, f32[488,128]{1,0:T(8,128)S(1)}, u32[]{:S(2)}, u32[]{:S(2)}) collective-permute-start(f32[488,128]{1,0:T(8,128)S(1)} %get-tuple-element.13), channel_id=1, source_target_pairs={{0,8},{8,0},{16,24},{24,16},{1,9},{9,1},{17,25},{25,17},{2,10},{10... | collective-permute-start | bytes 749576 | tf_op jit(solution)/shard_map/ppermute | solution.py:365
  1.7 0.2 shard_map.38
  1.9 1.0 %collective-permute-done.a_ref = f32[488,128]{1,0:T(8,128)S(1)} collective-permute-done((f32[488,128]{1,0:T(8,128)S(1)}, f32[488,128]{1,0:T(8,128)S(1)}, u32[]{:S(2)}, u32[]{:S(2)}) %collective-permute-start) | collective-permute-done | bytes 249888 | tf_op jit(solution)/shard_map/ppermute | solution.py:365
  2.9 0.1 maximum_select_fusion
  3.0 2.9 %collective-permute-start.2 = (f32[32,128]{1,0:T(8,128)S(1)}, f32[32,128]{1,0:T(8,128)S(1)}, u32[]{:S(2)}, u32[]{:S(2)}) collective-permute-start(f32[32,128]{1,0:T(8,128)S(1)} %maximum_select_fusion), channel_id=1, source_target_pairs={{0,1},{1,0},{2,3},{3,2},{4,5},{5,4},{6,7},{7,6},{8,9},{9,8},{10,11... | collective-permute-start | bytes 49160 | tf_op jit(solution)/shard_map/ppermute | solution.py:365
  5.8 1.7 %collective-permute-done.2 = f32[32,128]{1,0:T(8,128)S(1)} collective-permute-done((f32[32,128]{1,0:T(8,128)S(1)}, f32[32,128]{1,0:T(8,128)S(1)}, u32[]{:S(2)}, u32[]{:S(2)}) %collective-permute-start.2) | collective-permute-done | bytes 16416 | tf_op jit(solution)/shard_map/ppermute | solution.py:365
  7.6 0.1 bitcast_select_fusion.1
  7.7 2.1 %collective-permute-start.3 = (f32[64,128]{1,0:T(8,128)S(1)}, f32[64,128]{1,0:T(8,128)S(1)}, u32[]{:S(2)}, u32[]{:S(2)}) collective-permute-start(f32[64,128]{1,0:T(8,128)S(1)} %bitcast_select_fusion.1), channel_id=1, source_target_pairs={{0,2},{2,0},{4,6},{6,4},{1,3},{3,1},{5,7},{7,5},{8,10},{10,8},{12,... | collective-permute-start | bytes 98312 | tf_op jit(solution)/shard_map/ppermute | solution.py:365
  9.8 0.0 collective-permute-start.1
  9.8 1.0 %shard_map.42.fz_ref = f32[5,72,128]{2,1,0:T(8,128)S(1)} custom-call(f32[5,144,128]{2,1,0:T(8,128)S(1)} %get-tuple-element.18.q_ref.qt_ref, f32[2,64,128]{2,1,0:T(8,128)S(1)} %get-tuple-element.17.after), custom_call_target="tpu_custom_call" | custom-call | flops 16000000 | bytes 1000000 | tf_op jit(solution)/shard_map/pallas_call | solution.py:461
  10.8 1.0 %shard_map.43.fz2_ref = f32[5,72,128]{2,1,0:T(8,128)S(1)} custom-call(f32[5,144,128]{2,1,0:T(8,128)S(1)} %get-tuple-element.18.q_ref.qt_ref, f32[8,128]{1,0:T(8,128)S(1)} %slice_maximum_fusion.after), custom_call_target="tpu_custom_call" | custom-call | flops 16000000 | bytes 1000000 | tf_op jit(solution)/shard_map/pallas_call | solution.py:461
  11.8 0.0 collective-permute-done.3
  11.8 0.1 bitcast_select_fusion
  11.9 3.9 %collective-permute-start.4 = (f32[64,128]{1,0:T(8,128)S(1)}, f32[64,128]{1,0:T(8,128)S(1)}, u32[]{:S(2)}, u32[]{:S(2)}) collective-permute-start(f32[64,128]{1,0:T(8,128)S(1)} %bitcast_select_fusion), channel_id=1, source_target_pairs={{0,6},{2,4},{4,2},{6,0},{1,7},{3,5},{5,3},{7,1},{8,14},{10,12},{12... | collective-permute-start | bytes 98312 | tf_op jit(solution)/shard_map/ppermute | solution.py:365
  15.8 2.0 %shard_map.41.fy_ref = f32[5,176,128]{2,1,0:T(8,128)S(1)} custom-call(f32[5,144,128]{2,1,0:T(8,128)S(1)} %get-tuple-element.12.q_ref, f32[8,128]{1,0:T(8,128)S(1)} %broadcast_maximum_fusion.2.after), custom_call_target="tpu_custom_call" | custom-call | flops 16000000 | bytes 1000000 | tf_op jit(solution)/shard_map/pallas_call | solution.py:461
  17.8 0.2 collective-permute-done.1.b_ref
  18.0 2.2 %shard_map.39.tx_ref = f32[5,96,128]{2,1,0:T(8,128)S(1)} custom-call(f32[5,144,128]{2,1,0:T(8,128)S(1)} %get-tuple-element.12.q_ref, f32[488,128]{1,0:T(8,128)S(1)} %collective-permute-done.a_ref, f32[480,128]{1,0:T(8,128)S(1)} %collective-permute-done.1.b_ref, f32[8,128]{1,0:T(8,128)S(1)} %broadcast_maximum_fusion.1.after), custom_call_target="tpu_custom_call" | custom-call | flops 16000000 | bytes 1000000 | tf_op jit(solution)/shard_map/pallas_call | solution.py:491
  20.2 0.0 collective-permute-done.4
  20.2 1.4 %collective-permute-start.5 = (f32[8,128]{1,0:T(8,128)S(1)}, f32[8,128]{1,0:T(8,128)S(1)}, u32[]{:S(2)}, u32[]{:S(2)}) collective-permute-start(f32[8,128]{1,0:T(8,128)S(1)} %broadcast_maximum_fusion.after), channel_id=1, source_target_pairs={{0,16},{8,24},{16,0},{24,8},{1,17},{9,25},{17,1},{25,9},{2,18},{10... | collective-permute-start | bytes 12296 | tf_op jit(solution)/shard_map/ppermute | solution.py:365
  21.6 1.0 %shard_map.44.t_ref = f32[5,128,128]{2,1,0:T(8,128)S(1)} custom-call(f32[5,144,128]{2,1,0:T(8,128)S(1)} %get-tuple-element.12.q_ref, f32[5,144,128]{2,1,0:T(8,128)S(1)} %get-tuple-element.18.q_ref.qt_ref, f32[64,128]{1,0:T(8,128)S(1)} %get-tuple-element.20.ylo, f32[64,128]{1,0:T(8,128)S(1)} %get-tuple-element.19.yhi, f32[16,128]{1,0:T(8,128)S(1)} %get-tuple-element.22.zlo, ...), custom_call_target="tpu_custom_call" | custom-call | flops 8000000 | bytes 1000000 | tf_op jit(solution)/shard_map/pallas_call | solution.py:504
  22.7 0.7 %shard_map.40.rest_ref = f32[5,32,128]{2,1,0:T(8,128)S(1)} custom-call(f32[5,144,128]{2,1,0:T(8,128)S(1)} %get-tuple-element.12.q_ref, f32[488,128]{1,0:T(8,128)S(1)} %collective-permute-done.a_ref, f32[480,128]{1,0:T(8,128)S(1)} %collective-permute-done.1.b_ref, f32[8,128]{1,0:T(8,128)S(1)} %broadcast_maximum_fusion.after), custom_call_target="tpu_custom_call" | custom-call | flops 16000000 | bytes 1000000 | tf_op jit(solution)/shard_map/pallas_call | solution.py:491
  23.4 0.5 %collective-permute-done.5 = f32[8,128]{1,0:T(8,128)S(1)} collective-permute-done((f32[8,128]{1,0:T(8,128)S(1)}, f32[8,128]{1,0:T(8,128)S(1)}, u32[]{:S(2)}, u32[]{:S(2)}) %collective-permute-start.5) | collective-permute-done | bytes 4128 | tf_op jit(solution)/shard_map/ppermute | solution.py:365
  23.9 0.8 %shard_map.45 = f32[5,4,32,128]{3,2,1,0:T(8,128)} custom-call(f32[5,144,128]{2,1,0:T(8,128)S(1)} %get-tuple-element.12.q_ref, f32[5,96,128]{2,1,0:T(8,128)S(1)} %shard_map.39.tx_ref, f32[5,32,128]{2,1,0:T(8,128)S(1)} %shard_map.40.rest_ref, f32[5,128,128]{2,1,0:T(8,128)S(1)} %shard_map.44.t_ref, f32[8,128]{1,0:T(8,128)S(1)} %fusion.1.top_ref), custom_call_target="tpu_custom_call" | custom-call | flops 1000000 | bytes 1000000 | tf_op jit(solution)/shard_map/pallas_call | solution.py:513
  (16 shorter events, 0.1 us)
Async XLA Ops:
  1.2 1.7 %collective-permute-start = (f32[488,128]{1,0:T(8,128)S(1)}, f32[488,128]{1,0:T(8,128)S(1)}, u32[]{:S(2)}, u32[]{:S(2)}) collective-permute-start(f32[488,128]{1,0:T(8,128)S(1)} %get-tuple-element.13), channel_id=1, source_target_pairs={{0,8},{8,0},{16,24},{24,16},{1,9},{9,1},{17,25},{25,17},{2,10},{10... | collective-permute-start | bytes 749576 | tf_op jit(solution)/shard_map/ppermute | solution.py:365
  3.0 4.6 %collective-permute-start.2 = (f32[32,128]{1,0:T(8,128)S(1)}, f32[32,128]{1,0:T(8,128)S(1)}, u32[]{:S(2)}, u32[]{:S(2)}) collective-permute-start(f32[32,128]{1,0:T(8,128)S(1)} %maximum_select_fusion), channel_id=1, source_target_pairs={{0,1},{1,0},{2,3},{3,2},{4,5},{5,4},{6,7},{7,6},{8,9},{9,8},{10,11... | collective-permute-start | bytes 49160 | tf_op jit(solution)/shard_map/ppermute | solution.py:365
  7.7 4.1 %collective-permute-start.3 = (f32[64,128]{1,0:T(8,128)S(1)}, f32[64,128]{1,0:T(8,128)S(1)}, u32[]{:S(2)}, u32[]{:S(2)}) collective-permute-start(f32[64,128]{1,0:T(8,128)S(1)} %bitcast_select_fusion.1), channel_id=1, source_target_pairs={{0,2},{2,0},{4,6},{6,4},{1,3},{3,1},{5,7},{7,5},{8,10},{10,8},{12,... | collective-permute-start | bytes 98312 | tf_op jit(solution)/shard_map/ppermute | solution.py:365
  9.8 8.2 %collective-permute-start.1 = (f32[480,128]{1,0:T(8,128)S(1)}, f32[480,128]{1,0:T(8,128)S(1)}, u32[]{:S(2)}, u32[]{:S(2)}) collective-permute-start(f32[480,128]{1,0:T(8,128)S(1)} %get-tuple-element.15), channel_id=1, source_target_pairs={{0,24},{8,16},{16,8},{24,0},{1,25},{9,17},{17,9},{25,1},{2,26},{10... | collective-permute-start | bytes 737288 | tf_op jit(solution)/shard_map/ppermute | solution.py:365
  11.9 8.3 %collective-permute-start.4 = (f32[64,128]{1,0:T(8,128)S(1)}, f32[64,128]{1,0:T(8,128)S(1)}, u32[]{:S(2)}, u32[]{:S(2)}) collective-permute-start(f32[64,128]{1,0:T(8,128)S(1)} %bitcast_select_fusion), channel_id=1, source_target_pairs={{0,6},{2,4},{4,2},{6,0},{1,7},{3,5},{5,3},{7,1},{8,14},{10,12},{12... | collective-permute-start | bytes 98312 | tf_op jit(solution)/shard_map/ppermute | solution.py:365
  20.2 3.7 %collective-permute-start.5 = (f32[8,128]{1,0:T(8,128)S(1)}, f32[8,128]{1,0:T(8,128)S(1)}, u32[]{:S(2)}, u32[]{:S(2)}) collective-permute-start(f32[8,128]{1,0:T(8,128)S(1)} %broadcast_maximum_fusion.after), channel_id=1, source_target_pairs={{0,16},{8,24},{16,0},{24,8},{1,17},{9,25},{17,1},{25,9},{2,18},{10... | collective-permute-start | bytes 12296 | tf_op jit(solution)/shard_map/ppermute | solution.py:365

commit v7 on v6

--- a/solution.py
+++ b/solution.py
@@ -279,18 +279,47 @@
     face_pass(q_ref, aux, cx, count, 1, comps, put, first)
 
 
-def edge_kernel(nx, ny, nz, block, q_ref, qt_ref, ylo, yhi, zlo, zhi, fy_ref, fz_ref, fz2_ref, after, out_ref, prim, uf, aux, cx, flux, fy, fz):
+def z_ends_kernel(nz, qt_ref, lo, hi, fz_ref, fz2_ref, after, out_ref, prim, uf, aux, cx, flux, fz):
+    for k in range(5):
+        prim[k] = jnp.ones(prim.shape[1:], f32)
+        for j in range(6):
+            if j < 3:
+                prim[k, 8 * j : 8 * j + 3 - j, :] = lo[3 * k + j : 3 * k + 3, :]
+            if j > 0:
+                prim[k, 8 * j + max(3 - j, 0) : 8 * j + 3, :] = qt_ref[k, max(j - 3, 0) : j, :]
+            if j < 5:
+                prim[k, 8 * j + 3 : 8 * j + 3 + min(5 - j, 3), :] = qt_ref[k, nz - 5 + j : nz - 5 + j + min(5 - j, 3), :]
+            if j > 2:
+                prim[k, 8 * j + 8 - j : 8 * j + 6, :] = hi[3 * k : 3 * k + j - 2, :]
+
+    def put(k, i, value):
+        flux[k, rows(i), :] = value
+
+    comps = (2, 0, 1)
+    cell_pass(prim, uf, aux, 6, comps)
+    diff_pass(uf, aux, cx, 4, 5, 8)
+    face_pass(prim, aux, cx, 1, 8, comps, put)
+    part = fz_ref.shape[1] - 8
+    for k in range(5):
+        fz[k, 3 : part + 3, :] = fz_ref[k, 3 : part + 3, :]
+        fz[k, part + 3 : nz + 3, :] = fz2_ref[k, 3 : nz - part + 3, :]
+        fz[k, 0:3, :] = flux[k, 0:3, :]
+        fz[k, nz - 2 : nz + 1, :] = flux[k, 3:6, :]
+        out_ref[k] = (fz[k, 1 : nz + 1, :] - fz[k, 0:nz, :]).T
+
+
+def y_ends_kernel(nx, ny, block, q_ref, lo, hi, fy_ref, tz_ref, after, out_ref, prim, uf, aux, cx, flux, fy):
     sb = rup(2 * nx, 8)
     for k in range(5):
         for e in range(8):
             if e < 3:
-                low = ylo[(3 * k + e) * nx : (3 * k + e + 1) * nx, :]
+                low = lo[(3 * k + e) * nx : (3 * k + e + 1) * nx, :]
             else:
                 low = q_ref[k, pl.ds(e - 3, nx, stride=ny), :]
             if e < 5:
                 high = q_ref[k, pl.ds(ny - 5 + e, nx, stride=ny), :]
             else:
-                high = yhi[(3 * k + e - 5) * nx : (3 * k + e - 4) * nx, :]
+                high = hi[(3 * k + e - 5) * nx : (3 * k + e - 4) * nx, :]
             prim[k, e * sb : e * sb + nx, :] = low
             prim[k, e * sb + nx : e * sb + 2 * nx, :] = high
     t = sb // 8
@@ -307,28 +336,10 @@
         for f in range(3):
             fy[k, pl.ds(f, nx, stride=block), :] = flux[k, f * sb : f * sb + nx, :]
             fy[k, pl.ds(ny - 2 + f, nx, stride=block), :] = flux[k, f * sb + nx : f * sb + 2 * nx, :]
-    for k in range(5):
-        prim[k, 0:3, :] = zlo[3 * k : 3 * k + 3, :]
-        prim[k, 3:8, :] = qt_ref[k, 0:5, :]
-        prim[k, 8:13, :] = qt_ref[k, nz - 5 : nz, :]
-        prim[k, 13:16, :] = zhi[3 * k : 3 * k + 3, :]
-    comps = (2, 0, 1)
-    cell_pass(prim, uf, aux, 2, comps)
-    diff_pass(uf, aux, cx, 2, 2, 1)
-    face_pass(prim, aux, cx, 2, 1, comps, put)
-    for k in range(5):
-        part = fz_ref.shape[1] - 8
-        fz[k, 3 : part + 3, :] = fz_ref[k, 3 : part + 3, :]
-        fz[k, part + 3 : nz + 3, :] = fz2_ref[k, 3 : nz - part + 3, :]
-        fz[k, 0:3, :] = flux[k, 0:3, :]
-        fz[k, nz - 2 : nz + 1, :] = flux[k, 8:11, :]
-    for k in range(5):
-        across = (fz[k, 1 : nz + 1, :] - fz[k, 0:nz, :]).T
         for x in range(nx):
             at = x * block
-            out_ref[k, x * ny : (x + 1) * ny, :] = across[x * ny : (x + 1) * ny, :] + (
-                fy[k, at + 1 : at + 1 + ny, :] - fy[k, at : at + ny, :]
-            )
+            here = slice(x * ny, (x + 1) * ny)
+            out_ref[k, here, :] = tz_ref[k, here, :] + (fy[k, at + 1 : at + 1 + ny, :] - fy[k, at : at + ny, :])
 
 
 def final_kernel(nx, ny, split, q_ref, tx_ref, rest_ref, t_ref, top_ref, out_ref):
@@ -483,6 +494,7 @@
     zlo, zhi, ztop = edge_trade("gz", ze[0], ze[1], 15, ztop)
     top = ztop if n == nz else jnp.full((8, nz), jnp.max(ztop))
     block = rup(ny + 6, 8)
+    ytop = top
     fy = inner(q, 0, n // 8, 0, nz, ny, block, (1, 0, 2), nx * block + 16, top)
     mids = []
     ylo, yhi, top = edge_trade("gy", ye[0], ye[1], 15 * nx, top, mids)
@@ -496,19 +508,23 @@
             [VMEM] * 3 + [ANY],
         )(q, got_a, got_b, after)
 
-    split = rup(3 * ny // 4, 8)
+    split = rup(ny // 2, 8)
     tx = along_x(0, split, mids[0] if mids else top)
     tx_rest = along_x(split, ny - split, top)
-    near = 8 * rup(2 * nx, 8) + 16
-    lanes = max(n, nz)
+    tz = call(
+        functools.partial(z_ends_kernel, nz),
+        S((5, n, nz), f32),
+        sweep_flops // 4,
+        fields(5, 10, 4, 25, 5, r=64, w=n) + [pltpu.VMEM((5, nz + 16, n), f32)],
+        [VMEM] * 5 + [ANY],
+    )(qt, zlo, zhi, *fz, ytop)
     t = call(
-        functools.partial(edge_kernel, nx, ny, nz, block),
+        functools.partial(y_ends_kernel, nx, ny, block),
         S((5, n, nz), f32),
-        sweep_flops // 2,
-        fields(5, 10, 4, 25, 5, r=near, w=lanes)
-        + [pltpu.VMEM((5, nx * block + 16, nz), f32), pltpu.VMEM((5, nz + 16, n), f32)],
-        [VMEM] * 9 + [ANY],
-    )(q, qt, ylo, yhi, zlo, zhi, fy, *fz, top)
+        sweep_flops // 4,
+        fields(5, 10, 4, 25, 5, r=8 * rup(2 * nx, 8) + 16, w=nz) + [pltpu.VMEM((5, nx * block + 16, nz), f32)],
+        [VMEM] * 5 + [ANY],
+    )(q, ylo, yhi, fy, tz, top)
     top = top_over(top, "gx", 2 if xeven else 1)
     return call(functools.partial(final_kernel, nx, ny, split), S((5, nx, ny, nz), f32), 1000000)(
         q, tx, tx_rest, t, top

time: 24.9 us -> 24.3 us (0.976)
  waiting for transfers between devices: 3.33 us -> 2.72 us
    ppermute x6, waiting for transfers between devices: 3.33 us -> 2.72 us  [permute(): return lax.ppermute(value, axis, pairs)]
    pallas_call x1 -> x2, Pallas kernels: 1.03 us -> 1.01 us  [the longest x1 0.62 us: local(): call(functools.partial(y_ends_kernel, nx, ny, block), S((5, n, nz), f32),...]
  transfers between devices with their start and end apart: 6 -> 6, of which waited for: 4 -> 2; matrix products, arithmetic and copies ran while one was open for 0% -> 0% of each run, Pallas kernels for 33% -> 33%
where the time goes in v7:
time: 24.3 us; the launch traced here: 24.2 us
  starting transfers between devices  11.1 us (46%)
  Pallas kernels  9.98 us (41%)
  waiting for transfers between devices  2.72 us (11%)
  other arithmetic  0.27 us (1%)
    ppermute x6, starting transfers between devices, permute(): return lax.ppermute(value, axis, pairs)  11.1 us
    pallas_call x3, Pallas kernels, inner(): call(functools.partial(inner_kernel, first, count, more, length, block, c...  3.95 us
    pallas_call x2, Pallas kernels, along_x(): call(functools.partial(x_kernel, nx, ny, first, ys, xeven), S((5, nx * ys...  2.87 us
    ppermute x6, waiting for transfers between devices, permute(): return lax.ppermute(value, axis, pairs)  2.72 us
    pallas_call x1, Pallas kernels, local(): call(functools.partial(prepare_kernel, nx, ny, nz, xeven), (S((5, n + 16,...  1.17 us
    pallas_call x1, Pallas kernels, local(): call(functools.partial(final_kernel, nx, ny, split), S((5, nx, ny, nz), f...  0.81 us
    pallas_call x1, Pallas kernels, local(): call(functools.partial(y_ends_kernel, nx, ny, block), S((5, n, nz), f32),...  0.62 us
  transfers between devices with their start and end apart: 6, of which 2 were waited for; matrix products, arithmetic and copies ran while one was open for 0% of the time, Pallas kernels for 33%

profile of v7, /device:TPU:0, one launch (start us, length us, event | category | flops | bytes accessed | tf_op | source)
XLA Modules:
  0.0 24.2 jit_solution(2089416104730490719)
XLA Ops:
  0.0 1.2 %shard_map.37 = (f32[5,144,128]{2,1,0:T(8,128)S(1)}, f32[488,128]{1,0:T(8,128)S(1)}, f32[8,128]{1,0:T(8,128)S(1)}) custom-call(f32[128,128]{1,0:T(8,128)} %bitcast.24, f32[3,128,128]{2,1,0:T(8,128)} %bitcast.23, f32[128,128]{1,0:T(8,128)} %bitcast.25), custom_call_target="tpu_custom_call" | custom-call | flops 2000000 | bytes 1000000 | tf_op jit(solution)/shard_map/pallas_call | solution.py:449
  1.2 0.6 %collective-permute-start = (f32[488,128]{1,0:T(8,128)S(1)}, f32[488,128]{1,0:T(8,128)S(1)}, u32[]{:S(2)}, u32[]{:S(2)}) collective-permute-start(f32[488,128]{1,0:T(8,128)S(1)} %get-tuple-element.13), channel_id=1, source_target_pairs={{0,8},{8,0},{16,24},{24,16},{1,9},{9,1},{17,25},{25,17},{2,10},{10... | collective-permute-start | bytes 749576 | tf_op jit(solution)/shard_map/ppermute | solution.py:376
  1.7 0.2 shard_map.38
  1.9 1.0 %collective-permute-done.a_ref = f32[488,128]{1,0:T(8,128)S(1)} collective-permute-done((f32[488,128]{1,0:T(8,128)S(1)}, f32[488,128]{1,0:T(8,128)S(1)}, u32[]{:S(2)}, u32[]{:S(2)}) %collective-permute-start) | collective-permute-done | bytes 249888 | tf_op jit(solution)/shard_map/ppermute | solution.py:376
  2.9 0.1 maximum_select_fusion
  3.0 2.9 %collective-permute-start.2 = (f32[32,128]{1,0:T(8,128)S(1)}, f32[32,128]{1,0:T(8,128)S(1)}, u32[]{:S(2)}, u32[]{:S(2)}) collective-permute-start(f32[32,128]{1,0:T(8,128)S(1)} %maximum_select_fusion), channel_id=1, source_target_pairs={{0,1},{1,0},{2,3},{3,2},{4,5},{5,4},{6,7},{7,6},{8,9},{9,8},{10,11... | collective-permute-start | bytes 49160 | tf_op jit(solution)/shard_map/ppermute | solution.py:376
  5.8 1.7 %collective-permute-done.2 = f32[32,128]{1,0:T(8,128)S(1)} collective-permute-done((f32[32,128]{1,0:T(8,128)S(1)}, f32[32,128]{1,0:T(8,128)S(1)}, u32[]{:S(2)}, u32[]{:S(2)}) %collective-permute-start.2) | collective-permute-done | bytes 16416 | tf_op jit(solution)/shard_map/ppermute | solution.py:376
  7.6 0.1 bitcast_select_fusion.1
  7.7 2.1 %collective-permute-start.3 = (f32[64,128]{1,0:T(8,128)S(1)}, f32[64,128]{1,0:T(8,128)S(1)}, u32[]{:S(2)}, u32[]{:S(2)}) collective-permute-start(f32[64,128]{1,0:T(8,128)S(1)} %bitcast_select_fusion.1), channel_id=1, source_target_pairs={{0,2},{2,0},{4,6},{6,4},{1,3},{3,1},{5,7},{7,5},{8,10},{10,8},{12,... | collective-permute-start | bytes 98312 | tf_op jit(solution)/shard_map/ppermute | solution.py:376
  9.8 0.0 collective-permute-start.1
  9.8 1.0 %shard_map.42.fz_ref = f32[5,72,128]{2,1,0:T(8,128)S(1)} custom-call(f32[5,144,128]{2,1,0:T(8,128)S(1)} %get-tuple-element.18.q_ref.qt_ref, f32[2,64,128]{2,1,0:T(8,128)S(1)} %get-tuple-element.17.after), custom_call_target="tpu_custom_call" | custom-call | flops 16000000 | bytes 1000000 | tf_op jit(solution)/shard_map/pallas_call | solution.py:472
  10.8 1.0 %shard_map.43.fz2_ref = f32[5,72,128]{2,1,0:T(8,128)S(1)} custom-call(f32[5,144,128]{2,1,0:T(8,128)S(1)} %get-tuple-element.18.q_ref.qt_ref, f32[8,128]{1,0:T(8,128)S(1)} %slice_maximum_fusion.after), custom_call_target="tpu_custom_call" | custom-call | flops 16000000 | bytes 1000000 | tf_op jit(solution)/shard_map/pallas_call | solution.py:472
  11.8 0.0 collective-permute-done.3
  11.8 0.1 bitcast_select_fusion
  11.9 3.9 %collective-permute-start.4 = (f32[64,128]{1,0:T(8,128)S(1)}, f32[64,128]{1,0:T(8,128)S(1)}, u32[]{:S(2)}, u32[]{:S(2)}) collective-permute-start(f32[64,128]{1,0:T(8,128)S(1)} %bitcast_select_fusion), channel_id=1, source_target_pairs={{0,6},{2,4},{4,2},{6,0},{1,7},{3,5},{5,3},{7,1},{8,14},{10,12},{12... | collective-permute-start | bytes 98312 | tf_op jit(solution)/shard_map/ppermute | solution.py:376
  15.8 0.4 %shard_map.44.tz_ref = f32[5,128,128]{2,1,0:T(8,128)S(1)} custom-call(f32[5,144,128]{2,1,0:T(8,128)S(1)} %get-tuple-element.18.q_ref.qt_ref, f32[16,128]{1,0:T(8,128)S(1)} %get-tuple-element.22.lo, f32[16,128]{1,0:T(8,128)S(1)} %get-tuple-element.21.hi, f32[5,72,128]{2,1,0:T(8,128)S(1)} %shard_map.42.fz_ref, f32[5,72,128]{2,1,0:T(8,128)S(1)} %shard_map.43.fz2_ref, ...), custom_call_target="tpu_custom_call" | custom-call | flops 4000000 | bytes 1000000 | tf_op jit(solution)/shard_map/pallas_call | solution.py:514
  16.2 2.0 %shard_map.41.fy_ref = f32[5,176,128]{2,1,0:T(8,128)S(1)} custom-call(f32[5,144,128]{2,1,0:T(8,128)S(1)} %get-tuple-element.12.q_ref, f32[8,128]{1,0:T(8,128)S(1)} %broadcast_maximum_fusion.2.after), custom_call_target="tpu_custom_call" | custom-call | flops 16000000 | bytes 1000000 | tf_op jit(solution)/shard_map/pallas_call | solution.py:472
  18.2 0.0 collective-permute-done.1.b_ref
  18.2 1.4 %shard_map.39.tx_ref = f32[5,64,128]{2,1,0:T(8,128)S(1)} custom-call(f32[5,144,128]{2,1,0:T(8,128)S(1)} %get-tuple-element.12.q_ref, f32[488,128]{1,0:T(8,128)S(1)} %collective-permute-done.a_ref, f32[480,128]{1,0:T(8,128)S(1)} %collective-permute-done.1.b_ref, f32[8,128]{1,0:T(8,128)S(1)} %broadcast_maximum_fusion.1.after), custom_call_target="tpu_custom_call" | custom-call | flops 16000000 | bytes 1000000 | tf_op jit(solution)/shard_map/pallas_call | solution.py:503
  19.7 0.0 collective-permute-done.4
  19.7 1.6 %collective-permute-start.5 = (f32[8,128]{1,0:T(8,128)S(1)}, f32[8,128]{1,0:T(8,128)S(1)}, u32[]{:S(2)}, u32[]{:S(2)}) collective-permute-start(f32[8,128]{1,0:T(8,128)S(1)} %broadcast_maximum_fusion.after), channel_id=1, source_target_pairs={{0,16},{8,24},{16,0},{24,8},{1,17},{9,25},{17,1},{25,9},{2,18},{10... | collective-permute-start | bytes 12296 | tf_op jit(solution)/shard_map/ppermute | solution.py:376
  21.3 0.6 %shard_map.45.t_ref = f32[5,128,128]{2,1,0:T(8,128)S(1)} custom-call(f32[5,144,128]{2,1,0:T(8,128)S(1)} %get-tuple-element.12.q_ref, f32[64,128]{1,0:T(8,128)S(1)} %get-tuple-element.20.lo, f32[64,128]{1,0:T(8,128)S(1)} %get-tuple-element.19.hi, f32[5,176,128]{2,1,0:T(8,128)S(1)} %shard_map.41.fy_ref, f32[5,128,128]{2,1,0:T(8,128)S(1)} %shard_map.44.tz_ref, ...), custom_call_target="tpu_custom_call" | custom-call | flops 4000000 | bytes 1000000 | tf_op jit(solution)/shard_map/pallas_call | solution.py:521
  21.9 1.4 %shard_map.40.rest_ref = f32[5,64,128]{2,1,0:T(8,128)S(1)} custom-call(f32[5,144,128]{2,1,0:T(8,128)S(1)} %get-tuple-element.12.q_ref, f32[488,128]{1,0:T(8,128)S(1)} %collective-permute-done.a_ref, f32[480,128]{1,0:T(8,128)S(1)} %collective-permute-done.1.b_ref, f32[8,128]{1,0:T(8,128)S(1)} %broadcast_maximum_fusion.after), custom_call_target="tpu_custom_call" | custom-call | flops 16000000 | bytes 1000000 | tf_op jit(solution)/shard_map/pallas_call | solution.py:503
  23.3 0.0 collective-permute-done.5
  23.4 0.8 %shard_map.46 = f32[5,4,32,128]{3,2,1,0:T(8,128)} custom-call(f32[5,144,128]{2,1,0:T(8,128)S(1)} %get-tuple-element.12.q_ref, f32[5,64,128]{2,1,0:T(8,128)S(1)} %shard_map.39.tx_ref, f32[5,64,128]{2,1,0:T(8,128)S(1)} %shard_map.40.rest_ref, f32[5,128,128]{2,1,0:T(8,128)S(1)} %shard_map.45.t_ref, f32[8,128]{1,0:T(8,128)S(1)} %fusion.1.top_ref), custom_call_target="tpu_custom_call" | custom-call | flops 1000000 | bytes 1000000 | tf_op jit(solution)/shard_map/pallas_call | solution.py:529
  (16 shorter events, 0.1 us)
Async XLA Ops:
  1.2 1.7 %collective-permute-start = (f32[488,128]{1,0:T(8,128)S(1)}, f32[488,128]{1,0:T(8,128)S(1)}, u32[]{:S(2)}, u32[]{:S(2)}) collective-permute-start(f32[488,128]{1,0:T(8,128)S(1)} %get-tuple-element.13), channel_id=1, source_target_pairs={{0,8},{8,0},{16,24},{24,16},{1,9},{9,1},{17,25},{25,17},{2,10},{10... | collective-permute-start | bytes 749576 | tf_op jit(solution)/shard_map/ppermute | solution.py:376
  3.0 4.6 %collective-permute-start.2 = (f32[32,128]{1,0:T(8,128)S(1)}, f32[32,128]{1,0:T(8,128)S(1)}, u32[]{:S(2)}, u32[]{:S(2)}) collective-permute-start(f32[32,128]{1,0:T(8,128)S(1)} %maximum_select_fusion), channel_id=1, source_target_pairs={{0,1},{1,0},{2,3},{3,2},{4,5},{5,4},{6,7},{7,6},{8,9},{9,8},{10,11... | collective-permute-start | bytes 49160 | tf_op jit(solution)/shard_map/ppermute | solution.py:376
  7.7 4.1 %collective-permute-start.3 = (f32[64,128]{1,0:T(8,128)S(1)}, f32[64,128]{1,0:T(8,128)S(1)}, u32[]{:S(2)}, u32[]{:S(2)}) collective-permute-start(f32[64,128]{1,0:T(8,128)S(1)} %bitcast_select_fusion.1), channel_id=1, source_target_pairs={{0,2},{2,0},{4,6},{6,4},{1,3},{3,1},{5,7},{7,5},{8,10},{10,8},{12,... | collective-permute-start | bytes 98312 | tf_op jit(solution)/shard_map/ppermute | solution.py:376
  9.8 8.4 %collective-permute-start.1 = (f32[480,128]{1,0:T(8,128)S(1)}, f32[480,128]{1,0:T(8,128)S(1)}, u32[]{:S(2)}, u32[]{:S(2)}) collective-permute-start(f32[480,128]{1,0:T(8,128)S(1)} %get-tuple-element.15), channel_id=1, source_target_pairs={{0,24},{8,16},{16,8},{24,0},{1,25},{9,17},{17,9},{25,1},{2,26},{10... | collective-permute-start | bytes 737288 | tf_op jit(solution)/shard_map/ppermute | solution.py:376
  11.9 7.8 %collective-permute-start.4 = (f32[64,128]{1,0:T(8,128)S(1)}, f32[64,128]{1,0:T(8,128)S(1)}, u32[]{:S(2)}, u32[]{:S(2)}) collective-permute-start(f32[64,128]{1,0:T(8,128)S(1)} %bitcast_select_fusion), channel_id=1, source_target_pairs={{0,6},{2,4},{4,2},{6,0},{1,7},{3,5},{5,3},{7,1},{8,14},{10,12},{12... | collective-permute-start | bytes 98312 | tf_op jit(solution)/shard_map/ppermute | solution.py:376
  19.7 3.7 %collective-permute-start.5 = (f32[8,128]{1,0:T(8,128)S(1)}, f32[8,128]{1,0:T(8,128)S(1)}, u32[]{:S(2)}, u32[]{:S(2)}) collective-permute-start(f32[8,128]{1,0:T(8,128)S(1)} %broadcast_maximum_fusion.after), channel_id=1, source_target_pairs={{0,16},{8,24},{16,0},{24,8},{1,17},{9,25},{17,1},{25,9},{2,18},{10... | collective-permute-start | bytes 12296 | tf_op jit(solution)/shard_map/ppermute | solution.py:376

commit v8 on v7

--- a/solution.py
+++ b/solution.py
@@ -177,7 +177,7 @@
     lax.fori_loop(0, count, step, face_average(prim, aux, 0, s, comps, first))
 
 
-def prepare_kernel(nx, ny, nz, xeven, rho, vel, p, q_ref, xa_ref, top_ref, sems):
+def prepare_kernel(nx, ny, nz, rho, vel, p, q_ref, top_ref, sems):
     n = nx * ny
     sources = (rho, vel.at[0], vel.at[1], vel.at[2], p)
     copies = [
@@ -198,11 +198,6 @@
         top = speed if top is None else jnp.maximum(top, speed)
     top = jnp.broadcast_to(jnp.max(top, keepdims=True), (8, nz))
     top_ref[...] = top
-    width = 3 * ny
-    start, _ = edge_starts(nx, ny, xeven)
-    for k in range(5):
-        xa_ref[k * width : (k + 1) * width, :] = q_ref[k, pl.ds(start, width), :]
-    xa_ref[5 * width : 5 * width + 8, :] = top
 
 
 def edge_starts(nx, ny, xeven):
@@ -213,7 +208,7 @@
     return pl.multiple_of((1 - odd) * high, 8), pl.multiple_of(odd * high, 8)
 
 
-def turn_kernel(nx, ny, nz, xeven, q_ref, after, qt_ref, xb_ref, y_ref, z_ref):
+def turn_kernel(nx, ny, nz, xeven, q_ref, after, qt_ref, xa_ref, xb_ref, y_ref, z_ref):
     n = nx * ny
     for k in range(5):
         qt_ref[k, 0:nz, :] = q_ref[k, 0:n, :].T
@@ -227,9 +222,10 @@
                 row = e + side * (ny - 3)
                 y_ref[side, at : at + nx, :] = q_ref[k, pl.ds(row, nx, stride=ny), :]
     width = 3 * ny
-    _, start = edge_starts(nx, ny, xeven)
-    for k in range(5):
-        xb_ref[k * width : (k + 1) * width, :] = q_ref[k, pl.ds(start, width), :]
+    start_a, start_b = edge_starts(nx, ny, xeven)
+    for k in range(5):
+        xa_ref[k * width : (k + 1) * width, :] = q_ref[k, pl.ds(start_a, width), :]
+        xb_ref[k * width : (k + 1) * width, :] = q_ref[k, pl.ds(start_b, width), :]
     z_ref[...] = jnp.zeros(z_ref.shape, f32)
     for k in range(5):
         z_ref[0, 3 * k : 3 * k + 3, :] = qt_ref[k, 0:3, :]
@@ -342,8 +338,9 @@
             out_ref[k, here, :] = tz_ref[k, here, :] + (fy[k, at + 1 : at + 1 + ny, :] - fy[k, at : at + ny, :])
 
 
-def final_kernel(nx, ny, split, q_ref, tx_ref, rest_ref, t_ref, top_ref, out_ref):
-    step = (cfl_number * KB) / top_ref[0:1, :]
+def final_kernel(nx, ny, split, q_ref, tx_ref, rest_ref, t_ref, top_ref, out_ref, held, sems):
+    step = (cfl_number * KB) / top_ref[7:8, :]
+    copies = []
     for x in range(nx):
         for lo, hi, part in ((0, split, tx_ref), (split, ny, rest_ref)):
             here = slice(x * ny + lo, x * ny + hi)
@@ -352,7 +349,11 @@
             m1, m2, m3 = rho * u1, rho * u2, rho * u3
             energy = 2.5 * p + 0.5 * (m1 * u1 + m2 * u2 + m3 * u3)
             for k, value in enumerate((rho, m1, m2, m3, energy)):
-                out_ref[k, x, lo:hi] = value - step * (part[k, there, :] + t_ref[k, here, :])
+                held[k, x, lo:hi] = value - step * (part[k, there, :] + t_ref[k, here, :])
+        copies.append(pltpu.make_async_copy(held.at[:, x], out_ref.at[:, x], sems.at[x]))
+        copies[-1].start()
+    for copy in copies:
+        copy.wait()
 
 
 VMEM = pl.BlockSpec(memory_space=pltpu.VMEM)
@@ -360,8 +361,10 @@
 ANY = pl.BlockSpec(memory_space=pl.ANY)
 
 
-def call(kernel, outs, flops, scratch=(), in_specs=None):
+def call(kernel, outs, flops, scratch=(), in_specs=None, out_specs=None):
     extra = {} if in_specs is None else {"in_specs": in_specs}
+    if out_specs is not None:
+        extra["out_specs"] = out_specs
     return pl.pallas_call(
         kernel,
         out_shape=outs,
@@ -400,12 +403,13 @@
 
 
 def with_top(edges, used, top):
-    row = lax.broadcasted_iota(jnp.int32, edges.shape, 0)
-    return jnp.where(row >= used, top[0:1], edges)
-
-
-def got_top(top, got, row):
-    return jnp.maximum(top, got[row : row + 1])
+    tiles = edges.reshape(-1, 8, edges.shape[1])
+    row = 8 * lax.broadcasted_iota(jnp.int32, tiles.shape, 0) + lax.broadcasted_iota(jnp.int32, tiles.shape, 1)
+    return jnp.where(row >= used, top[None], tiles).reshape(edges.shape)
+
+
+def got_top(top, got):
+    return jnp.maximum(top, got[got.shape[0] - 8 :])
 
 
 def edge_trade(axis, low, high, used, top, mids=None):
@@ -415,19 +419,19 @@
         return high, low, top
     if n == 2:
         got = permute(with_top(jnp.concatenate([low, high]), size + used, top), axis, [(0, 1), (1, 0)])
-        return got[size:], got[:size], got_top(top, got, size + used)
+        return got[size:], got[:size], got_top(top, got)
     if n % 2:
         lower = permute(high, axis, [(i, (i + 1) % n) for i in range(n)])
         upper = permute(low, axis, [((i + 1) % n, i) for i in range(n)])
         return lower, upper, lax.pmax(top, axis)
     odd = lax.rem(lax.axis_index(axis), 2) == 1
     got_a = permute(with_top(jnp.where(odd, low, high), used, top), axis, pairs_a(n))
-    top = got_top(top, got_a, used)
+    top = got_top(top, got_a)
     if mids is not None:
         mids.append(top)
     got_b = permute(with_top(jnp.where(odd, high, low), used, top), axis, pairs_b(n))
     if n == 4:
-        top = got_top(top, got_b, used)
+        top = got_top(top, got_b)
     else:
         top = top_over(top, axis, 2)
     lower = jnp.where(odd, got_a, got_b)
@@ -446,17 +450,18 @@
         pltpu.with_memory_space_constraint(a, pltpu.HBM)
         for a in (density.reshape(n, nz), velocity.reshape(3, n, nz), pressure.reshape(n, nz))
     )
-    q, xa, top = call(
-        functools.partial(prepare_kernel, nx, ny, nz, xeven),
-        (S((5, n + 16, nz), f32), S((width + 8, nz), f32), S((8, nz), f32)),
+    q, top = call(
+        functools.partial(prepare_kernel, nx, ny, nz),
+        (S((5, n + 16, nz), f32), S((8, nz), f32)),
         2000000,
         [pltpu.SemaphoreType.DMA((5,))],
         [HBM] * 3,
     )(density, velocity, pressure)
-    qt, xb, ye, ze = call(
+    qt, xa, xb, ye, ze = call(
         functools.partial(turn_kernel, nx, ny, nz, xeven),
         (
             S((5, nz + 16, n), f32),
+            S((width, nz), f32),
             S((width, nz), f32),
             S((2, rup(15 * nx + 1, 8), nz), f32),
             S((2, 16, n), f32),
@@ -480,21 +485,20 @@
     if xeven:
         got_b = permute(xb, "gx", pairs_b(gx))
         got_a = permute(xa, "gx", pairs_a(gx))
-        top = jnp.maximum(top, got_a[width:])
+        top = jnp.maximum(top, permute(top, "gx", pairs_a(gx)))
     else:
         got_a = permute(xa, "gx", [(i, (i + 1) % gx) for i in range(gx)])
         got_b = permute(xb, "gx", [((i + 1) % gx, i) for i in range(gx)])
-    ztop = top if n == nz else jnp.full((8, n), jnp.max(top))
+    ztop = top if n == nz else jnp.full((8, n), jnp.max(top[7]))
     zt = nz // 8
-    half = zt // 2
+    half = max(zt * 7 // 16, 1)
     fz = [
         inner(qt, 0, half, 1, n, nz, 0, (2, 0, 1), 8 * half + 8, ye),
         inner(qt, half, zt - half, 0, n, nz, 0, (2, 0, 1), 8 * (zt - half) + 8, ztop),
     ]
     zlo, zhi, ztop = edge_trade("gz", ze[0], ze[1], 15, ztop)
-    top = ztop if n == nz else jnp.full((8, nz), jnp.max(ztop))
+    top = ztop if n == nz else jnp.full((8, nz), jnp.max(ztop[7]))
     block = rup(ny + 6, 8)
-    ytop = top
     fy = inner(q, 0, n // 8, 0, nz, ny, block, (1, 0, 2), nx * block + 16, top)
     mids = []
     ylo, yhi, top = edge_trade("gy", ye[0], ye[1], 15 * nx, top, mids)
@@ -517,7 +521,7 @@
         sweep_flops // 4,
         fields(5, 10, 4, 25, 5, r=64, w=n) + [pltpu.VMEM((5, nz + 16, n), f32)],
         [VMEM] * 5 + [ANY],
-    )(qt, zlo, zhi, *fz, ytop)
+    )(qt, zlo, zhi, *fz, mids[0] if mids else top)
     t = call(
         functools.partial(y_ends_kernel, nx, ny, block),
         S((5, n, nz), f32),
@@ -526,9 +530,15 @@
         [VMEM] * 5 + [ANY],
     )(q, ylo, yhi, fy, tz, top)
     top = top_over(top, "gx", 2 if xeven else 1)
-    return call(functools.partial(final_kernel, nx, ny, split), S((5, nx, ny, nz), f32), 1000000)(
-        q, tx, tx_rest, t, top
-    )
+    out = S((5, nx, ny, nz), f32)
+    return call(
+        functools.partial(final_kernel, nx, ny, split),
+        out,
+        1000000,
+        [pltpu.VMEM(out.shape, f32), pltpu.SemaphoreType.DMA((nx,))],
+        [VMEM] * 5,
+        HBM,
+    )(q, tx, tx_rest, t, top)
 
 
 def solution(mesh):

time: 24.3 us -> 26.3 us (1.082)
  waiting for transfers between devices: 2.72 us -> 5.34 us
  starting transfers between devices: 11.1 us -> 10.2 us
    ppermute x6 -> x7, waiting for transfers between devices: 2.72 us -> 5.34 us  [permute(): return lax.ppermute(value, axis, pairs)]
    ppermute x6 -> x7, starting transfers between devices: 11.1 us -> 10.2 us  [permute(): return lax.ppermute(value, axis, pairs)]
  transfers between devices with their start and end apart: 6 -> 7, of which waited for: 2 -> 4; matrix products, arithmetic and copies ran while one was open for 0% -> 2% of each run, Pallas kernels for 33% -> 20%
where the time goes in v8:
time: 26.3 us; the launch traced here: 26.1 us
  starting transfers between devices  10.2 us (39%)
  Pallas kernels  9.95 us (38%)
  waiting for transfers between devices  5.34 us (20%)
  other arithmetic  0.41 us (2%)
    ppermute x7, starting transfers between devices, permute(): return lax.ppermute(value, axis, pairs)  10.2 us
    ppermute x7, waiting for transfers between devices, permute(): return lax.ppermute(value, axis, pairs)  5.34 us
    pallas_call x3, Pallas kernels, inner(): call(functools.partial(inner_kernel, first, count, more, length, block, c...  3.94 us
    pallas_call x2, Pallas kernels, along_x(): call(functools.partial(x_kernel, nx, ny, first, ys, xeven), S((5, nx * ys...  2.87 us
    pallas_call x1, Pallas kernels, local(): call(functools.partial(prepare_kernel, nx, ny, nz), (S((5, n + 16, nz), f...  1.17 us
    pallas_call x1, Pallas kernels, local(): call(functools.partial(final_kernel, nx, ny, split), out, 1000000, [pltpu...  0.79 us
    pallas_call x1, Pallas kernels, local(): call(functools.partial(y_ends_kernel, nx, ny, block), S((5, n, nz), f32),...  0.62 us
  transfers between devices with their start and end apart: 7, of which 4 were waited for; matrix products, arithmetic and copies ran while one was open for 2% of the time, Pallas kernels for 20%

profile of v8, /device:TPU:0, one launch (start us, length us, event | category | flops | bytes accessed | tf_op | source)
XLA Modules:
  0.0 26.1 jit_solution(17719020739770135138)
XLA Ops:
  0.0 1.2 %shard_map.37 = (f32[5,144,128]{2,1,0:T(8,128)S(1)}, f32[8,128]{1,0:T(8,128)S(1)}) custom-call(f32[128,128]{1,0:T(8,128)} %bitcast.18, f32[3,128,128]{2,1,0:T(8,128)} %bitcast.17, f32[128,128]{1,0:T(8,128)} %bitcast.19), custom_call_target="tpu_custom_call" | custom-call | flops 2000000 | bytes 1000000 | tf_op jit(solution)/shard_map/pallas_call | solution.py:453
  1.2 0.6 %collective-permute-start.2 = (f32[8,128]{1,0:T(8,128)S(1)}, f32[8,128]{1,0:T(8,128)S(1)}, u32[]{:S(2)}, u32[]{:S(2)}) collective-permute-start(f32[8,128]{1,0:T(8,128)S(1)} %get-tuple-element.13.after), channel_id=1, source_target_pairs={{0,8},{8,0},{16,24},{24,16},{1,9},{9,1},{17,25},{25,17},{2,10},{10... | collective-permute-start | bytes 12296 | tf_op jit(solution)/shard_map/ppermute | solution.py:379
  1.7 0.1 add_compare_fusion.1
  1.8 0.2 shard_map.38
  2.0 0.1 ge.28
  2.1 0.5 %collective-permute-done.2 = f32[8,128]{1,0:T(8,128)S(1)} collective-permute-done((f32[8,128]{1,0:T(8,128)S(1)}, f32[8,128]{1,0:T(8,128)S(1)}, u32[]{:S(2)}, u32[]{:S(2)}) %collective-permute-start.2) | collective-permute-done | bytes 4128 | tf_op jit(solution)/shard_map/ppermute | solution.py:379
  2.6 0.1 maximum_select_fusion
  2.6 2.8 %collective-permute-start.3 = (f32[32,128]{1,0:T(8,128)S(1)}, f32[32,128]{1,0:T(8,128)S(1)}, u32[]{:S(2)}, u32[]{:S(2)}) collective-permute-start(f32[32,128]{1,0:T(8,128)S(1)} %maximum_select_fusion), channel_id=1, source_target_pairs={{0,1},{1,0},{2,3},{3,2},{4,5},{5,4},{6,7},{7,6},{8,9},{9,8},{10,11... | collective-permute-start | bytes 49160 | tf_op jit(solution)/shard_map/ppermute | solution.py:379
  5.5 0.1 add_compare_fusion
  5.6 0.1 ge.30
  5.7 1.6 %collective-permute-done.3 = f32[32,128]{1,0:T(8,128)S(1)} collective-permute-done((f32[32,128]{1,0:T(8,128)S(1)}, f32[32,128]{1,0:T(8,128)S(1)}, u32[]{:S(2)}, u32[]{:S(2)}) %collective-permute-start.3) | collective-permute-done | bytes 16416 | tf_op jit(solution)/shard_map/ppermute | solution.py:379
  7.2 0.1 bitcast_select_fusion.1
  7.3 2.1 %collective-permute-start.4 = (f32[64,128]{1,0:T(8,128)S(1)}, f32[64,128]{1,0:T(8,128)S(1)}, u32[]{:S(2)}, u32[]{:S(2)}) collective-permute-start(f32[64,128]{1,0:T(8,128)S(1)} %bitcast_select_fusion.1), channel_id=1, source_target_pairs={{0,2},{2,0},{4,6},{6,4},{1,3},{3,1},{5,7},{7,5},{8,10},{10,8},{12,... | collective-permute-start | bytes 98312 | tf_op jit(solution)/shard_map/ppermute | solution.py:379
  9.4 0.0 collective-permute-start
  9.4 1.6 %collective-permute-start.1 = (f32[480,128]{1,0:T(8,128)S(1)}, f32[480,128]{1,0:T(8,128)S(1)}, u32[]{:S(2)}, u32[]{:S(2)}) collective-permute-start(f32[480,128]{1,0:T(8,128)S(1)} %get-tuple-element.15), channel_id=1, source_target_pairs={{0,24},{8,16},{16,8},{24,0},{1,25},{9,17},{17,9},{25,1},{2,26},{10... | collective-permute-start | bytes 737288 | tf_op jit(solution)/shard_map/ppermute | solution.py:379
  11.0 0.9 %shard_map.42.fz_ref = f32[5,64,128]{2,1,0:T(8,128)S(1)} custom-call(f32[5,144,128]{2,1,0:T(8,128)S(1)} %get-tuple-element.18.q_ref.qt_ref, f32[2,64,128]{2,1,0:T(8,128)S(1)} %get-tuple-element.17.after), custom_call_target="tpu_custom_call" | custom-call | flops 16000000 | bytes 1000000 | tf_op jit(solution)/shard_map/pallas_call | solution.py:477
  11.9 1.1 %shard_map.43.fz2_ref = f32[5,80,128]{2,1,0:T(8,128)S(1)} custom-call(f32[5,144,128]{2,1,0:T(8,128)S(1)} %get-tuple-element.18.q_ref.qt_ref, f32[8,128]{1,0:T(8,128)S(1)} %max.15.after), custom_call_target="tpu_custom_call" | custom-call | flops 16000000 | bytes 1000000 | tf_op jit(solution)/shard_map/pallas_call | solution.py:477
  13.0 0.0 collective-permute-done.4
  13.0 0.1 bitcast_select_fusion
  13.1 2.5 %collective-permute-start.5 = (f32[64,128]{1,0:T(8,128)S(1)}, f32[64,128]{1,0:T(8,128)S(1)}, u32[]{:S(2)}, u32[]{:S(2)}) collective-permute-start(f32[64,128]{1,0:T(8,128)S(1)} %bitcast_select_fusion), channel_id=1, source_target_pairs={{0,6},{2,4},{4,2},{6,0},{1,7},{3,5},{5,3},{7,1},{8,14},{10,12},{12... | collective-permute-start | bytes 98312 | tf_op jit(solution)/shard_map/ppermute | solution.py:379
  15.6 2.0 %shard_map.41.fy_ref = f32[5,176,128]{2,1,0:T(8,128)S(1)} custom-call(f32[5,144,128]{2,1,0:T(8,128)S(1)} %get-tuple-element.12.q_ref, f32[8,128]{1,0:T(8,128)S(1)} %slice_maximum_fusion.2.after), custom_call_target="tpu_custom_call" | custom-call | flops 16000000 | bytes 1000000 | tf_op jit(solution)/shard_map/pallas_call | solution.py:477
  17.6 0.4 %shard_map.44.tz_ref = f32[5,128,128]{2,1,0:T(8,128)S(1)} custom-call(f32[5,144,128]{2,1,0:T(8,128)S(1)} %get-tuple-element.18.q_ref.qt_ref, f32[16,128]{1,0:T(8,128)S(1)} %get-tuple-element.22.lo, f32[16,128]{1,0:T(8,128)S(1)} %get-tuple-element.21.hi, f32[5,64,128]{2,1,0:T(8,128)S(1)} %shard_map.42.fz_ref, f32[5,80,128]{2,1,0:T(8,128)S(1)} %shard_map.43.fz2_ref, ...), custom_call_target="tpu_custom_call" | custom-call | flops 4000000 | bytes 1000000 | tf_op jit(solution)/shard_map/pallas_call | solution.py:518
  18.0 0.9 %collective-permute-done.5 = f32[64,128]{1,0:T(8,128)S(1)} collective-permute-done((f32[64,128]{1,0:T(8,128)S(1)}, f32[64,128]{1,0:T(8,128)S(1)}, u32[]{:S(2)}, u32[]{:S(2)}) %collective-permute-start.5) | collective-permute-done | bytes 32800 | tf_op jit(solution)/shard_map/ppermute | solution.py:379
  18.9 0.5 %collective-permute-start.6 = (f32[8,128]{1,0:T(8,128)S(1)}, f32[8,128]{1,0:T(8,128)S(1)}, u32[]{:S(2)}, u32[]{:S(2)}) collective-permute-start(f32[8,128]{1,0:T(8,128)S(1)} %slice_maximum_fusion.after), channel_id=1, source_target_pairs={{0,16},{8,24},{16,0},{24,8},{1,17},{9,25},{17,1},{25,9},{2,18},{10... | collective-permute-start | bytes 12296 | tf_op jit(solution)/shard_map/ppermute | solution.py:379
  19.4 0.6 %shard_map.45.t_ref = f32[5,128,128]{2,1,0:T(8,128)S(1)} custom-call(f32[5,144,128]{2,1,0:T(8,128)S(1)} %get-tuple-element.12.q_ref, f32[64,128]{1,0:T(8,128)S(1)} %get-tuple-element.20.lo, f32[64,128]{1,0:T(8,128)S(1)} %get-tuple-element.19.hi, f32[5,176,128]{2,1,0:T(8,128)S(1)} %shard_map.41.fy_ref, f32[5,128,128]{2,1,0:T(8,128)S(1)} %shard_map.44.tz_ref, ...), custom_call_target="tpu_custom_call" | custom-call | flops 4000000 | bytes 1000000 | tf_op jit(solution)/shard_map/pallas_call | solution.py:525
  20.0 2.4 %collective-permute-done.6 = f32[8,128]{1,0:T(8,128)S(1)} collective-permute-done((f32[8,128]{1,0:T(8,128)S(1)}, f32[8,128]{1,0:T(8,128)S(1)}, u32[]{:S(2)}, u32[]{:S(2)}) %collective-permute-start.6) | collective-permute-done | bytes 4128 | tf_op jit(solution)/shard_map/ppermute | solution.py:379
  22.5 0.0 collective-permute-done.a_ref
  22.5 0.0 collective-permute-done.1.b_ref
  22.5 1.4 %shard_map.39.tx_ref = f32[5,64,128]{2,1,0:T(8,128)S(1)} custom-call(f32[5,144,128]{2,1,0:T(8,128)S(1)} %get-tuple-element.12.q_ref, f32[480,128]{1,0:T(8,128)S(1)} %collective-permute-done.a_ref, f32[480,128]{1,0:T(8,128)S(1)} %collective-permute-done.1.b_ref, f32[8,128]{1,0:T(8,128)S(1)} %slice_maximum_fusion.1.after), custom_call_target="tpu_custom_call" | custom-call | flops 16000000 | bytes 1000000 | tf_op jit(solution)/shard_map/pallas_call | solution.py:507
  23.9 1.4 %shard_map.40.rest_ref = f32[5,64,128]{2,1,0:T(8,128)S(1)} custom-call(f32[5,144,128]{2,1,0:T(8,128)S(1)} %get-tuple-element.12.q_ref, f32[480,128]{1,0:T(8,128)S(1)} %collective-permute-done.a_ref, f32[480,128]{1,0:T(8,128)S(1)} %collective-permute-done.1.b_ref, f32[8,128]{1,0:T(8,128)S(1)} %slice_maximum_fusion.after), custom_call_target="tpu_custom_call" | custom-call | flops 16000000 | bytes 1000000 | tf_op jit(solution)/shard_map/pallas_call | solution.py:507
  25.4 0.8 %shard_map.46 = f32[5,4,32,128]{3,2,1,0:T(8,128)} custom-call(f32[5,144,128]{2,1,0:T(8,128)S(1)} %get-tuple-element.12.q_ref, f32[5,64,128]{2,1,0:T(8,128)S(1)} %shard_map.39.tx_ref, f32[5,64,128]{2,1,0:T(8,128)S(1)} %shard_map.40.rest_ref, f32[5,128,128]{2,1,0:T(8,128)S(1)} %shard_map.45.t_ref, f32[8,128]{1,0:T(8,128)S(1)} %max.19.top_ref), custom_call_target="tpu_custom_call" | custom-call | flops 1000000 | bytes 1000000 | tf_op jit(solution)/shard_map/pallas_call | solution.py:534
  (10 shorter events, 0.0 us)
Async XLA Ops:
  1.2 1.4 %collective-permute-start.2 = (f32[8,128]{1,0:T(8,128)S(1)}, f32[8,128]{1,0:T(8,128)S(1)}, u32[]{:S(2)}, u32[]{:S(2)}) collective-permute-start(f32[8,128]{1,0:T(8,128)S(1)} %get-tuple-element.13.after), channel_id=1, source_target_pairs={{0,8},{8,0},{16,24},{24,16},{1,9},{9,1},{17,25},{25,17},{2,10},{10... | collective-permute-start | bytes 12296 | tf_op jit(solution)/shard_map/ppermute | solution.py:379
  2.6 4.6 %collective-permute-start.3 = (f32[32,128]{1,0:T(8,128)S(1)}, f32[32,128]{1,0:T(8,128)S(1)}, u32[]{:S(2)}, u32[]{:S(2)}) collective-permute-start(f32[32,128]{1,0:T(8,128)S(1)} %maximum_select_fusion), channel_id=1, source_target_pairs={{0,1},{1,0},{2,3},{3,2},{4,5},{5,4},{6,7},{7,6},{8,9},{9,8},{10,11... | collective-permute-start | bytes 49160 | tf_op jit(solution)/shard_map/ppermute | solution.py:379
  7.3 5.7 %collective-permute-start.4 = (f32[64,128]{1,0:T(8,128)S(1)}, f32[64,128]{1,0:T(8,128)S(1)}, u32[]{:S(2)}, u32[]{:S(2)}) collective-permute-start(f32[64,128]{1,0:T(8,128)S(1)} %bitcast_select_fusion.1), channel_id=1, source_target_pairs={{0,2},{2,0},{4,6},{6,4},{1,3},{3,1},{5,7},{7,5},{8,10},{10,8},{12,... | collective-permute-start | bytes 98312 | tf_op jit(solution)/shard_map/ppermute | solution.py:379
  9.4 13.1 %collective-permute-start = (f32[480,128]{1,0:T(8,128)S(1)}, f32[480,128]{1,0:T(8,128)S(1)}, u32[]{:S(2)}, u32[]{:S(2)}) collective-permute-start(f32[480,128]{1,0:T(8,128)S(1)} %get-tuple-element.14), channel_id=1, source_target_pairs={{0,8},{8,0},{16,24},{24,16},{1,9},{9,1},{17,25},{25,17},{2,10},{10... | collective-permute-start | bytes 737288 | tf_op jit(solution)/shard_map/ppermute | solution.py:379
  9.4 13.1 %collective-permute-start.1 = (f32[480,128]{1,0:T(8,128)S(1)}, f32[480,128]{1,0:T(8,128)S(1)}, u32[]{:S(2)}, u32[]{:S(2)}) collective-permute-start(f32[480,128]{1,0:T(8,128)S(1)} %get-tuple-element.15), channel_id=1, source_target_pairs={{0,24},{8,16},{16,8},{24,0},{1,25},{9,17},{17,9},{25,1},{2,26},{10... | collective-permute-start | bytes 737288 | tf_op jit(solution)/shard_map/ppermute | solution.py:379
  13.1 5.8 %collective-permute-start.5 = (f32[64,128]{1,0:T(8,128)S(1)}, f32[64,128]{1,0:T(8,128)S(1)}, u32[]{:S(2)}, u32[]{:S(2)}) collective-permute-start(f32[64,128]{1,0:T(8,128)S(1)} %bitcast_select_fusion), channel_id=1, source_target_pairs={{0,6},{2,4},{4,2},{6,0},{1,7},{3,5},{5,3},{7,1},{8,14},{10,12},{12... | collective-permute-start | bytes 98312 | tf_op jit(solution)/shard_map/ppermute | solution.py:379
  18.9 3.6 %collective-permute-start.6 = (f32[8,128]{1,0:T(8,128)S(1)}, f32[8,128]{1,0:T(8,128)S(1)}, u32[]{:S(2)}, u32[]{:S(2)}) collective-permute-start(f32[8,128]{1,0:T(8,128)S(1)} %slice_maximum_fusion.after), channel_id=1, source_target_pairs={{0,16},{8,24},{16,0},{24,8},{1,17},{9,25},{17,1},{25,9},{2,18},{10... | collective-permute-start | bytes 12296 | tf_op jit(solution)/shard_map/ppermute | solution.py:379

commit v9 on v8

--- a/solution.py
+++ b/solution.py
@@ -208,28 +208,37 @@
     return pl.multiple_of((1 - odd) * high, 8), pl.multiple_of(odd * high, 8)
 
 
-def turn_kernel(nx, ny, nz, xeven, q_ref, after, qt_ref, xa_ref, xb_ref, y_ref, z_ref):
+def slots(axis):
+    n = lax.axis_size(axis)
+    if n % 2 or n < 4:
+        return 0, 1
+    odd = lax.rem(lax.axis_index(axis), 2)
+    return 1 - odd, odd
+
+
+def turn_kernel(nx, ny, nz, xeven, q_ref, after, qt_ref, xa_ref, xb_ref, y_ref, z_ref, free_ref):
     n = nx * ny
     for k in range(5):
         qt_ref[k, 0:nz, :] = q_ref[k, 0:n, :].T
-    pad = y_ref.shape[1] - 15 * nx
-    for side in (0, 1):
-        if pad:
-            y_ref[side, 15 * nx :, :] = jnp.zeros((pad, nz), f32)
+    size = y_ref.shape[1]
+    for slot, side in zip(slots("gy"), (0, 1)):
+        y_ref[slot, size - 8 :, :] = jnp.zeros((8, nz), f32)
         for k in range(5):
             for e in range(3):
                 at = (3 * k + e) * nx
                 row = e + side * (ny - 3)
-                y_ref[side, at : at + nx, :] = q_ref[k, pl.ds(row, nx, stride=ny), :]
+                y_ref[slot, at : at + nx, :] = q_ref[k, pl.ds(row, nx, stride=ny), :]
     width = 3 * ny
     start_a, start_b = edge_starts(nx, ny, xeven)
     for k in range(5):
         xa_ref[k * width : (k + 1) * width, :] = q_ref[k, pl.ds(start_a, width), :]
         xb_ref[k * width : (k + 1) * width, :] = q_ref[k, pl.ds(start_b, width), :]
-    z_ref[...] = jnp.zeros(z_ref.shape, f32)
-    for k in range(5):
-        z_ref[0, 3 * k : 3 * k + 3, :] = qt_ref[k, 0:3, :]
-        z_ref[1, 3 * k : 3 * k + 3, :] = qt_ref[k, nz - 3 : nz, :]
+    for slot, at in zip(slots("gz"), (0, nz - 3)):
+        z_ref[slot, 8:16, :] = jnp.zeros((8, n), f32)
+        for k in range(5):
+            z_ref[slot, 3 * k : 3 * k + 3, :] = qt_ref[k, at : at + 3, :]
+    row = lax.broadcasted_iota(jnp.int32, free_ref.shape, 0)
+    free_ref[...] = jnp.where(row == 7, 1.0, 0.0).astype(f32)
 
 
 def x_kernel(nx, ny, first, ys, xeven, q_ref, a_ref, b_ref, after, out_ref, prim, uf, aux, cx, flux):
@@ -295,10 +304,19 @@
     cell_pass(prim, uf, aux, 6, comps)
     diff_pass(uf, aux, cx, 4, 5, 8)
     face_pass(prim, aux, cx, 1, 8, comps, put)
-    part = fz_ref.shape[1] - 8
-    for k in range(5):
-        fz[k, 3 : part + 3, :] = fz_ref[k, 3 : part + 3, :]
-        fz[k, part + 3 : nz + 3, :] = fz2_ref[k, 3 : nz - part + 3, :]
+    a = fz_ref.shape[1] - 8
+    b = a + fz2_ref.shape[1] - 8
+    count = (nz - b) // 8
+
+    def put_inner(k, i, value):
+        fz[k, rows(i + b // 8, 3), :] = value
+
+    cell_pass(qt_ref, uf, aux, count, comps, b // 8)
+    diff_pass(uf, aux, cx, count, count, 1)
+    face_pass(qt_ref, aux, cx, count, 1, comps, put_inner, b // 8)
+    for k in range(5):
+        fz[k, 3 : a + 3, :] = fz_ref[k, 3 : a + 3, :]
+        fz[k, a + 3 : b + 3, :] = fz2_ref[k, 3 : b - a + 3, :]
         fz[k, 0:3, :] = flux[k, 0:3, :]
         fz[k, nz - 2 : nz + 1, :] = flux[k, 3:6, :]
         out_ref[k] = (fz[k, 1 : nz + 1, :] - fz[k, 0:nz, :]).T
@@ -375,10 +393,6 @@
     )
 
 
-def permute(value, axis, pairs):
-    return lax.ppermute(value, axis, pairs)
-
-
 def fields(*counts, r, w):
     return [pltpu.VMEM((count, r, w), f32) for count in counts]
 
@@ -397,39 +411,39 @@
         return lax.pmax(top, axis)
     d = first
     while d < n:
-        top = jnp.maximum(top, permute(top, axis, [(i, i ^ d) for i in range(n)]))
+        top = jnp.maximum(top, lax.ppermute(top, axis, [(i, i ^ d) for i in range(n)]))
         d *= 2
     return top
 
 
-def with_top(edges, used, top):
-    tiles = edges.reshape(-1, 8, edges.shape[1])
-    row = 8 * lax.broadcasted_iota(jnp.int32, tiles.shape, 0) + lax.broadcasted_iota(jnp.int32, tiles.shape, 1)
-    return jnp.where(row >= used, top[None], tiles).reshape(edges.shape)
+def with_top(edges, free, top):
+    at = edges.shape[0] - 8
+    return jnp.concatenate([edges[:at], edges[at:] + free * top])
 
 
 def got_top(top, got):
     return jnp.maximum(top, got[got.shape[0] - 8 :])
 
 
-def edge_trade(axis, low, high, used, top, mids=None):
+def edge_trade(axis, edges, free, top, mids=None):
     n = lax.axis_size(axis)
-    size = low.shape[0]
+    first, second = edges[0], edges[1]
+    size = first.shape[0]
     if n == 1:
-        return high, low, top
+        return second, first, top
     if n == 2:
-        got = permute(with_top(jnp.concatenate([low, high]), size + used, top), axis, [(0, 1), (1, 0)])
+        got = lax.ppermute(with_top(edges.reshape(2 * size, -1), free, top), axis, [(0, 1), (1, 0)])
         return got[size:], got[:size], got_top(top, got)
     if n % 2:
-        lower = permute(high, axis, [(i, (i + 1) % n) for i in range(n)])
-        upper = permute(low, axis, [((i + 1) % n, i) for i in range(n)])
+        lower = lax.ppermute(second, axis, [(i, (i + 1) % n) for i in range(n)])
+        upper = lax.ppermute(first, axis, [((i + 1) % n, i) for i in range(n)])
         return lower, upper, lax.pmax(top, axis)
     odd = lax.rem(lax.axis_index(axis), 2) == 1
-    got_a = permute(with_top(jnp.where(odd, low, high), used, top), axis, pairs_a(n))
+    got_a = lax.ppermute(with_top(first, free, top), axis, pairs_a(n))
     top = got_top(top, got_a)
     if mids is not None:
         mids.append(top)
-    got_b = permute(with_top(jnp.where(odd, high, low), used, top), axis, pairs_b(n))
+    got_b = lax.ppermute(with_top(second, free, top), axis, pairs_b(n))
     if n == 4:
         top = got_top(top, got_b)
     else:
@@ -457,7 +471,7 @@
         [pltpu.SemaphoreType.DMA((5,))],
         [HBM] * 3,
     )(density, velocity, pressure)
-    qt, xa, xb, ye, ze = call(
+    qt, xa, xb, ye, ze, free = call(
         functools.partial(turn_kernel, nx, ny, nz, xeven),
         (
             S((5, nz + 16, n), f32),
@@ -465,6 +479,7 @@
             S((width, nz), f32),
             S((2, rup(15 * nx + 1, 8), nz), f32),
             S((2, 16, n), f32),
+            S((8, nz), f32),
         ),
         2000000,
         (),
@@ -483,25 +498,25 @@
         )(source, after)
 
     if xeven:
-        got_b = permute(xb, "gx", pairs_b(gx))
-        got_a = permute(xa, "gx", pairs_a(gx))
-        top = jnp.maximum(top, permute(top, "gx", pairs_a(gx)))
+        got_b = lax.ppermute(xb, "gx", pairs_b(gx))
+        got_a = lax.ppermute(xa, "gx", pairs_a(gx))
+        top = jnp.maximum(top, lax.ppermute(top, "gx", pairs_a(gx)))
     else:
-        got_a = permute(xa, "gx", [(i, (i + 1) % gx) for i in range(gx)])
-        got_b = permute(xb, "gx", [((i + 1) % gx, i) for i in range(gx)])
+        got_a = lax.ppermute(xa, "gx", [(i, (i + 1) % gx) for i in range(gx)])
+        got_b = lax.ppermute(xb, "gx", [((i + 1) % gx, i) for i in range(gx)])
     ztop = top if n == nz else jnp.full((8, n), jnp.max(top[7]))
     zt = nz // 8
-    half = max(zt * 7 // 16, 1)
+    za, zb = zt * 7 // 16, zt * 6 // 16
     fz = [
-        inner(qt, 0, half, 1, n, nz, 0, (2, 0, 1), 8 * half + 8, ye),
-        inner(qt, half, zt - half, 0, n, nz, 0, (2, 0, 1), 8 * (zt - half) + 8, ztop),
+        inner(qt, 0, za, 1, n, nz, 0, (2, 0, 1), 8 * za + 8, ye),
+        inner(qt, za, zb, 1, n, nz, 0, (2, 0, 1), 8 * zb + 8, ztop),
     ]
-    zlo, zhi, ztop = edge_trade("gz", ze[0], ze[1], 15, ztop)
+    zlo, zhi, ztop = edge_trade("gz", ze, free if n == nz else jnp.broadcast_to(free[:, :1], (8, n)), ztop)
     top = ztop if n == nz else jnp.full((8, nz), jnp.max(ztop[7]))
     block = rup(ny + 6, 8)
     fy = inner(q, 0, n // 8, 0, nz, ny, block, (1, 0, 2), nx * block + 16, top)
     mids = []
-    ylo, yhi, top = edge_trade("gy", ye[0], ye[1], 15 * nx, top, mids)
+    ylo, yhi, top = edge_trade("gy", ye, free, top, mids)
 
     def along_x(first, ys, after):
         return call(

time: 26.3 us -> 25.8 us (0.981)
  waiting for transfers between devices: 5.34 us -> 4.33 us
  starting transfers between devices: 10.2 us -> 11.2 us
  other arithmetic: 0.41 us -> 0.05 us
    ppermute x7, waiting for transfers between devices: 5.34 us -> 4.33 us  [the longest x1 1.71 us: edge_trade(): lax.ppermute(with_top(edges.reshape(2 * size, -1), free, top), axis, [(0,...]
    ppermute x7, starting transfers between devices: 10.2 us -> 11.2 us  [the longest x1 2.85 us: edge_trade(): lax.ppermute(with_top(edges.reshape(2 * size, -1), free, top), axis, [(0,...]
    pallas_call x1, Pallas kernels: 0.39 us -> 0.8 us  [local(): call(functools.partial(z_ends_kernel, nz), S((5, n, nz), f32), sweep_flop...]
    pallas_call x3, Pallas kernels: 3.94 us -> 3.59 us  [inner(): call(functools.partial(inner_kernel, first, count, more, length, block, c...]
  transfers between devices with their start and end apart: 7 -> 7, of which waited for: 4 -> 4; matrix products, arithmetic and copies ran while one was open for 2% -> 0% of each run, Pallas kernels for 20% -> 20%
where the time goes in v9:
time: 25.8 us; the launch traced here: 25.6 us
  starting transfers between devices  11.2 us (43%)
  Pallas kernels  10 us (39%)
  waiting for transfers between devices  4.33 us (17%)
    pallas_call x3, Pallas kernels, inner(): call(functools.partial(inner_kernel, first, count, more, length, block, c...  3.59 us
    pallas_call x2, Pallas kernels, along_x(): call(functools.partial(x_kernel, nx, ny, first, ys, xeven), S((5, nx * ys...  2.87 us
    ppermute x1, starting transfers between devices, edge_trade(): lax.ppermute(with_top(edges.reshape(2 * size, -1), free, top), axis, [(0,...  2.85 us
    ppermute x1, starting transfers between devices, edge_trade(): got_b = lax.ppermute(with_top(second, free, top), axis, pairs_b(n))  2.72 us
    ppermute x1, starting transfers between devices, edge_trade(): got_a = lax.ppermute(with_top(first, free, top), axis, pairs_a(n))  2.13 us
    ppermute x1, waiting for transfers between devices, edge_trade(): lax.ppermute(with_top(edges.reshape(2 * size, -1), free, top), axis, [(0,...  1.71 us
    ppermute x1, waiting for transfers between devices, top_over(): lax.ppermute(top, axis, [(i, i ^ d) for i in range(n)])  1.68 us
    ppermute x1, starting transfers between devices, local(): got_b = lax.ppermute(xb, 'gx', pairs_b(gx))  1.6 us
  transfers between devices with their start and end apart: 7, of which 4 were waited for; matrix products, arithmetic and copies ran while one was open for 0% of the time, Pallas kernels for 20%

profile of v9, /device:TPU:0, one launch (start us, length us, event | category | flops | bytes accessed | tf_op | source)
XLA Modules:
  0.0 25.6 jit_solution(15081611287908088596)
XLA Ops:
  0.0 1.2 %shard_map.37 = (f32[5,144,128]{2,1,0:T(8,128)S(1)}, f32[8,128]{1,0:T(8,128)S(1)}) custom-call(f32[128,128]{1,0:T(8,128)} %bitcast.15, f32[3,128,128]{2,1,0:T(8,128)} %bitcast.14, f32[128,128]{1,0:T(8,128)} %bitcast.16), custom_call_target="tpu_custom_call" | custom-call | flops 2000000 | bytes 1000000 | tf_op jit(solution)/shard_map/pallas_call | solution.py:467
  1.2 0.6 %collective-permute-start.2 = (f32[8,128]{1,0:T(8,128)S(1)}, f32[8,128]{1,0:T(8,128)S(1)}, u32[]{:S(2)}, u32[]{:S(2)}) collective-permute-start(f32[8,128]{1,0:T(8,128)S(1)} %get-tuple-element.14.after), channel_id=1, source_target_pairs={{0,8},{8,0},{16,24},{24,16},{1,9},{9,1},{17,25},{25,17},{2,10},{10... | collective-permute-start | bytes 12296 | tf_op jit(solution)/shard_map/ppermute | solution.py:503
  1.7 0.2 shard_map.38
  1.9 0.6 %collective-permute-done.2 = f32[8,128]{1,0:T(8,128)S(1)} collective-permute-done((f32[8,128]{1,0:T(8,128)S(1)}, f32[8,128]{1,0:T(8,128)S(1)}, u32[]{:S(2)}, u32[]{:S(2)}) %collective-permute-start.2) | collective-permute-done | bytes 4128 | tf_op jit(solution)/shard_map/ppermute | solution.py:503
  2.6 2.8 %collective-permute-start.3 = (f32[32,128]{1,0:T(8,128)S(1)}, f32[32,128]{1,0:T(8,128)S(1)}, u32[]{:S(2)}, u32[]{:S(2)}) collective-permute-start(f32[32,128]{1,0:T(8,128)S(1)} %pad_maximum_fusion.2), channel_id=1, source_target_pairs={{0,1},{1,0},{2,3},{3,2},{4,5},{5,4},{6,7},{7,6},{8,9},{9,8},{10,11... | collective-permute-start | bytes 49160 | tf_op jit(solution)/shard_map/ppermute | solution.py:435
  5.4 1.7 %collective-permute-done.3 = f32[32,128]{1,0:T(8,128)S(1)} collective-permute-done((f32[32,128]{1,0:T(8,128)S(1)}, f32[32,128]{1,0:T(8,128)S(1)}, u32[]{:S(2)}, u32[]{:S(2)}) %collective-permute-start.3) | collective-permute-done | bytes 16416 | tf_op jit(solution)/shard_map/ppermute | solution.py:435
  7.1 2.1 %collective-permute-start.4 = (f32[64,128]{1,0:T(8,128)S(1)}, f32[64,128]{1,0:T(8,128)S(1)}, u32[]{:S(2)}, u32[]{:S(2)}) collective-permute-start(f32[64,128]{1,0:T(8,128)S(1)} %pad_maximum_fusion), channel_id=1, source_target_pairs={{0,2},{2,0},{4,6},{6,4},{1,3},{3,1},{5,7},{7,5},{8,10},{10,8},{12,... | collective-permute-start | bytes 98312 | tf_op jit(solution)/shard_map/ppermute | solution.py:442
  9.3 0.0 collective-permute-start
  9.3 1.6 %collective-permute-start.1 = (f32[480,128]{1,0:T(8,128)S(1)}, f32[480,128]{1,0:T(8,128)S(1)}, u32[]{:S(2)}, u32[]{:S(2)}) collective-permute-start(f32[480,128]{1,0:T(8,128)S(1)} %get-tuple-element.16), channel_id=1, source_target_pairs={{0,24},{8,16},{16,8},{24,0},{1,25},{9,17},{17,9},{25,1},{2,26},{10... | collective-permute-start | bytes 737288 | tf_op jit(solution)/shard_map/ppermute | solution.py:501
  10.9 0.9 %shard_map.42.fz_ref = f32[5,64,128]{2,1,0:T(8,128)S(1)} custom-call(f32[5,144,128]{2,1,0:T(8,128)S(1)} %get-tuple-element.20.q_ref.qt_ref, f32[2,64,128]{2,1,0:T(8,128)S(1)} %get-tuple-element.19.after), custom_call_target="tpu_custom_call" | custom-call | flops 16000000 | bytes 1000000 | tf_op jit(solution)/shard_map/pallas_call | solution.py:492
  11.8 0.7 %shard_map.43.fz2_ref = f32[5,56,128]{2,1,0:T(8,128)S(1)} custom-call(f32[5,144,128]{2,1,0:T(8,128)S(1)} %get-tuple-element.20.q_ref.qt_ref, f32[8,128]{1,0:T(8,128)S(1)} %get-tuple-element.26.after), custom_call_target="tpu_custom_call" | custom-call | flops 16000000 | bytes 1000000 | tf_op jit(solution)/shard_map/pallas_call | solution.py:492
  12.5 0.0 collective-permute-done.4
  12.6 2.7 %collective-permute-start.5 = (f32[64,128]{1,0:T(8,128)S(1)}, f32[64,128]{1,0:T(8,128)S(1)}, u32[]{:S(2)}, u32[]{:S(2)}) collective-permute-start(f32[64,128]{1,0:T(8,128)S(1)} %pad_maximum_fusion.1), channel_id=1, source_target_pairs={{0,6},{2,4},{4,2},{6,0},{1,7},{3,5},{5,3},{7,1},{8,14},{10,12},{12... | collective-permute-start | bytes 98312 | tf_op jit(solution)/shard_map/ppermute | solution.py:446
  15.3 2.0 %shard_map.41.fy_ref = f32[5,176,128]{2,1,0:T(8,128)S(1)} custom-call(f32[5,144,128]{2,1,0:T(8,128)S(1)} %get-tuple-element.13.q_ref, f32[8,128]{1,0:T(8,128)S(1)} %get-tuple-element.24.after), custom_call_target="tpu_custom_call" | custom-call | flops 16000000 | bytes 1000000 | tf_op jit(solution)/shard_map/pallas_call | solution.py:492
  17.3 0.8 %shard_map.44.tz_ref = f32[5,128,128]{2,1,0:T(8,128)S(1)} custom-call(f32[5,144,128]{2,1,0:T(8,128)S(1)} %get-tuple-element.20.q_ref.qt_ref, f32[16,128]{1,0:T(8,128)S(1)} %get-tuple-element.32.lo, f32[16,128]{1,0:T(8,128)S(1)} %get-tuple-element.31.hi, f32[5,64,128]{2,1,0:T(8,128)S(1)} %shard_map.42.fz_ref, f32[5,56,128]{2,1,0:T(8,128)S(1)} %shard_map.43.fz2_ref, ...), custom_call_target="tpu_custom_call" | custom-call | flops 4000000 | bytes 1000000 | tf_op jit(solution)/shard_map/pallas_call | solution.py:533
  18.1 0.3 %collective-permute-done.5 = f32[64,128]{1,0:T(8,128)S(1)} collective-permute-done((f32[64,128]{1,0:T(8,128)S(1)}, f32[64,128]{1,0:T(8,128)S(1)}, u32[]{:S(2)}, u32[]{:S(2)}) %collective-permute-start.5) | collective-permute-done | bytes 32800 | tf_op jit(solution)/shard_map/ppermute | solution.py:446
  18.4 1.3 %collective-permute-start.6 = (f32[8,128]{1,0:T(8,128)S(1)}, f32[8,128]{1,0:T(8,128)S(1)}, u32[]{:S(2)}, u32[]{:S(2)}) collective-permute-start(f32[8,128]{1,0:T(8,128)S(1)} %slice_maximum_fusion.after), channel_id=1, source_target_pairs={{0,16},{8,24},{16,0},{24,8},{1,17},{9,25},{17,1},{25,9},{2,18},{10... | collective-permute-start | bytes 12296 | tf_op jit(solution)/shard_map/ppermute | solution.py:414
  19.7 0.6 %shard_map.45.t_ref = f32[5,128,128]{2,1,0:T(8,128)S(1)} custom-call(f32[5,144,128]{2,1,0:T(8,128)S(1)} %get-tuple-element.13.q_ref, f32[64,128]{1,0:T(8,128)S(1)} %get-tuple-element.28.lo, f32[64,128]{1,0:T(8,128)S(1)} %get-tuple-element.27.hi, f32[5,176,128]{2,1,0:T(8,128)S(1)} %shard_map.41.fy_ref, f32[5,128,128]{2,1,0:T(8,128)S(1)} %shard_map.44.tz_ref, ...), custom_call_target="tpu_custom_call" | custom-call | flops 4000000 | bytes 1000000 | tf_op jit(solution)/shard_map/pallas_call | solution.py:540
  20.3 1.7 %collective-permute-done.6 = f32[8,128]{1,0:T(8,128)S(1)} collective-permute-done((f32[8,128]{1,0:T(8,128)S(1)}, f32[8,128]{1,0:T(8,128)S(1)}, u32[]{:S(2)}, u32[]{:S(2)}) %collective-permute-start.6) | collective-permute-done | bytes 4128 | tf_op jit(solution)/shard_map/ppermute | solution.py:414
  22.0 0.0 collective-permute-done.a_ref
  22.0 0.0 collective-permute-done.1.b_ref
  22.0 1.4 %shard_map.39.tx_ref = f32[5,64,128]{2,1,0:T(8,128)S(1)} custom-call(f32[5,144,128]{2,1,0:T(8,128)S(1)} %get-tuple-element.13.q_ref, f32[480,128]{1,0:T(8,128)S(1)} %collective-permute-done.a_ref, f32[480,128]{1,0:T(8,128)S(1)} %collective-permute-done.1.b_ref, f32[8,128]{1,0:T(8,128)S(1)} %get-tuple-element.22.after), custom_call_target="tpu_custom_call" | custom-call | flops 16000000 | bytes 1000000 | tf_op jit(solution)/shard_map/pallas_call | solution.py:522
  23.4 1.4 %shard_map.40.rest_ref = f32[5,64,128]{2,1,0:T(8,128)S(1)} custom-call(f32[5,144,128]{2,1,0:T(8,128)S(1)} %get-tuple-element.13.q_ref, f32[480,128]{1,0:T(8,128)S(1)} %collective-permute-done.a_ref, f32[480,128]{1,0:T(8,128)S(1)} %collective-permute-done.1.b_ref, f32[8,128]{1,0:T(8,128)S(1)} %slice_maximum_fusion.after), custom_call_target="tpu_custom_call" | custom-call | flops 16000000 | bytes 1000000 | tf_op jit(solution)/shard_map/pallas_call | solution.py:522
  24.9 0.8 %shard_map.46 = f32[5,4,32,128]{3,2,1,0:T(8,128)} custom-call(f32[5,144,128]{2,1,0:T(8,128)S(1)} %get-tuple-element.13.q_ref, f32[5,64,128]{2,1,0:T(8,128)S(1)} %shard_map.39.tx_ref, f32[5,64,128]{2,1,0:T(8,128)S(1)} %shard_map.40.rest_ref, f32[5,128,128]{2,1,0:T(8,128)S(1)} %shard_map.45.t_ref, f32[8,128]{1,0:T(8,128)S(1)} %max.19.top_ref), custom_call_target="tpu_custom_call" | custom-call | flops 1000000 | bytes 1000000 | tf_op jit(solution)/shard_map/pallas_call | solution.py:549
  (12 shorter events, 0.1 us)
Async XLA Ops:
  1.2 1.4 %collective-permute-start.2 = (f32[8,128]{1,0:T(8,128)S(1)}, f32[8,128]{1,0:T(8,128)S(1)}, u32[]{:S(2)}, u32[]{:S(2)}) collective-permute-start(f32[8,128]{1,0:T(8,128)S(1)} %get-tuple-element.14.after), channel_id=1, source_target_pairs={{0,8},{8,0},{16,24},{24,16},{1,9},{9,1},{17,25},{25,17},{2,10},{10... | collective-permute-start | bytes 12296 | tf_op jit(solution)/shard_map/ppermute | solution.py:503
  2.6 4.6 %collective-permute-start.3 = (f32[32,128]{1,0:T(8,128)S(1)}, f32[32,128]{1,0:T(8,128)S(1)}, u32[]{:S(2)}, u32[]{:S(2)}) collective-permute-start(f32[32,128]{1,0:T(8,128)S(1)} %pad_maximum_fusion.2), channel_id=1, source_target_pairs={{0,1},{1,0},{2,3},{3,2},{4,5},{5,4},{6,7},{7,6},{8,9},{9,8},{10,11... | collective-permute-start | bytes 49160 | tf_op jit(solution)/shard_map/ppermute | solution.py:435
  7.1 5.4 %collective-permute-start.4 = (f32[64,128]{1,0:T(8,128)S(1)}, f32[64,128]{1,0:T(8,128)S(1)}, u32[]{:S(2)}, u32[]{:S(2)}) collective-permute-start(f32[64,128]{1,0:T(8,128)S(1)} %pad_maximum_fusion), channel_id=1, source_target_pairs={{0,2},{2,0},{4,6},{6,4},{1,3},{3,1},{5,7},{7,5},{8,10},{10,8},{12,... | collective-permute-start | bytes 98312 | tf_op jit(solution)/shard_map/ppermute | solution.py:442
  9.3 12.7 %collective-permute-start = (f32[480,128]{1,0:T(8,128)S(1)}, f32[480,128]{1,0:T(8,128)S(1)}, u32[]{:S(2)}, u32[]{:S(2)}) collective-permute-start(f32[480,128]{1,0:T(8,128)S(1)} %get-tuple-element.15), channel_id=1, source_target_pairs={{0,8},{8,0},{16,24},{24,16},{1,9},{9,1},{17,25},{25,17},{2,10},{10... | collective-permute-start | bytes 737288 | tf_op jit(solution)/shard_map/ppermute | solution.py:502
  9.3 12.7 %collective-permute-start.1 = (f32[480,128]{1,0:T(8,128)S(1)}, f32[480,128]{1,0:T(8,128)S(1)}, u32[]{:S(2)}, u32[]{:S(2)}) collective-permute-start(f32[480,128]{1,0:T(8,128)S(1)} %get-tuple-element.16), channel_id=1, source_target_pairs={{0,24},{8,16},{16,8},{24,0},{1,25},{9,17},{17,9},{25,1},{2,26},{10... | collective-permute-start | bytes 737288 | tf_op jit(solution)/shard_map/ppermute | solution.py:501
  12.6 5.8 %collective-permute-start.5 = (f32[64,128]{1,0:T(8,128)S(1)}, f32[64,128]{1,0:T(8,128)S(1)}, u32[]{:S(2)}, u32[]{:S(2)}) collective-permute-start(f32[64,128]{1,0:T(8,128)S(1)} %pad_maximum_fusion.1), channel_id=1, source_target_pairs={{0,6},{2,4},{4,2},{6,0},{1,7},{3,5},{5,3},{7,1},{8,14},{10,12},{12... | collective-permute-start | bytes 98312 | tf_op jit(solution)/shard_map/ppermute | solution.py:446
  18.4 3.6 %collective-permute-start.6 = (f32[8,128]{1,0:T(8,128)S(1)}, f32[8,128]{1,0:T(8,128)S(1)}, u32[]{:S(2)}, u32[]{:S(2)}) collective-permute-start(f32[8,128]{1,0:T(8,128)S(1)} %slice_maximum_fusion.after), channel_id=1, source_target_pairs={{0,16},{8,24},{16,0},{24,8},{1,17},{9,25},{17,1},{25,9},{2,18},{10... | collective-permute-start | bytes 12296 | tf_op jit(solution)/shard_map/ppermute | solution.py:414

commit v10 on v9

--- a/solution.py
+++ b/solution.py
@@ -174,7 +174,14 @@
             put(order[m], i, values[m])
         return ahead
 
-    lax.fori_loop(0, count, step, face_average(prim, aux, 0, s, comps, first))
+    def steps(j, average):
+        for u in range(2):
+            average = step(2 * j + u, average)
+        return average
+
+    average = lax.fori_loop(0, count // 2, steps, face_average(prim, aux, 0, s, comps, first))
+    if count % 2:
+        step(count - 1, average)
 
 
 def prepare_kernel(nx, ny, nz, rho, vel, p, q_ref, top_ref, sems):
@@ -393,6 +400,10 @@
     )
 
 
+def permute(value, axis, pairs):
+    return lax.ppermute(value, axis, pairs)
+
+
 def fields(*counts, r, w):
     return [pltpu.VMEM((count, r, w), f32) for count in counts]
 
@@ -411,7 +422,7 @@
         return lax.pmax(top, axis)
     d = first
     while d < n:
-        top = jnp.maximum(top, lax.ppermute(top, axis, [(i, i ^ d) for i in range(n)]))
+        top = jnp.maximum(top, permute(top, axis, [(i, i ^ (d | (first > 1))) for i in range(n)]))
         d *= 2
     return top
 
@@ -432,18 +443,18 @@
     if n == 1:
         return second, first, top
     if n == 2:
-        got = lax.ppermute(with_top(edges.reshape(2 * size, -1), free, top), axis, [(0, 1), (1, 0)])
+        got = permute(with_top(edges.reshape(2 * size, -1), free, top), axis, [(0, 1), (1, 0)])
         return got[size:], got[:size], got_top(top, got)
     if n % 2:
-        lower = lax.ppermute(second, axis, [(i, (i + 1) % n) for i in range(n)])
-        upper = lax.ppermute(first, axis, [((i + 1) % n, i) for i in range(n)])
+        lower = permute(second, axis, [(i, (i + 1) % n) for i in range(n)])
+        upper = permute(first, axis, [((i + 1) % n, i) for i in range(n)])
         return lower, upper, lax.pmax(top, axis)
     odd = lax.rem(lax.axis_index(axis), 2) == 1
-    got_a = lax.ppermute(with_top(first, free, top), axis, pairs_a(n))
+    got_a = permute(with_top(first, free, top), axis, pairs_a(n))
     top = got_top(top, got_a)
     if mids is not None:
         mids.append(top)
-    got_b = lax.ppermute(with_top(second, free, top), axis, pairs_b(n))
+    got_b = permute(with_top(second, free, top), axis, pairs_b(n))
     if n == 4:
         top = got_top(top, got_b)
     else:
@@ -498,15 +509,15 @@
         )(source, after)
 
     if xeven:
-        got_b = lax.ppermute(xb, "gx", pairs_b(gx))
-        got_a = lax.ppermute(xa, "gx", pairs_a(gx))
-        top = jnp.maximum(top, lax.ppermute(top, "gx", pairs_a(gx)))
+        got_b = permute(xb, "gx", pairs_b(gx))
+        got_a = permute(xa, "gx", pairs_a(gx))
+        top = jnp.maximum(top, permute(top, "gx", pairs_a(gx)))
     else:
-        got_a = lax.ppermute(xa, "gx", [(i, (i + 1) % gx) for i in range(gx)])
-        got_b = lax.ppermute(xb, "gx", [((i + 1) % gx, i) for i in range(gx)])
+        got_a = permute(xa, "gx", [(i, (i + 1) % gx) for i in range(gx)])
+        got_b = permute(xb, "gx", [((i + 1) % gx, i) for i in range(gx)])
     ztop = top if n == nz else jnp.full((8, n), jnp.max(top[7]))
     zt = nz // 8
-    za, zb = zt * 7 // 16, zt * 6 // 16
+    za, zb = zt * 7 // 16, zt * 4 // 16
     fz = [
         inner(qt, 0, za, 1, n, nz, 0, (2, 0, 1), 8 * za + 8, ye),
         inner(qt, za, zb, 1, n, nz, 0, (2, 0, 1), 8 * zb + 8, ztop),
@@ -527,7 +538,7 @@
             [VMEM] * 3 + [ANY],
         )(q, got_a, got_b, after)
 
-    split = rup(ny // 2, 8)
+    split = rup(ny // 4, 8)
     tx = along_x(0, split, mids[0] if mids else top)
     tx_rest = along_x(split, ny - split, top)
     tz = call(

time: 25.8 us -> 25 us (0.969)
  starting transfers between devices: 11.2 us -> 10.2 us
  waiting for transfers between devices: 4.33 us -> 4.83 us
  Pallas kernels: 10 us -> 9.62 us
    ppermute x7, starting transfers between devices: 11.2 us -> 10.2 us  [permute(): return lax.ppermute(value, axis, pairs)]
    ppermute x7, waiting for transfers between devices: 4.33 us -> 4.83 us  [permute(): return lax.ppermute(value, axis, pairs)]
    pallas_call x3, Pallas kernels: 3.59 us -> 3.18 us  [inner(): call(functools.partial(inner_kernel, first, count, more, length, block, c...]
  transfers between devices with their start and end apart: 7 -> 7, of which waited for: 4 -> 3; matrix products, arithmetic and copies ran while one was open for 0% -> 0% of each run, Pallas kernels for 20% -> 20%
where the time goes in v10:
time: 25 us; the launch traced here: 24.9 us
  starting transfers between devices  10.2 us (41%)
  Pallas kernels  9.62 us (38%)
  waiting for transfers between devices  4.83 us (19%)
    ppermute x7, starting transfers between devices, permute(): return lax.ppermute(value, axis, pairs)  10.2 us
    ppermute x7, waiting for transfers between devices, permute(): return lax.ppermute(value, axis, pairs)  4.83 us
    pallas_call x3, Pallas kernels, inner(): call(functools.partial(inner_kernel, first, count, more, length, block, c...  3.18 us
    pallas_call x2, Pallas kernels, along_x(): call(functools.partial(x_kernel, nx, ny, first, ys, xeven), S((5, nx * ys...  2.78 us
    pallas_call x1, Pallas kernels, local(): call(functools.partial(prepare_kernel, nx, ny, nz), (S((5, n + 16, nz), f...  1.17 us
    pallas_call x1, Pallas kernels, local(): call(functools.partial(z_ends_kernel, nz), S((5, n, nz), f32), sweep_flop...  1.01 us
    pallas_call x1, Pallas kernels, local(): call(functools.partial(final_kernel, nx, ny, split), out, 1000000, [pltpu...  0.78 us
    pallas_call x1, Pallas kernels, local(): call(functools.partial(y_ends_kernel, nx, ny, block), S((5, n, nz), f32),...  0.53 us
  transfers between devices with their start and end apart: 7, of which 3 were waited for; matrix products, arithmetic and copies ran while one was open for 0% of the time, Pallas kernels for 20%

profile of v10, /device:TPU:0, one launch (start us, length us, event | category | flops | bytes accessed | tf_op | source)
XLA Modules:
  0.0 24.9 jit_solution(3146706693145264640)
XLA Ops:
  0.0 1.2 %shard_map.37 = (f32[5,144,128]{2,1,0:T(8,128)S(1)}, f32[8,128]{1,0:T(8,128)S(1)}) custom-call(f32[128,128]{1,0:T(8,128)} %bitcast.15, f32[3,128,128]{2,1,0:T(8,128)} %bitcast.14, f32[128,128]{1,0:T(8,128)} %bitcast.16), custom_call_target="tpu_custom_call" | custom-call | flops 2000000 | bytes 1000000 | tf_op jit(solution)/shard_map/pallas_call | solution.py:478
  1.2 0.6 %collective-permute-start.2 = (f32[8,128]{1,0:T(8,128)S(1)}, f32[8,128]{1,0:T(8,128)S(1)}, u32[]{:S(2)}, u32[]{:S(2)}) collective-permute-start(f32[8,128]{1,0:T(8,128)S(1)} %get-tuple-element.14.after), channel_id=1, source_target_pairs={{0,8},{8,0},{16,24},{24,16},{1,9},{9,1},{17,25},{25,17},{2,10},{10... | collective-permute-start | bytes 12296 | tf_op jit(solution)/shard_map/ppermute | solution.py:404
  1.7 0.2 shard_map.38
  1.9 0.6 %collective-permute-done.2 = f32[8,128]{1,0:T(8,128)S(1)} collective-permute-done((f32[8,128]{1,0:T(8,128)S(1)}, f32[8,128]{1,0:T(8,128)S(1)}, u32[]{:S(2)}, u32[]{:S(2)}) %collective-permute-start.2) | collective-permute-done | bytes 4128 | tf_op jit(solution)/shard_map/ppermute | solution.py:404
  2.6 2.8 %collective-permute-start.3 = (f32[32,128]{1,0:T(8,128)S(1)}, f32[32,128]{1,0:T(8,128)S(1)}, u32[]{:S(2)}, u32[]{:S(2)}) collective-permute-start(f32[32,128]{1,0:T(8,128)S(1)} %pad_maximum_fusion.2), channel_id=1, source_target_pairs={{0,1},{1,0},{2,3},{3,2},{4,5},{5,4},{6,7},{7,6},{8,9},{9,8},{10,11... | collective-permute-start | bytes 49160 | tf_op jit(solution)/shard_map/ppermute | solution.py:404
  5.4 1.7 %collective-permute-done.3 = f32[32,128]{1,0:T(8,128)S(1)} collective-permute-done((f32[32,128]{1,0:T(8,128)S(1)}, f32[32,128]{1,0:T(8,128)S(1)}, u32[]{:S(2)}, u32[]{:S(2)}) %collective-permute-start.3) | collective-permute-done | bytes 16416 | tf_op jit(solution)/shard_map/ppermute | solution.py:404
  7.1 2.1 %collective-permute-start.4 = (f32[64,128]{1,0:T(8,128)S(1)}, f32[64,128]{1,0:T(8,128)S(1)}, u32[]{:S(2)}, u32[]{:S(2)}) collective-permute-start(f32[64,128]{1,0:T(8,128)S(1)} %pad_maximum_fusion), channel_id=1, source_target_pairs={{0,2},{2,0},{4,6},{6,4},{1,3},{3,1},{5,7},{7,5},{8,10},{10,8},{12,... | collective-permute-start | bytes 98312 | tf_op jit(solution)/shard_map/ppermute | solution.py:404
  9.3 0.0 collective-permute-start
  9.3 1.6 %collective-permute-start.1 = (f32[480,128]{1,0:T(8,128)S(1)}, f32[480,128]{1,0:T(8,128)S(1)}, u32[]{:S(2)}, u32[]{:S(2)}) collective-permute-start(f32[480,128]{1,0:T(8,128)S(1)} %get-tuple-element.16), channel_id=1, source_target_pairs={{0,24},{8,16},{16,8},{24,0},{1,25},{9,17},{17,9},{25,1},{2,26},{10... | collective-permute-start | bytes 737288 | tf_op jit(solution)/shard_map/ppermute | solution.py:404
  10.9 0.8 %shard_map.42.fz_ref = f32[5,64,128]{2,1,0:T(8,128)S(1)} custom-call(f32[5,144,128]{2,1,0:T(8,128)S(1)} %get-tuple-element.20.q_ref.qt_ref, f32[2,64,128]{2,1,0:T(8,128)S(1)} %get-tuple-element.19.after), custom_call_target="tpu_custom_call" | custom-call | flops 16000000 | bytes 1000000 | tf_op jit(solution)/shard_map/pallas_call | solution.py:503
  11.7 0.5 %shard_map.43.fz2_ref = f32[5,40,128]{2,1,0:T(8,128)S(1)} custom-call(f32[5,144,128]{2,1,0:T(8,128)S(1)} %get-tuple-element.20.q_ref.qt_ref, f32[8,128]{1,0:T(8,128)S(1)} %get-tuple-element.26.after), custom_call_target="tpu_custom_call" | custom-call | flops 16000000 | bytes 1000000 | tf_op jit(solution)/shard_map/pallas_call | solution.py:503
  12.2 0.0 collective-permute-done.4
  12.3 3.0 %collective-permute-start.5 = (f32[64,128]{1,0:T(8,128)S(1)}, f32[64,128]{1,0:T(8,128)S(1)}, u32[]{:S(2)}, u32[]{:S(2)}) collective-permute-start(f32[64,128]{1,0:T(8,128)S(1)} %pad_maximum_fusion.1), channel_id=1, source_target_pairs={{0,6},{2,4},{4,2},{6,0},{1,7},{3,5},{5,3},{7,1},{8,14},{10,12},{12... | collective-permute-start | bytes 98312 | tf_op jit(solution)/shard_map/ppermute | solution.py:404
  15.3 1.9 %shard_map.41.fy_ref = f32[5,176,128]{2,1,0:T(8,128)S(1)} custom-call(f32[5,144,128]{2,1,0:T(8,128)S(1)} %get-tuple-element.13.q_ref, f32[8,128]{1,0:T(8,128)S(1)} %get-tuple-element.24.after), custom_call_target="tpu_custom_call" | custom-call | flops 16000000 | bytes 1000000 | tf_op jit(solution)/shard_map/pallas_call | solution.py:503
  17.1 1.0 %shard_map.44.tz_ref = f32[5,128,128]{2,1,0:T(8,128)S(1)} custom-call(f32[5,144,128]{2,1,0:T(8,128)S(1)} %get-tuple-element.20.q_ref.qt_ref, f32[16,128]{1,0:T(8,128)S(1)} %get-tuple-element.32.lo, f32[16,128]{1,0:T(8,128)S(1)} %get-tuple-element.31.hi, f32[5,64,128]{2,1,0:T(8,128)S(1)} %shard_map.42.fz_ref, f32[5,40,128]{2,1,0:T(8,128)S(1)} %shard_map.43.fz2_ref, ...), custom_call_target="tpu_custom_call" | custom-call | flops 4000000 | bytes 1000000 | tf_op jit(solution)/shard_map/pallas_call | solution.py:544
  18.2 0.0 collective-permute-done.5
  18.2 0.1 collective-permute-start.6
  18.3 0.5 %shard_map.45.t_ref = f32[5,128,128]{2,1,0:T(8,128)S(1)} custom-call(f32[5,144,128]{2,1,0:T(8,128)S(1)} %get-tuple-element.13.q_ref, f32[64,128]{1,0:T(8,128)S(1)} %get-tuple-element.28.lo, f32[64,128]{1,0:T(8,128)S(1)} %get-tuple-element.27.hi, f32[5,176,128]{2,1,0:T(8,128)S(1)} %shard_map.41.fy_ref, f32[5,128,128]{2,1,0:T(8,128)S(1)} %shard_map.44.tz_ref, ...), custom_call_target="tpu_custom_call" | custom-call | flops 4000000 | bytes 1000000 | tf_op jit(solution)/shard_map/pallas_call | solution.py:551
  18.8 2.5 %collective-permute-done.6 = f32[8,128]{1,0:T(8,128)S(1)} collective-permute-done((f32[8,128]{1,0:T(8,128)S(1)}, f32[8,128]{1,0:T(8,128)S(1)}, u32[]{:S(2)}, u32[]{:S(2)}) %collective-permute-start.6) | collective-permute-done | bytes 4128 | tf_op jit(solution)/shard_map/ppermute | solution.py:404
  21.3 0.0 collective-permute-done.a_ref
  21.3 0.0 collective-permute-done.1.b_ref
  21.3 0.7 %shard_map.39.tx_ref = f32[5,32,128]{2,1,0:T(8,128)S(1)} custom-call(f32[5,144,128]{2,1,0:T(8,128)S(1)} %get-tuple-element.13.q_ref, f32[480,128]{1,0:T(8,128)S(1)} %collective-permute-done.a_ref, f32[480,128]{1,0:T(8,128)S(1)} %collective-permute-done.1.b_ref, f32[8,128]{1,0:T(8,128)S(1)} %get-tuple-element.22.after), custom_call_target="tpu_custom_call" | custom-call | flops 16000000 | bytes 1000000 | tf_op jit(solution)/shard_map/pallas_call | solution.py:533
  22.0 2.1 %shard_map.40.rest_ref = f32[5,96,128]{2,1,0:T(8,128)S(1)} custom-call(f32[5,144,128]{2,1,0:T(8,128)S(1)} %get-tuple-element.13.q_ref, f32[480,128]{1,0:T(8,128)S(1)} %collective-permute-done.a_ref, f32[480,128]{1,0:T(8,128)S(1)} %collective-permute-done.1.b_ref, f32[8,128]{1,0:T(8,128)S(1)} %slice_maximum_fusion.after), custom_call_target="tpu_custom_call" | custom-call | flops 16000000 | bytes 1000000 | tf_op jit(solution)/shard_map/pallas_call | solution.py:533
  24.1 0.8 %shard_map.46 = f32[5,4,32,128]{3,2,1,0:T(8,128)} custom-call(f32[5,144,128]{2,1,0:T(8,128)S(1)} %get-tuple-element.13.q_ref, f32[5,32,128]{2,1,0:T(8,128)S(1)} %shard_map.39.tx_ref, f32[5,96,128]{2,1,0:T(8,128)S(1)} %shard_map.40.rest_ref, f32[5,128,128]{2,1,0:T(8,128)S(1)} %shard_map.45.t_ref, f32[8,128]{1,0:T(8,128)S(1)} %max.19.top_ref), custom_call_target="tpu_custom_call" | custom-call | flops 1000000 | bytes 1000000 | tf_op jit(solution)/shard_map/pallas_call | solution.py:560
  (12 shorter events, 0.1 us)
Async XLA Ops:
  1.2 1.4 %collective-permute-start.2 = (f32[8,128]{1,0:T(8,128)S(1)}, f32[8,128]{1,0:T(8,128)S(1)}, u32[]{:S(2)}, u32[]{:S(2)}) collective-permute-start(f32[8,128]{1,0:T(8,128)S(1)} %get-tuple-element.14.after), channel_id=1, source_target_pairs={{0,8},{8,0},{16,24},{24,16},{1,9},{9,1},{17,25},{25,17},{2,10},{10... | collective-permute-start | bytes 12296 | tf_op jit(solution)/shard_map/ppermute | solution.py:404
  2.6 4.6 %collective-permute-start.3 = (f32[32,128]{1,0:T(8,128)S(1)}, f32[32,128]{1,0:T(8,128)S(1)}, u32[]{:S(2)}, u32[]{:S(2)}) collective-permute-start(f32[32,128]{1,0:T(8,128)S(1)} %pad_maximum_fusion.2), channel_id=1, source_target_pairs={{0,1},{1,0},{2,3},{3,2},{4,5},{5,4},{6,7},{7,6},{8,9},{9,8},{10,11... | collective-permute-start | bytes 49160 | tf_op jit(solution)/shard_map/ppermute | solution.py:404
  7.1 5.1 %collective-permute-start.4 = (f32[64,128]{1,0:T(8,128)S(1)}, f32[64,128]{1,0:T(8,128)S(1)}, u32[]{:S(2)}, u32[]{:S(2)}) collective-permute-start(f32[64,128]{1,0:T(8,128)S(1)} %pad_maximum_fusion), channel_id=1, source_target_pairs={{0,2},{2,0},{4,6},{6,4},{1,3},{3,1},{5,7},{7,5},{8,10},{10,8},{12,... | collective-permute-start | bytes 98312 | tf_op jit(solution)/shard_map/ppermute | solution.py:404
  9.3 12.0 %collective-permute-start = (f32[480,128]{1,0:T(8,128)S(1)}, f32[480,128]{1,0:T(8,128)S(1)}, u32[]{:S(2)}, u32[]{:S(2)}) collective-permute-start(f32[480,128]{1,0:T(8,128)S(1)} %get-tuple-element.15), channel_id=1, source_target_pairs={{0,8},{8,0},{16,24},{24,16},{1,9},{9,1},{17,25},{25,17},{2,10},{10... | collective-permute-start | bytes 737288 | tf_op jit(solution)/shard_map/ppermute | solution.py:404
  9.3 12.0 %collective-permute-start.1 = (f32[480,128]{1,0:T(8,128)S(1)}, f32[480,128]{1,0:T(8,128)S(1)}, u32[]{:S(2)}, u32[]{:S(2)}) collective-permute-start(f32[480,128]{1,0:T(8,128)S(1)} %get-tuple-element.16), channel_id=1, source_target_pairs={{0,24},{8,16},{16,8},{24,0},{1,25},{9,17},{17,9},{25,1},{2,26},{10... | collective-permute-start | bytes 737288 | tf_op jit(solution)/shard_map/ppermute | solution.py:404
  12.3 5.9 %collective-permute-start.5 = (f32[64,128]{1,0:T(8,128)S(1)}, f32[64,128]{1,0:T(8,128)S(1)}, u32[]{:S(2)}, u32[]{:S(2)}) collective-permute-start(f32[64,128]{1,0:T(8,128)S(1)} %pad_maximum_fusion.1), channel_id=1, source_target_pairs={{0,6},{2,4},{4,2},{6,0},{1,7},{3,5},{5,3},{7,1},{8,14},{10,12},{12... | collective-permute-start | bytes 98312 | tf_op jit(solution)/shard_map/ppermute | solution.py:404
  18.2 3.1 %collective-permute-start.6 = (f32[8,128]{1,0:T(8,128)S(1)}, f32[8,128]{1,0:T(8,128)S(1)}, u32[]{:S(2)}, u32[]{:S(2)}) collective-permute-start(f32[8,128]{1,0:T(8,128)S(1)} %slice_maximum_fusion.after), channel_id=1, source_target_pairs={{0,24},{8,16},{16,8},{24,0},{1,25},{9,17},{17,9},{25,1},{2,26},{10... | collective-permute-start | bytes 12296 | tf_op jit(solution)/shard_map/ppermute | solution.py:404

commit v11 on v10

--- a/solution.py
+++ b/solution.py
@@ -75,7 +75,7 @@
     def pair(i):
         aux[2, rows(i), :] = jnp.maximum(aux[3, rows(i), :], aux[3, rows(i, s), :])
 
-    over(count, 2, body)
+    over(count, 4, body)
     over(pairs, 8, pair)
 
 
@@ -517,7 +517,7 @@
         got_b = permute(xb, "gx", [((i + 1) % gx, i) for i in range(gx)])
     ztop = top if n == nz else jnp.full((8, n), jnp.max(top[7]))
     zt = nz // 8
-    za, zb = zt * 7 // 16, zt * 4 // 16
+    za, zb = zt * 7 // 16, zt * 7 // 16
     fz = [
         inner(qt, 0, za, 1, n, nz, 0, (2, 0, 1), 8 * za + 8, ye),
         inner(qt, za, zb, 1, n, nz, 0, (2, 0, 1), 8 * zb + 8, ztop),
@@ -538,7 +538,7 @@
             [VMEM] * 3 + [ANY],
         )(q, got_a, got_b, after)
 
-    split = rup(ny // 4, 8)
+    split = rup(ny // 2, 8)
     tx = along_x(0, split, mids[0] if mids else top)
     tx_rest = along_x(split, ny - split, top)
     tz = call(

time: 25 us -> 25.1 us (level)
  waiting for transfers between devices: 4.83 us -> 5.54 us
  starting transfers between devices: 10.2 us -> 9.84 us
    ppermute x7, waiting for transfers between devices: 4.83 us -> 5.54 us  [permute(): return lax.ppermute(value, axis, pairs)]
    pallas_call x1, Pallas kernels: 1.01 us -> 0.56 us  [local(): call(functools.partial(z_ends_kernel, nz), S((5, n, nz), f32), sweep_flop...]
    ppermute x7, starting transfers between devices: 10.2 us -> 9.84 us  [permute(): return lax.ppermute(value, axis, pairs)]
    pallas_call x3, Pallas kernels: 3.18 us -> 3.48 us  [inner(): call(functools.partial(inner_kernel, first, count, more, length, block, c...]
  transfers between devices with their start and end apart: 7 -> 7, of which waited for: 3 -> 4; matrix products, arithmetic and copies ran while one was open for 0% -> 0% of each run, Pallas kernels for 20% -> 19%
where the time goes in v11:
time: 25.1 us; the launch traced here: 24.9 us
  starting transfers between devices  9.84 us (39%)
  Pallas kernels  9.39 us (37%)
  waiting for transfers between devices  5.54 us (22%)
    ppermute x7, starting transfers between devices, permute(): return lax.ppermute(value, axis, pairs)  9.84 us
    ppermute x7, waiting for transfers between devices, permute(): return lax.ppermute(value, axis, pairs)  5.54 us
    pallas_call x3, Pallas kernels, inner(): call(functools.partial(inner_kernel, first, count, more, length, block, c...  3.48 us
    pallas_call x2, Pallas kernels, along_x(): call(functools.partial(x_kernel, nx, ny, first, ys, xeven), S((5, nx * ys...  2.69 us
    pallas_call x1, Pallas kernels, local(): call(functools.partial(prepare_kernel, nx, ny, nz), (S((5, n + 16, nz), f...  1.17 us
    pallas_call x1, Pallas kernels, local(): call(functools.partial(final_kernel, nx, ny, split), out, 1000000, [pltpu...  0.79 us
    pallas_call x1, Pallas kernels, local(): call(functools.partial(z_ends_kernel, nz), S((5, n, nz), f32), sweep_flop...  0.56 us
    pallas_call x1, Pallas kernels, local(): call(functools.partial(y_ends_kernel, nx, ny, block), S((5, n, nz), f32),...  0.53 us
  transfers between devices with their start and end apart: 7, of which 4 were waited for; matrix products, arithmetic and copies ran while one was open for 0% of the time, Pallas kernels for 19%

profile of v11, /device:TPU:0, one launch (start us, length us, event | category | flops | bytes accessed | tf_op | source)
XLA Modules:
  0.0 24.9 jit_solution(1344455941476334981)
XLA Ops:
  0.0 1.2 %shard_map.37 = (f32[5,144,128]{2,1,0:T(8,128)S(1)}, f32[8,128]{1,0:T(8,128)S(1)}) custom-call(f32[128,128]{1,0:T(8,128)} %bitcast.15, f32[3,128,128]{2,1,0:T(8,128)} %bitcast.14, f32[128,128]{1,0:T(8,128)} %bitcast.16), custom_call_target="tpu_custom_call" | custom-call | flops 2000000 | bytes 1000000 | tf_op jit(solution)/shard_map/pallas_call | solution.py:478
  1.2 0.6 %collective-permute-start.2 = (f32[8,128]{1,0:T(8,128)S(1)}, f32[8,128]{1,0:T(8,128)S(1)}, u32[]{:S(2)}, u32[]{:S(2)}) collective-permute-start(f32[8,128]{1,0:T(8,128)S(1)} %get-tuple-element.14.after), channel_id=1, source_target_pairs={{0,8},{8,0},{16,24},{24,16},{1,9},{9,1},{17,25},{25,17},{2,10},{10... | collective-permute-start | bytes 12296 | tf_op jit(solution)/shard_map/ppermute | solution.py:404
  1.7 0.2 shard_map.38
  1.9 0.6 %collective-permute-done.2 = f32[8,128]{1,0:T(8,128)S(1)} collective-permute-done((f32[8,128]{1,0:T(8,128)S(1)}, f32[8,128]{1,0:T(8,128)S(1)}, u32[]{:S(2)}, u32[]{:S(2)}) %collective-permute-start.2) | collective-permute-done | bytes 4128 | tf_op jit(solution)/shard_map/ppermute | solution.py:404
  2.6 2.8 %collective-permute-start.3 = (f32[32,128]{1,0:T(8,128)S(1)}, f32[32,128]{1,0:T(8,128)S(1)}, u32[]{:S(2)}, u32[]{:S(2)}) collective-permute-start(f32[32,128]{1,0:T(8,128)S(1)} %pad_maximum_fusion.2), channel_id=1, source_target_pairs={{0,1},{1,0},{2,3},{3,2},{4,5},{5,4},{6,7},{7,6},{8,9},{9,8},{10,11... | collective-permute-start | bytes 49160 | tf_op jit(solution)/shard_map/ppermute | solution.py:404
  5.4 1.7 %collective-permute-done.3 = f32[32,128]{1,0:T(8,128)S(1)} collective-permute-done((f32[32,128]{1,0:T(8,128)S(1)}, f32[32,128]{1,0:T(8,128)S(1)}, u32[]{:S(2)}, u32[]{:S(2)}) %collective-permute-start.3) | collective-permute-done | bytes 16416 | tf_op jit(solution)/shard_map/ppermute | solution.py:404
  7.1 2.1 %collective-permute-start.4 = (f32[64,128]{1,0:T(8,128)S(1)}, f32[64,128]{1,0:T(8,128)S(1)}, u32[]{:S(2)}, u32[]{:S(2)}) collective-permute-start(f32[64,128]{1,0:T(8,128)S(1)} %pad_maximum_fusion), channel_id=1, source_target_pairs={{0,2},{2,0},{4,6},{6,4},{1,3},{3,1},{5,7},{7,5},{8,10},{10,8},{12,... | collective-permute-start | bytes 98312 | tf_op jit(solution)/shard_map/ppermute | solution.py:404
  9.3 0.0 collective-permute-start
  9.3 1.6 %collective-permute-start.1 = (f32[480,128]{1,0:T(8,128)S(1)}, f32[480,128]{1,0:T(8,128)S(1)}, u32[]{:S(2)}, u32[]{:S(2)}) collective-permute-start(f32[480,128]{1,0:T(8,128)S(1)} %get-tuple-element.16), channel_id=1, source_target_pairs={{0,24},{8,16},{16,8},{24,0},{1,25},{9,17},{17,9},{25,1},{2,26},{10... | collective-permute-start | bytes 737288 | tf_op jit(solution)/shard_map/ppermute | solution.py:404
  10.9 0.8 %shard_map.42.fz_ref = f32[5,64,128]{2,1,0:T(8,128)S(1)} custom-call(f32[5,144,128]{2,1,0:T(8,128)S(1)} %get-tuple-element.20.q_ref.qt_ref, f32[2,64,128]{2,1,0:T(8,128)S(1)} %get-tuple-element.19.after), custom_call_target="tpu_custom_call" | custom-call | flops 16000000 | bytes 1000000 | tf_op jit(solution)/shard_map/pallas_call | solution.py:503
  11.7 0.8 %shard_map.43.fz2_ref = f32[5,64,128]{2,1,0:T(8,128)S(1)} custom-call(f32[5,144,128]{2,1,0:T(8,128)S(1)} %get-tuple-element.20.q_ref.qt_ref, f32[8,128]{1,0:T(8,128)S(1)} %get-tuple-element.26.after), custom_call_target="tpu_custom_call" | custom-call | flops 16000000 | bytes 1000000 | tf_op jit(solution)/shard_map/pallas_call | solution.py:503
  12.6 0.0 collective-permute-done.4
  12.6 2.7 %collective-permute-start.5 = (f32[64,128]{1,0:T(8,128)S(1)}, f32[64,128]{1,0:T(8,128)S(1)}, u32[]{:S(2)}, u32[]{:S(2)}) collective-permute-start(f32[64,128]{1,0:T(8,128)S(1)} %pad_maximum_fusion.1), channel_id=1, source_target_pairs={{0,6},{2,4},{4,2},{6,0},{1,7},{3,5},{5,3},{7,1},{8,14},{10,12},{12... | collective-permute-start | bytes 98312 | tf_op jit(solution)/shard_map/ppermute | solution.py:404
  15.3 1.8 %shard_map.41.fy_ref = f32[5,176,128]{2,1,0:T(8,128)S(1)} custom-call(f32[5,144,128]{2,1,0:T(8,128)S(1)} %get-tuple-element.13.q_ref, f32[8,128]{1,0:T(8,128)S(1)} %get-tuple-element.24.after), custom_call_target="tpu_custom_call" | custom-call | flops 16000000 | bytes 1000000 | tf_op jit(solution)/shard_map/pallas_call | solution.py:503
  17.1 0.6 %shard_map.44.tz_ref = f32[5,128,128]{2,1,0:T(8,128)S(1)} custom-call(f32[5,144,128]{2,1,0:T(8,128)S(1)} %get-tuple-element.20.q_ref.qt_ref, f32[16,128]{1,0:T(8,128)S(1)} %get-tuple-element.32.lo, f32[16,128]{1,0:T(8,128)S(1)} %get-tuple-element.31.hi, f32[5,64,128]{2,1,0:T(8,128)S(1)} %shard_map.42.fz_ref, f32[5,64,128]{2,1,0:T(8,128)S(1)} %shard_map.43.fz2_ref, ...), custom_call_target="tpu_custom_call" | custom-call | flops 4000000 | bytes 1000000 | tf_op jit(solution)/shard_map/pallas_call | solution.py:544
  17.7 0.7 %collective-permute-done.5 = f32[64,128]{1,0:T(8,128)S(1)} collective-permute-done((f32[64,128]{1,0:T(8,128)S(1)}, f32[64,128]{1,0:T(8,128)S(1)}, u32[]{:S(2)}, u32[]{:S(2)}) %collective-permute-start.5) | collective-permute-done | bytes 32800 | tf_op jit(solution)/shard_map/ppermute | solution.py:404
  18.4 0.0 collective-permute-start.6
  18.4 0.5 %shard_map.45.t_ref = f32[5,128,128]{2,1,0:T(8,128)S(1)} custom-call(f32[5,144,128]{2,1,0:T(8,128)S(1)} %get-tuple-element.13.q_ref, f32[64,128]{1,0:T(8,128)S(1)} %get-tuple-element.28.lo, f32[64,128]{1,0:T(8,128)S(1)} %get-tuple-element.27.hi, f32[5,176,128]{2,1,0:T(8,128)S(1)} %shard_map.41.fy_ref, f32[5,128,128]{2,1,0:T(8,128)S(1)} %shard_map.44.tz_ref, ...), custom_call_target="tpu_custom_call" | custom-call | flops 4000000 | bytes 1000000 | tf_op jit(solution)/shard_map/pallas_call | solution.py:551
  18.9 2.5 %collective-permute-done.6 = f32[8,128]{1,0:T(8,128)S(1)} collective-permute-done((f32[8,128]{1,0:T(8,128)S(1)}, f32[8,128]{1,0:T(8,128)S(1)}, u32[]{:S(2)}, u32[]{:S(2)}) %collective-permute-start.6) | collective-permute-done | bytes 4128 | tf_op jit(solution)/shard_map/ppermute | solution.py:404
  21.4 0.0 collective-permute-done.a_ref
  21.4 0.0 collective-permute-done.1.b_ref
  21.4 1.3 %shard_map.39.tx_ref = f32[5,64,128]{2,1,0:T(8,128)S(1)} custom-call(f32[5,144,128]{2,1,0:T(8,128)S(1)} %get-tuple-element.13.q_ref, f32[480,128]{1,0:T(8,128)S(1)} %collective-permute-done.a_ref, f32[480,128]{1,0:T(8,128)S(1)} %collective-permute-done.1.b_ref, f32[8,128]{1,0:T(8,128)S(1)} %get-tuple-element.22.after), custom_call_target="tpu_custom_call" | custom-call | flops 16000000 | bytes 1000000 | tf_op jit(solution)/shard_map/pallas_call | solution.py:533
  22.8 1.3 %shard_map.40.rest_ref = f32[5,64,128]{2,1,0:T(8,128)S(1)} custom-call(f32[5,144,128]{2,1,0:T(8,128)S(1)} %get-tuple-element.13.q_ref, f32[480,128]{1,0:T(8,128)S(1)} %collective-permute-done.a_ref, f32[480,128]{1,0:T(8,128)S(1)} %collective-permute-done.1.b_ref, f32[8,128]{1,0:T(8,128)S(1)} %slice_maximum_fusion.after), custom_call_target="tpu_custom_call" | custom-call | flops 16000000 | bytes 1000000 | tf_op jit(solution)/shard_map/pallas_call | solution.py:533
  24.1 0.8 %shard_map.46 = f32[5,4,32,128]{3,2,1,0:T(8,128)} custom-call(f32[5,144,128]{2,1,0:T(8,128)S(1)} %get-tuple-element.13.q_ref, f32[5,64,128]{2,1,0:T(8,128)S(1)} %shard_map.39.tx_ref, f32[5,64,128]{2,1,0:T(8,128)S(1)} %shard_map.40.rest_ref, f32[5,128,128]{2,1,0:T(8,128)S(1)} %shard_map.45.t_ref, f32[8,128]{1,0:T(8,128)S(1)} %max.19.top_ref), custom_call_target="tpu_custom_call" | custom-call | flops 1000000 | bytes 1000000 | tf_op jit(solution)/shard_map/pallas_call | solution.py:560
  (12 shorter events, 0.1 us)
Async XLA Ops:
  1.2 1.4 %collective-permute-start.2 = (f32[8,128]{1,0:T(8,128)S(1)}, f32[8,128]{1,0:T(8,128)S(1)}, u32[]{:S(2)}, u32[]{:S(2)}) collective-permute-start(f32[8,128]{1,0:T(8,128)S(1)} %get-tuple-element.14.after), channel_id=1, source_target_pairs={{0,8},{8,0},{16,24},{24,16},{1,9},{9,1},{17,25},{25,17},{2,10},{10... | collective-permute-start | bytes 12296 | tf_op jit(solution)/shard_map/ppermute | solution.py:404
  2.6 4.6 %collective-permute-start.3 = (f32[32,128]{1,0:T(8,128)S(1)}, f32[32,128]{1,0:T(8,128)S(1)}, u32[]{:S(2)}, u32[]{:S(2)}) collective-permute-start(f32[32,128]{1,0:T(8,128)S(1)} %pad_maximum_fusion.2), channel_id=1, source_target_pairs={{0,1},{1,0},{2,3},{3,2},{4,5},{5,4},{6,7},{7,6},{8,9},{9,8},{10,11... | collective-permute-start | bytes 49160 | tf_op jit(solution)/shard_map/ppermute | solution.py:404
  7.1 5.4 %collective-permute-start.4 = (f32[64,128]{1,0:T(8,128)S(1)}, f32[64,128]{1,0:T(8,128)S(1)}, u32[]{:S(2)}, u32[]{:S(2)}) collective-permute-start(f32[64,128]{1,0:T(8,128)S(1)} %pad_maximum_fusion), channel_id=1, source_target_pairs={{0,2},{2,0},{4,6},{6,4},{1,3},{3,1},{5,7},{7,5},{8,10},{10,8},{12,... | collective-permute-start | bytes 98312 | tf_op jit(solution)/shard_map/ppermute | solution.py:404
  9.3 12.1 %collective-permute-start = (f32[480,128]{1,0:T(8,128)S(1)}, f32[480,128]{1,0:T(8,128)S(1)}, u32[]{:S(2)}, u32[]{:S(2)}) collective-permute-start(f32[480,128]{1,0:T(8,128)S(1)} %get-tuple-element.15), channel_id=1, source_target_pairs={{0,8},{8,0},{16,24},{24,16},{1,9},{9,1},{17,25},{25,17},{2,10},{10... | collective-permute-start | bytes 737288 | tf_op jit(solution)/shard_map/ppermute | solution.py:404
  9.3 12.1 %collective-permute-start.1 = (f32[480,128]{1,0:T(8,128)S(1)}, f32[480,128]{1,0:T(8,128)S(1)}, u32[]{:S(2)}, u32[]{:S(2)}) collective-permute-start(f32[480,128]{1,0:T(8,128)S(1)} %get-tuple-element.16), channel_id=1, source_target_pairs={{0,24},{8,16},{16,8},{24,0},{1,25},{9,17},{17,9},{25,1},{2,26},{10... | collective-permute-start | bytes 737288 | tf_op jit(solution)/shard_map/ppermute | solution.py:404
  12.6 5.8 %collective-permute-start.5 = (f32[64,128]{1,0:T(8,128)S(1)}, f32[64,128]{1,0:T(8,128)S(1)}, u32[]{:S(2)}, u32[]{:S(2)}) collective-permute-start(f32[64,128]{1,0:T(8,128)S(1)} %pad_maximum_fusion.1), channel_id=1, source_target_pairs={{0,6},{2,4},{4,2},{6,0},{1,7},{3,5},{5,3},{7,1},{8,14},{10,12},{12... | collective-permute-start | bytes 98312 | tf_op jit(solution)/shard_map/ppermute | solution.py:404
  18.4 3.0 %collective-permute-start.6 = (f32[8,128]{1,0:T(8,128)S(1)}, f32[8,128]{1,0:T(8,128)S(1)}, u32[]{:S(2)}, u32[]{:S(2)}) collective-permute-start(f32[8,128]{1,0:T(8,128)S(1)} %slice_maximum_fusion.after), channel_id=1, source_target_pairs={{0,24},{8,16},{16,8},{24,0},{1,25},{9,17},{17,9},{25,1},{2,26},{10... | collective-permute-start | bytes 12296 | tf_op jit(solution)/shard_map/ppermute | solution.py:404
